TPU v7x, 32 devices: a whole 2x2x4 slice. The times are simulated.
32 devices in a mesh: dp: 4 (over x, core), fsdp: 8 (over z, y).
Axes of the slice: x: 2, y: 2, z: 4, core: 2. Of those that a mesh axis runs over, the one named last changes fastest.
Arguments:
- tokens: bfloat16 [25088, 1024], P(('dp', 'fsdp')), may hold values from -6 to 6
- scale_codes: int32 [128], P(('dp', 'fsdp')), may hold values from 0 to 15
- w_qkv: float32 [1024, 3072], P('fsdp'), may hold values from -0.1875 to 0.1875
- b_q: float32 [1024], P('fsdp'), may hold values from -3 to 3
- b_v: float32 [1024], P('fsdp'), may hold values from -3 to 3
- w_out: float32 [1024, 1024], P('fsdp'), may hold values from -1.5 to 1.5
- b_out: float32 [1024], P('fsdp'), may hold values from -3 to 3
- gain_one: float32 [1024], P('fsdp'), may hold values from 0.5 to 1.5
- shift_one: float32 [1024], P('fsdp'), may hold values from -2 to 2
- w_fc1: float32 [1024, 4096], P('fsdp'), may hold values from -0.1875 to 0.1875
- b_fc1: float32 [4096], P('fsdp'), may hold values from -3 to 3
- w_fc2: float32 [4096, 1024], P('fsdp'), may hold values from -0.09375 to 0.09375
- b_fc2: float32 [1024], P('fsdp'), may hold values from -3 to 3
- gain_two: float32 [1024], P('fsdp'), may hold values from 0.5 to 1.5
- shift_two: float32 [1024], P('fsdp'), may hold values from -2 to 2
- cotangent: bfloat16 [25088, 1024], P(('dp', 'fsdp')), may hold values from -6 to 6
Outputs:
- block_out: bfloat16 [25088, 1024], P(('dp', 'fsdp'))
- grad_tokens: float32 [25088, 1024], P(('dp', 'fsdp'))
- grad_w_qkv: float32 [1024, 3072], P('fsdp')
- grad_b_q: float32 [1024], P('fsdp')
- grad_b_v: float32 [1024], P('fsdp')
- grad_w_out: float32 [1024, 1024], P('fsdp')
- grad_b_out: float32 [1024], P('fsdp')
- grad_gain_one: float32 [1024], P('fsdp')
- grad_shift_one: float32 [1024], P('fsdp')
- grad_w_fc1: float32 [1024, 4096], P('fsdp')
- grad_b_fc1: float32 [4096], P('fsdp')
- grad_w_fc2: float32 [4096, 1024], P('fsdp')
- grad_b_fc2: float32 [1024], P('fsdp')
- grad_gain_two: float32 [1024], P('fsdp')
- grad_shift_two: float32 [1024], P('fsdp')
All inputs are finite; a program needn't handle non-finite values.
Results may differ from a plain program's by a relative error of at most 0.015.
Values may be sent and summed in bfloat16 or wider, within the bound.
No kernel may reach another device: no remote copies, remote signals or barrier semaphores. Data moves between devices by JAX's collectives and lax.ppermute only.
A program may use at most 256 MiB of HBM per device.

v0:
```python
import math

import jax
import jax.numpy as jnp
from jax import lax
from jax.sharding import PartitionSpec as P

HEADS = 16
GRID = 14
NSCALE = 16


norm_eps = 1e-06


def positions(codes, grid_side, width):
    ratio = 0.3 * jnp.exp(codes.astype(jnp.float32) * (math.log(10.0 / 0.3) / (NSCALE - 1)))
    quarter = width // 4
    omega = jnp.exp(jnp.arange(quarter).astype(jnp.float32) * (-math.log(10000.0) / quarter))
    cells = jnp.arange(grid_side * grid_side, dtype=jnp.int32)
    row_place = (cells // grid_side).astype(jnp.float32)
    col_place = (cells % grid_side).astype(jnp.float32)
    row_angle = ratio[:, None, None] * row_place[None, :, None] * omega[None, None, :]
    col_angle = ratio[:, None, None] * col_place[None, :, None] * omega[None, None, :]
    return jnp.concatenate(
        [jnp.sin(row_angle), jnp.cos(row_angle), jnp.sin(col_angle), jnp.cos(col_angle)], axis=-1
    )


def norm_affine(hidden, gain, shift):
    center = jnp.mean(hidden, axis=-1, keepdims=True)
    offset = hidden - center
    spread = jnp.mean(offset * offset, axis=-1, keepdims=True)
    return offset * lax.rsqrt(spread + norm_eps) * gain + shift


def matmul(left, right):
    return jnp.dot(left, right, preferred_element_type=jnp.float32)


def inner_rows(left, right):
    return lax.dot_general(
        left, right, (((0,), (0,)), ((), ())), preferred_element_type=jnp.float32
    )


def times_transposed(left, right):
    return lax.dot_general(
        left, right, (((1,), (1,)), ((), ())), preferred_element_type=jnp.float32
    )


def column_total(values):
    return jnp.sum(values.astype(jnp.float32), axis=0)


def local(
    tokens,
    scale_codes,
    w_qkv,
    b_q,
    b_v,
    w_out,
    b_out,
    gain_one,
    shift_one,
    w_fc1,
    b_fc1,
    w_fc2,
    b_fc2,
    gain_two,
    shift_two,
    cotangent,
):
    half = jnp.bfloat16
    row_count, width = tokens.shape
    n_img = scale_codes.shape[0]
    patches = row_count // n_img
    head_size = width // HEADS
    factor = 1.0 / math.sqrt(head_size)
    place = positions(scale_codes, GRID, width).reshape(row_count, width)
    x_zero = tokens.astype(jnp.float32) + place
    attn_params = (
        lax.all_gather(w_qkv.astype(half), "fsdp", axis=0, tiled=True),
        lax.all_gather(b_q.astype(half), "fsdp", axis=0, tiled=True),
        lax.all_gather(b_v.astype(half), "fsdp", axis=0, tiled=True),
        lax.all_gather(w_out.astype(half), "fsdp", axis=0, tiled=True),
        lax.all_gather(b_out.astype(half), "fsdp", axis=0, tiled=True),
        lax.all_gather(gain_one.astype(half), "fsdp", axis=0, tiled=True),
        lax.all_gather(shift_one.astype(half), "fsdp", axis=0, tiled=True),
    )
    full_qkv, full_bq, full_bv, full_out, full_bout, full_gone, full_sone = attn_params
    gain_one_f = full_gone.astype(jnp.float32)
    shift_one_f = full_sone.astype(jnp.float32)
    normed_one = norm_affine(x_zero, gain_one_f, shift_one_f).astype(half)
    qkv_bias = jnp.concatenate([full_bq, jnp.zeros_like(full_bq), full_bv]).astype(jnp.float32)
    projected = (
        (matmul(normed_one, full_qkv) + qkv_bias)
        .astype(half)
        .reshape(n_img, patches, 3, HEADS, head_size)
    )
    queries = projected[:, :, 0]
    keys_all = projected[:, :, 1]
    values_all = projected[:, :, 2]
    scores = (
        jnp.einsum("iqhd,ikhd->ihqk", queries, keys_all, preferred_element_type=jnp.float32)
        * factor
    )
    top_score = jnp.max(scores, axis=-1, keepdims=True)
    raised = jnp.exp(scores - top_score)
    totals = jnp.sum(raised, axis=-1, keepdims=True)
    probs = raised / totals
    log_total = top_score + jnp.log(totals)
    mixed = jnp.einsum(
        "ihqk,ikhd->iqhd", probs.astype(half), values_all, preferred_element_type=jnp.float32
    )
    mixed = mixed.reshape(row_count, width).astype(half)
    after_attn = x_zero + (matmul(mixed, full_out) + full_bout.astype(jnp.float32))
    mlp_params = (
        lax.all_gather(w_fc1.astype(half), "fsdp", axis=0, tiled=True),
        lax.all_gather(b_fc1.astype(half), "fsdp", axis=0, tiled=True),
        lax.all_gather(w_fc2.astype(half), "fsdp", axis=0, tiled=True),
        lax.all_gather(b_fc2.astype(half), "fsdp", axis=0, tiled=True),
        lax.all_gather(gain_two.astype(half), "fsdp", axis=0, tiled=True),
        lax.all_gather(shift_two.astype(half), "fsdp", axis=0, tiled=True),
    )
    full_fc1, full_bfc1, full_fc2, full_bfc2, full_gtwo, full_stwo = mlp_params
    gain_two_f = full_gtwo.astype(jnp.float32)
    shift_two_f = full_stwo.astype(jnp.float32)
    normed_two = norm_affine(after_attn, gain_two_f, shift_two_f).astype(half)
    hidden_pre = matmul(normed_two, full_fc1) + full_bfc1.astype(jnp.float32)
    hidden_act = jax.nn.gelu(hidden_pre, approximate=False).astype(half)
    block_out = (
        after_attn + (matmul(hidden_act, full_fc2) + full_bfc2.astype(jnp.float32))
    ).astype(half)
    back_mlp = (
        lax.all_gather(w_fc1.astype(half), "fsdp", axis=0, tiled=True),
        lax.all_gather(b_fc1.astype(half), "fsdp", axis=0, tiled=True),
        lax.all_gather(w_fc2.astype(half), "fsdp", axis=0, tiled=True),
        lax.all_gather(b_fc2.astype(half), "fsdp", axis=0, tiled=True),
        lax.all_gather(gain_two.astype(half), "fsdp", axis=0, tiled=True),
        lax.all_gather(shift_two.astype(half), "fsdp", axis=0, tiled=True),
    )
    back_fc1 = back_mlp[0]
    back_fc2 = back_mlp[2]
    back_gtwo = back_mlp[4].astype(jnp.float32)
    back_stwo = back_mlp[5].astype(jnp.float32)
    grad_w_fc2 = inner_rows(hidden_act, cotangent)
    grad_b_fc2 = column_total(cotangent)
    grad_act = times_transposed(cotangent, back_fc2)
    unused_act, gelu_pull = jax.vjp(lambda pre: jax.nn.gelu(pre, approximate=False), hidden_pre)
    grad_pre = gelu_pull(grad_act)[0].astype(half)
    grad_w_fc1 = inner_rows(normed_two, grad_pre)
    grad_b_fc1 = column_total(grad_pre)
    grad_two_in = times_transposed(grad_pre, back_fc1)
    unused_two, norm_two_pull = jax.vjp(norm_affine, after_attn, back_gtwo, back_stwo)
    part_two, grad_gain_two, grad_shift_two = norm_two_pull(grad_two_in)
    grad_after = cotangent.astype(jnp.float32) + part_two
    mlp_shards = (
        lax.psum_scatter(grad_w_fc1, "fsdp", scatter_dimension=0, tiled=True),
        lax.psum_scatter(grad_b_fc1, "fsdp", scatter_dimension=0, tiled=True),
        lax.psum_scatter(grad_w_fc2, "fsdp", scatter_dimension=0, tiled=True),
        lax.psum_scatter(grad_b_fc2, "fsdp", scatter_dimension=0, tiled=True),
        lax.psum_scatter(grad_gain_two, "fsdp", scatter_dimension=0, tiled=True),
        lax.psum_scatter(grad_shift_two, "fsdp", scatter_dimension=0, tiled=True),
    )
    back_attn = (
        lax.all_gather(w_qkv.astype(half), "fsdp", axis=0, tiled=True),
        lax.all_gather(b_q.astype(half), "fsdp", axis=0, tiled=True),
        lax.all_gather(b_v.astype(half), "fsdp", axis=0, tiled=True),
        lax.all_gather(w_out.astype(half), "fsdp", axis=0, tiled=True),
        lax.all_gather(b_out.astype(half), "fsdp", axis=0, tiled=True),
        lax.all_gather(gain_one.astype(half), "fsdp", axis=0, tiled=True),
        lax.all_gather(shift_one.astype(half), "fsdp", axis=0, tiled=True),
    )
    back_qkv = back_attn[0]
    back_out = back_attn[3]
    back_gone = back_attn[5].astype(jnp.float32)
    back_sone = back_attn[6].astype(jnp.float32)
    branch_grad = grad_after.astype(half)
    grad_w_out = inner_rows(mixed, branch_grad)
    grad_b_out = column_total(branch_grad)
    grad_mixed = (
        times_transposed(branch_grad, back_out)
        .astype(half)
        .reshape(n_img, patches, HEADS, head_size)
    )
    again_scores = (
        jnp.einsum("iqhd,ikhd->ihqk", queries, keys_all, preferred_element_type=jnp.float32)
        * factor
    )
    again_probs = jnp.exp(again_scores - log_total)
    grad_values = jnp.einsum(
        "ihqk,iqhd->ikhd", again_probs.astype(half), grad_mixed, preferred_element_type=jnp.float32
    )
    grad_probs = jnp.einsum(
        "iqhd,ikhd->ihqk", grad_mixed, values_all, preferred_element_type=jnp.float32
    )
    weighted = jnp.sum(again_probs * grad_probs, axis=-1, keepdims=True)
    grad_scores = (again_probs * (grad_probs - weighted)).astype(half)
    grad_queries = (
        jnp.einsum("ihqk,ikhd->iqhd", grad_scores, keys_all, preferred_element_type=jnp.float32)
        * factor
    )
    grad_keys = (
        jnp.einsum("ihqk,iqhd->ikhd", grad_scores, queries, preferred_element_type=jnp.float32)
        * factor
    )
    grad_proj = (
        jnp.stack([grad_queries, grad_keys, grad_values], axis=2)
        .reshape(row_count, 3 * width)
        .astype(half)
    )
    grad_w_qkv = inner_rows(normed_one, grad_proj)
    grad_b_q = column_total(grad_proj[:, :width])
    grad_b_v = column_total(grad_proj[:, 2 * width :])
    grad_one_in = times_transposed(grad_proj, back_qkv)
    unused_one, norm_one_pull = jax.vjp(norm_affine, x_zero, back_gone, back_sone)
    part_one, grad_gain_one, grad_shift_one = norm_one_pull(grad_one_in)
    grad_tokens = grad_after + part_one
    attn_shards = (
        lax.psum_scatter(grad_w_qkv, "fsdp", scatter_dimension=0, tiled=True),
        lax.psum_scatter(grad_b_q, "fsdp", scatter_dimension=0, tiled=True),
        lax.psum_scatter(grad_b_v, "fsdp", scatter_dimension=0, tiled=True),
        lax.psum_scatter(grad_w_out, "fsdp", scatter_dimension=0, tiled=True),
        lax.psum_scatter(grad_b_out, "fsdp", scatter_dimension=0, tiled=True),
        lax.psum_scatter(grad_gain_one, "fsdp", scatter_dimension=0, tiled=True),
        lax.psum_scatter(grad_shift_one, "fsdp", scatter_dimension=0, tiled=True),
    )
    summed = (
        lax.psum(attn_shards[0].astype(jnp.bfloat16), "dp").astype(jnp.float32),
        lax.psum(attn_shards[1].astype(jnp.bfloat16), "dp").astype(jnp.float32),
        lax.psum(attn_shards[2].astype(jnp.bfloat16), "dp").astype(jnp.float32),
        lax.psum(attn_shards[3].astype(jnp.bfloat16), "dp").astype(jnp.float32),
        lax.psum(attn_shards[4].astype(jnp.bfloat16), "dp").astype(jnp.float32),
        lax.psum(attn_shards[5].astype(jnp.bfloat16), "dp").astype(jnp.float32),
        lax.psum(attn_shards[6].astype(jnp.bfloat16), "dp").astype(jnp.float32),
        lax.psum(mlp_shards[0].astype(jnp.bfloat16), "dp").astype(jnp.float32),
        lax.psum(mlp_shards[1].astype(jnp.bfloat16), "dp").astype(jnp.float32),
        lax.psum(mlp_shards[2].astype(jnp.bfloat16), "dp").astype(jnp.float32),
        lax.psum(mlp_shards[3].astype(jnp.bfloat16), "dp").astype(jnp.float32),
        lax.psum(mlp_shards[4].astype(jnp.bfloat16), "dp").astype(jnp.float32),
        lax.psum(mlp_shards[5].astype(jnp.bfloat16), "dp").astype(jnp.float32),
    )
    return (
        block_out,
        grad_tokens,
        summed[0],
        summed[1],
        summed[2],
        summed[3],
        summed[4],
        summed[5],
        summed[6],
        summed[7],
        summed[8],
        summed[9],
        summed[10],
        summed[11],
        summed[12],
    )


def solution(mesh):
    placed = (
        P(("dp", "fsdp"), None),
        P(("dp", "fsdp")),
        P("fsdp", None),
        P("fsdp"),
        P("fsdp"),
        P("fsdp", None),
        P("fsdp"),
        P("fsdp"),
        P("fsdp"),
        P("fsdp", None),
        P("fsdp"),
        P("fsdp", None),
        P("fsdp"),
        P("fsdp"),
        P("fsdp"),
        P(("dp", "fsdp"), None),
    )
    return jax.shard_map(
        local,
        mesh=mesh,
        in_specs=placed,
        out_specs=(
            P(("dp", "fsdp"), None),
            P(("dp", "fsdp"), None),
            P("fsdp", None),
            P("fsdp"),
            P("fsdp"),
            P("fsdp", None),
            P("fsdp"),
            P("fsdp"),
            P("fsdp"),
            P("fsdp", None),
            P("fsdp"),
            P("fsdp", None),
            P("fsdp"),
            P("fsdp"),
            P("fsdp"),
        ),
        check_vma=False,
    )
```

profile of v0, /device:TPU:0, one launch (start us, length us, event | category | flops | bytes accessed | tf_op | source)
XLA Modules:
  0.0 1432.5 jit_solution(16230341930971764661)
XLA Ops:
  16.1 22.5 %all-gather.6 = bf16[8,1,128]{2,1,0:T(2,128)(2,1)S(1)} all-gather(bf16[1,1,128]{2,1,0:T(2,128)(2,1)S(1)} %convert_bitcast_fusion.3), channel_id=1, replica_groups=mesh['dp'=4,'fsdp'=8] {'fsdp'}, dimensions={0}, use_global_device_ids=true | all-gather | bytes 2304 | tf_op jit(solution)/shard_map/all_gather | solution.py:125
  38.6 16.3 %all-gather.5 = bf16[8,1,128]{2,1,0:T(2,128)(2,1)S(1)} all-gather(bf16[1,1,128]{2,1,0:T(2,128)(2,1)S(1)} %convert_bitcast_fusion.4), channel_id=1, replica_groups=mesh['dp'=4,'fsdp'=8] {'fsdp'}, dimensions={0}, use_global_device_ids=true | all-gather | bytes 2304 | tf_op jit(solution)/shard_map/all_gather | solution.py:124
  54.9 18.5 %all-gather.1 = bf16[8,1,128]{2,1,0:T(2,128)(2,1)S(1)} all-gather(bf16[1,1,128]{2,1,0:T(2,128)(2,1)S(1)} %convert_bitcast_fusion.8), channel_id=1, replica_groups=mesh['dp'=4,'fsdp'=8] {'fsdp'}, dimensions={0}, use_global_device_ids=true | all-gather | bytes 2304 | tf_op jit(solution)/shard_map/all_gather | solution.py:90
  73.4 16.4 %all-gather = bf16[8,1,128]{2,1,0:T(2,128)(2,1)S(1)} all-gather(bf16[1,1,128]{2,1,0:T(2,128)(2,1)S(1)} %convert_bitcast_fusion.9), channel_id=1, replica_groups=mesh['dp'=4,'fsdp'=8] {'fsdp'}, dimensions={0}, use_global_device_ids=true | all-gather | bytes 2304 | tf_op jit(solution)/shard_map/all_gather | solution.py:89
  89.9 18.4 %all-gather.4 = bf16[8,1,128]{2,1,0:T(2,128)(2,1)S(1)} all-gather(bf16[1,1,128]{2,1,0:T(2,128)(2,1)S(1)} %convert_bitcast_fusion.5), channel_id=1, replica_groups=mesh['dp'=4,'fsdp'=8] {'fsdp'}, dimensions={0}, use_global_device_ids=true | all-gather | bytes 2304 | tf_op jit(solution)/shard_map/all_gather | solution.py:88
  108.3 16.2 %all-gather.3 = bf16[8,1,128]{2,1,0:T(2,128)(2,1)S(1)} all-gather(bf16[1,1,128]{2,1,0:T(2,128)(2,1)S(1)} %convert_bitcast_fusion.6), channel_id=1, replica_groups=mesh['dp'=4,'fsdp'=8] {'fsdp'}, dimensions={0}, use_global_device_ids=true | all-gather | bytes 2304 | tf_op jit(solution)/shard_map/all_gather | solution.py:86
  124.5 18.2 %all-gather.2 = bf16[8,1,128]{2,1,0:T(2,128)(2,1)S(1)} all-gather(bf16[1,1,128]{2,1,0:T(2,128)(2,1)S(1)} %convert_bitcast_fusion.7), channel_id=1, replica_groups=mesh['dp'=4,'fsdp'=8] {'fsdp'}, dimensions={0}, use_global_device_ids=true | all-gather | bytes 2304 | tf_op jit(solution)/shard_map/all_gather | solution.py:85
  142.8 26.3 %all-gather.7 = bf16[8,1,512]{2,1,0:T(2,128)(2,1)S(1)} all-gather(bf16[1,1,512]{2,1,0:T(2,128)(2,1)S(1)} %reshape.247), channel_id=1, replica_groups=mesh['dp'=4,'fsdp'=8] {'fsdp'}, dimensions={0}, use_global_device_ids=true | all-gather | bytes 9216 | tf_op jit(solution)/shard_map/all_gather | solution.py:121
  169.2 5.6 multiply_sine_fusion.1
  177.3 10.6 add_convert_fusion.1
  187.9 12.7 reshape.267
  200.7 6.4 fusion.48
  207.1 3.7 copy.74
  210.8 4.3 copy.75
  215.1 5.9 copy.76
  221.0 3.6 multiply_reduce_fusion.1
  236.8 4.9 convert_element_type.262
  241.7 4.3 fusion.50
  248.2 41.3 %all-gather.18.cloned.1.call-done = bf16[1024,4096]{1,0:T(8,128)(2,1)} async-done(((bf16[128,4096]{1,0:T(8,128)(2,1)}), bf16[1024,4096]{1,0:T(8,128)(2,1)}) %all-gather.18.cloned.1.call-update) | async-done | bytes 8388624 | tf_op jit(solution)/shard_map/all_gather | solution.py:120
  289.5 13.2 fusion.42
  302.7 112.5 %all-gather.20.cloned.1.call-done = bf16[4096,1024]{1,0:T(8,128)(2,1)} async-done(((bf16[512,1024]{1,0:T(8,128)(2,1)}), bf16[4096,1024]{1,0:T(8,128)(2,1)}) %all-gather.20.cloned.1.call-update) | async-done | bytes 8388624 | tf_op jit(solution)/shard_map/all_gather | solution.py:122
  415.2 41.2 %convert_reduce_fusion = (f32[4096]{0:T(1024)}, bf16[784,4096]{1,0:T(8,128)(2,1)}, f32[784,4096]{1,0:T(8,128)}) fusion(f32[784,4096]{1,0:T(8,128)} %fusion.42, f32[4096]{0:T(1024)S(1)} %bitcast.97, bf16[784,1024]{1,0:T(8,128)(2,1)S(1)} %copy-done.12, bf16[4096,1024]{1,0:T(8,128)(2,1)} %all-gather.20.cloned.1.call-done), kind=kOutput, calls=%fused_computation.7 | convolution fusion | flops 6817509376 | bytes 42139648 | tf_op jit(solution)/shard_map/dot_general | solution.py:48
  456.4 10.6 multiply_reduce_fusion.2
  470.7 4.3 fusion.51
  475.9 3.4 convolution_convert_fusion
  479.4 3.4 reshape.268
  482.8 5.4 copy.60
  488.2 14.4 %multiply_reduce_fusion = (f32[4,16,196]{2,1,0:T(8,128)S(1)}, f32[4,16,196,196]{2,3,1,0:T(8,128)}) fusion(f32[4,16,196,196]{2,3,1,0:T(8,128)} %copy-done, f32[4,16,196]{2,1,0:T(8,128)S(1)} %log_add_fusion, bf16[4,196,16,64]{1,3,2,0:T(8,128)(2,1)} %copy.60, bf16[4,196,1,16,64]{1,4,3,0,2:T(8,128)(2,1)} %copy.74), kind=kOutput, calls=%fused_computation.2 | convolution fusion | flops 324525824 | bytes 22980608 | tf_op jit(solution)/shard_map/iqhd,ikhd->ihqk/dot_general | solution.py:196
  502.6 6.6 multiply_convert_fusion
  509.2 5.2 fusion.29
  514.4 4.2 fusion.26
  518.6 5.4 convert_bitcast_fusion
  524.0 4.4 pad_maximum_fusion
  528.4 9.1 copy.65
  537.6 12.7 convert_element_type.285
  550.3 13.0 fusion.40
  564.0 15.8 %fusion.41 = f32[1024,4096]{1,0:T(8,128)} fusion(bf16[784,4096]{1,0:T(8,128)(2,1)} %get-tuple-element.46, f32[784,1024]{1,0:T(8,128)} %copy-done.7, f32[1024]{0:T(1024)S(1)} %bitcast.110, f32[1024]{0:T(1024)S(1)} %bitcast.106, f32[784]{0:T(1024)S(1)} %fusion.33, f32[784]{0:T(1024)S(1)} %broadcast_multiply_fusion), kind=kOutput, calls=%fused_computation.116 | convolution fusion | flops 6580682752 | bytes 26425472 | tf_op jit(solution)/shard_map/dot_general | solution.py:42
  579.9 9.9 multiply_convert_fusion.1
  592.5 11.6 fusion.52
  606.6 18.7 %all-gather.8 = bf16[8,1,128]{2,1,0:T(2,128)(2,1)S(1)} all-gather(bf16[1,1,128]{2,1,0:T(2,128)(2,1)S(1)} %convert_bitcast_fusion.2), channel_id=1, replica_groups=mesh['dp'=4,'fsdp'=8] {'fsdp'}, dimensions={0}, use_global_device_ids=true | all-gather | bytes 2304 | tf_op jit(solution)/shard_map/all_gather | solution.py:123
  625.3 10.8 multiply_reduce_fusion.3
  642.8 36.7 %all-reduce.9 = (bf16[1024]{0:T(1024)(128)(2,1)S(1)}, bf16[1024]{0:T(1024)(128)(2,1)S(1)}, bf16[1024]{0:T(1024)(128)(2,1)S(1)}, bf16[1024]{0:T(1024)(128)(2,1)S(...) all-reduce(f32[1024]{0:T(1024)S(1)} %get-tuple-element.20, ...), channel_id=3, replica_groups=mesh['dp'=4,'fsdp'=8] {'fsdp'}, use_global_device_ids=true, to_apply=%region_14.15.clone | all-reduce | flops 12288 | bytes 73728
  680.1 6.3 all-reduce.10
  693.0 80.4 %reduce-scatter.5.cloned.1.call-done = f32[128,3072]{1,0:T(8,128)} async-done(((f32[1024,3072]{1,0:T(8,128)}), f32[128,3072]{1,0:T(8,128)}) %reduce-scatter.5.cloned.1.call-update) | async-done | bytes 1572880 | tf_op jit(solution)/shard_map/reduce_scatter | solution.py:222
  775.8 283.8 %reduce-scatter.9.cloned.1.call-done = f32[128,4096]{1,0:T(8,128)} async-done(((f32[1024,4096]{1,0:T(8,128)}), f32[128,4096]{1,0:T(8,128)}) %reduce-scatter.9.cloned.1.call-update) | async-done | bytes 2097168 | tf_op jit(solution)/shard_map/reduce_scatter | solution.py:160
  1062.2 282.9 %reduce-scatter.11.cloned.1.call-done = f32[512,1024]{1,0:T(8,128)} async-done(((f32[4096,1024]{1,0:T(8,128)}), f32[512,1024]{1,0:T(8,128)}) %reduce-scatter.11.cloned.1.call-update) | async-done | bytes 2097168 | tf_op jit(solution)/shard_map/reduce_scatter | solution.py:162
  1347.8 12.0 add_convert_fusion.2
  1359.8 57.3 %all-reduce.14.cloned.1.call-done = (bf16[128,3072]{1,0:T(8,128)(2,1)}, bf16[128,1024]{1,0:T(8,128)(2,1)}, bf16[128,4096]{1,0:T(8,128)(2,1)}, bf16[512,1024]{1,0:T(8,128)(2,1)}) async-done(((bf16[128,3072]{1,0:T(8,128)(2,1)}, bf16[128,1024]{1,0:T(8,128)(2,1)}, bf16[128,4096]{1,0:T(8,128)(2,1)}, bf16[512,1024]{1,0:T(8,128)(2,1)}), (bf16[128,3072]{1,0:T(8,128)(2,1)}, bf16[128,1024]{1,0:T(8,128)(2,1)}, ...) | async-done | bytes 3145744 | tf_op jit(solution)/shard_map/psum | solution.py:231
  (211 shorter events, 65.1 us)
Async XLA Ops:
  7.2 4.6 copy-start.15
  7.2 170.1 %all-gather.14.cloned.1.call-start = ((), (), s32[]{:S(2)}) async-start(), calls=%async_computation.4 | async-start | bytes 7077888 | tf_op jit(solution)/shard_map/all_gather | solution.py:84
  9.8 231.9 %all-gather.16.cloned.1.call-start = ((), (), s32[]{:S(2)}) async-start(), calls=%async_computation.5 | async-start | bytes 2359296 | tf_op jit(solution)/shard_map/all_gather | solution.py:87
  11.7 4.4 copy-start.39
  11.7 26.9 %copy-start.40 = (f32[128]{0:T(128)S(1)}, f32[128]{0:T(128)}, u32[]{:S(2)}) copy-start(f32[128]{0:T(128)} %param.29) | copy-start | bytes 1540
  11.7 43.2 %copy-start.41 = (f32[128]{0:T(128)S(1)}, f32[128]{0:T(128)}, u32[]{:S(2)}) copy-start(f32[128]{0:T(128)} %param.24) | copy-start | bytes 1540
  11.7 61.7 %copy-start.42 = (f32[128]{0:T(128)S(1)}, f32[128]{0:T(128)}, u32[]{:S(2)}) copy-start(f32[128]{0:T(128)} %param.23) | copy-start | bytes 1540
  11.7 78.1 %copy-start.43 = (f32[128]{0:T(128)S(1)}, f32[128]{0:T(128)}, u32[]{:S(2)}) copy-start(f32[128]{0:T(128)} %param.22) | copy-start | bytes 1540
  11.7 96.5 %copy-start.44 = (f32[128]{0:T(128)S(1)}, f32[128]{0:T(128)}, u32[]{:S(2)}) copy-start(f32[128]{0:T(128)} %param.20) | copy-start | bytes 1540
  11.7 112.7 %copy-start.45 = (f32[128]{0:T(128)S(1)}, f32[128]{0:T(128)}, u32[]{:S(2)}) copy-start(f32[128]{0:T(128)} %param.19) | copy-start | bytes 1540
  11.7 130.9 %copy-start.46 = (s32[4]{0:T(128)S(1)}, s32[4]{0:T(128)}, u32[]{:S(2)}) copy-start(s32[4]{0:T(128)} %param.17) | copy-start | bytes 52
  11.7 277.7 %all-gather.18.cloned.1.call-start = ((), (), s32[]{:S(2)}) async-start(), calls=%async_computation.6 | async-start | bytes 9437184 | tf_op jit(solution)/shard_map/all_gather | solution.py:120
  12.9 402.2 %all-gather.20.cloned.1.call-start = ((), (), s32[]{:S(2)}) async-start(), calls=%async_computation.7 | async-start | bytes 9437184 | tf_op jit(solution)/shard_map/all_gather | solution.py:122
  15.7 675.4 %reduce-scatter.7.cloned.1.call-start = ((), (), s32[]{:S(2)}) async-start(), calls=%async_computation.9 | async-start | bytes 4718592 | tf_op jit(solution)/shard_map/reduce_scatter | solution.py:225
  38.5 250.9 %copy-start.33 = (f32[8,1,128]{2,1,0:T(1,128)}, f32[8,1,128]{2,1,0:T(1,128)S(1)}, u32[]{:S(2)}) copy-start(f32[8,1,128]{2,1,0:T(1,128)S(1)} %convert_element_type.320) | copy-start | bytes 12292
  73.4 103.9 %copy-start.35 = (f32[8,1,128]{2,1,0:T(1,128)}, f32[8,1,128]{2,1,0:T(1,128)S(1)}, u32[]{:S(2)}) copy-start(f32[8,1,128]{2,1,0:T(1,128)S(1)} %convert_element_type.317) | copy-start | bytes 12292
  89.8 87.5 %copy-start.28 = (f32[8,1,128]{2,1,0:T(1,128)}, f32[8,1,128]{2,1,0:T(1,128)S(1)}, u32[]{:S(2)}) copy-start(f32[8,1,128]{2,1,0:T(1,128)S(1)} %convert_element_type.316) | copy-start | bytes 12292
  176.7 11.2 copy-start.1
  176.8 11.2 copy-start.22
  177.2 10.7 copy-start.24
  177.3 10.7 copy-start.30
  215.1 9.5 copy-start.6
  224.6 5.1 copy-start
  224.6 5.1 copy-start.18
  224.6 5.7 copy-start.10
  233.7 8.0 copy-start.2
  248.2 54.5 %copy-start.26 = (f32[784]{0:T(1024)}, f32[784]{0:T(1024)S(1)}, u32[]{:S(2)}) copy-start(f32[784]{0:T(1024)S(1)} %multiply_reduce_fusion.6) | copy-start | bytes 9412
  289.4 125.7 %copy-start.12 = (bf16[784,1024]{1,0:T(8,128)(2,1)S(1)}, bf16[784,1024]{1,0:T(8,128)(2,1)}, u32[]{:S(2)}) copy-start(bf16[784,1024]{1,0:T(8,128)(2,1)} %param.31) | copy-start | bytes 4816900
  415.2 41.2 %copy-start.8 = (f32[784,1024]{1,0:T(8,128)S(1)}, f32[784,1024]{1,0:T(8,128)}, u32[]{:S(2)}) copy-start(f32[784,1024]{1,0:T(8,128)} %copy-done.7) | copy-start | bytes 9633796
  415.2 41.2 %copy-start.38 = (bf16[1024,4096]{1,0:T(8,128)(2,1)S(1)}, bf16[1024,4096]{1,0:T(8,128)(2,1)}, u32[]{:S(2)}) copy-start(bf16[1024,4096]{1,0:T(8,128)(2,1)} %all-gather.18.cloned.1.call-done) | copy-start | bytes 25165828
  456.4 10.6 copy-start.27
  475.0 298.3 %reduce-scatter.5.cloned.1.call-start = ((), (), s32[]{:S(2)}) async-start(), calls=%async_computation.8 | async-start | bytes 14155776 | tf_op jit(solution)/shard_map/reduce_scatter | solution.py:222
  482.8 19.8 %slice-start = ((s8[13107200]{0:T(1024)(128)(4,1)}), s8[524288]{0:T(1024)(128)(4,1)S(1)}, s32[]{:S(2)}) async-start(s8[13107200]{0:T(1024)(128)(4,1)} %bitcast.95), calls=%async_computation.13 | async-start | bytes 1048576
  488.1 14.4 %slice-start.1 = ((s8[13107200]{0:T(1024)(128)(4,1)}), s8[4194304]{0:T(1024)(128)(4,1)S(1)}, s32[]{:S(2)}) async-start(s8[13107200]{0:T(1024)(128)(4,1)} %bitcast.95), calls=%async_computation.14 | async-start | bytes 8388608
  488.1 14.4 %slice-start.2 = ((s8[13107200]{0:T(1024)(128)(4,1)}), s8[4194304]{0:T(1024)(128)(4,1)S(1)}, s32[]{:S(2)}) async-start(s8[13107200]{0:T(1024)(128)(4,1)} %bitcast.95), calls=%async_computation.15 | async-start | bytes 8388608
  488.1 14.4 %slice-start.3 = ((s8[13107200]{0:T(1024)(128)(4,1)}), s8[4194304]{0:T(1024)(128)(4,1)S(1)}, s32[]{:S(2)}) async-start(s8[13107200]{0:T(1024)(128)(4,1)} %bitcast.95), calls=%async_computation.16 | async-start | bytes 8388608
  537.5 12.7 copy-start.3
  537.5 12.7 copy-start.23
  537.5 12.7 copy-start.29
  537.5 12.7 copy-start.31
  537.5 12.7 copy-start.36
  563.3 496.2 %reduce-scatter.9.cloned.1.call-start = ((), (), s32[]{:S(2)}) async-start(), calls=%async_computation.10 | async-start | bytes 18874368 | tf_op jit(solution)/shard_map/reduce_scatter | solution.py:160
  579.8 765.3 %reduce-scatter.11.cloned.1.call-start = ((), (), s32[]{:S(2)}) async-start(), calls=%async_computation.11 | async-start | bytes 18874368 | tf_op jit(solution)/shard_map/reduce_scatter | solution.py:162
  579.9 12.6 copy-start.13
  604.1 813.0 %all-reduce.14.cloned.1.call-start = ((), (), s32[]{:S(2)}) async-start(), calls=%async_computation.12 | async-start | bytes 6291456 | tf_op jit(solution)/shard_map/psum | solution.py:231
  625.3 10.8 copy-start.25
  775.8 572.1 %copy-start.9 = (f32[784,1024]{1,0:T(8,128)S(1)}, f32[784,1024]{1,0:T(8,128)}, u32[]{:S(2)}) copy-start(f32[784,1024]{1,0:T(8,128)} %copy-done.7) | copy-start | bytes 9633796
  1417.1 7.1 copy-start.17
  (14 other events, 28.4 us)
Sparse Core Ops, SparseCore 0:
  10.8 101.9 all-gather.13
  115.5 47.7 all-gather.15
  166.0 123.4 all-gather.17
  292.0 123.1 all-gather.19
  475.2 86.2 reduce-scatter.6
  565.4 207.9 reduce-scatter.4
  777.6 281.8 reduce-scatter.8
  1063.3 281.7 reduce-scatter.10
  1349.0 68.0 all-reduce.13
where the time goes:
time: 1440 us; the launch traced here: 1430 us
  waiting for transfers between devices  858 us (60%)
  blocking collectives  214 us (15%)
  matrix products  187 us (13%)
  local copies, waits for them, and re-layouts  84.6 us (6%)
  other arithmetic  71.8 us (5%)
  between operations  16.1 us (1%)
    reduce_scatter x1, waiting for transfers between devices, local(): lax.psum_scatter(grad_w_fc1, 'fsdp', scatter_dimension=0, tiled=True)  284 us
    reduce_scatter x1, waiting for transfers between devices, local(): lax.psum_scatter(grad_w_fc2, 'fsdp', scatter_dimension=0, tiled=True)  283 us
    all_gather x1, waiting for transfers between devices, local(): lax.all_gather(w_fc2.astype(half), 'fsdp', axis=0, tiled=True)  112 us
    reduce_scatter x1, waiting for transfers between devices, local(): lax.psum_scatter(grad_w_qkv, 'fsdp', scatter_dimension=0, tiled=True)  80.4 us
    dot_general x4, matrix products, times_transposed(): lax.dot_general(left, right, (((1,), (1,)), ((), ())), preferred_element_...  66.1 us
    psum x1, waiting for transfers between devices, local(): lax.psum(attn_shards[0].astype(jnp.bfloat16), 'dp').astype(jnp.float32)  57.3 us
    dot_general x4, matrix products, inner_rows(): lax.dot_general(left, right, (((0,), (0,)), ((), ())), preferred_element_...  44.7 us
    all_gather x1, waiting for transfers between devices, local(): lax.all_gather(w_fc1.astype(half), 'fsdp', axis=0, tiled=True)  41.3 us
  transfers between devices with their start and end apart: 9, of which 6 were waited for; matrix products, arithmetic and copies ran while one was open for 18% of the time, Pallas kernels for 0%

commit v1 on v0

v1 whole, which is shorter than its diff:
```python
import math

import jax
import jax.numpy as jnp
from jax import lax
from jax.experimental import pallas as pl
from jax.experimental.pallas import tpu as pltpu
from jax.sharding import PartitionSpec as P

HEADS = 16
GRID = 14
NSCALE = 16
norm_eps = 1e-06
half = jnp.bfloat16
full = jnp.float32


def swap(value, axis, size, bit):
    return lax.ppermute(value, axis, [(i, i ^ (1 << bit)) for i in range(size)])


def core_swap(value):
    return swap(value, "dp", 4, 0)


def x_swap(value):
    return swap(value, "dp", 4, 1)


def masks(n):
    found = [0]
    for bit in reversed(range(n.bit_length() - 1)):
        found = found + [m | (1 << bit) for m in found]
    return found


def gather_shards(piece, n, last=0):
    held = piece[None]
    for bit in reversed(range(last, n.bit_length() - 1)):
        held = jnp.concatenate([held, swap(held, "fsdp", n, bit)])
    return held


def gather_quarters(piece, n):
    own = gather_shards(piece, n)
    beside = core_swap(own)
    across = x_swap(own)
    return own, beside, across, core_swap(across)


def add_half(a, b):
    return (a.astype(full) + b.astype(full)).astype(half)


def scatter_shards(low, high, n):
    for bit in range(n.bit_length() - 1):
        got = swap(high, "fsdp", n, bit)
        size = low.shape[0] // 2
        if size:
            low, high = add_half(low[:size], got[:size]), add_half(low[size:], got[size:])
        else:
            low = add_half(low, got)
    return low[0]


def reduce_quarters(parts, n):
    middle = n // 2
    beside = core_swap(parts[1])
    across = add_half(parts[2], core_swap(parts[3]))
    got = x_swap(across)
    total = [
        (parts[0][s].astype(full) + beside[s].astype(full) + got[s].astype(full)).astype(half)
        for s in (slice(0, middle), slice(middle, None))
    ]
    return scatter_shards(total[0], total[1], n)


def spread_quarters(piece, q):
    pair = [piece, core_swap(piece)]
    there = x_swap(jnp.stack(pair))
    pieces = pair + [there[0], there[1]]
    odd = (q & 1) == 1
    upper = q >= 2
    once = [jnp.where(odd, pieces[i ^ 1], pieces[i]) for i in range(4)]
    return [jnp.where(upper, once[i ^ 2], once[i]) for i in range(4)]


def moved(sources, shape, n, plan, order):
    def kernel(order_ref, *refs):
        ins, outs, sem = refs[: len(sources)], refs[len(sources) : -1], refs[-1]

        def step(r, carry):
            for src, dst in plan(r, order_ref, ins, outs):
                pltpu.make_async_copy(src, dst, sem.at[0]).start()
            return carry

        lax.fori_loop(0, n, step, 0)
        for out in outs:
            pltpu.make_async_copy(out, out, sem.at[0]).wait()

    anywhere = pl.BlockSpec(memory_space=pl.ANY)
    shapes = [jax.ShapeDtypeStruct(s, half) for s in shape]
    return pl.pallas_call(
        kernel,
        out_shape=shapes,
        grid_spec=pltpu.PrefetchScalarGridSpec(
            num_scalar_prefetch=1,
            grid=(1,),
            in_specs=[anywhere] * len(sources),
            out_specs=[anywhere] * len(shapes),
            scratch_shapes=[pltpu.SemaphoreType.DMA((1,))],
        ),
        name="moved",
    )(order, *sources)


def table(codes, width):
    ratio = 0.3 * jnp.exp(codes.astype(full) * (math.log(10.0 / 0.3) / (NSCALE - 1)))
    quarter = width // 4
    omega = jnp.exp(jnp.arange(quarter).astype(full) * (-math.log(10000.0) / quarter))
    steps = jnp.arange(GRID, dtype=jnp.int32).astype(full)
    angle = ratio[:, None, None] * steps[None, :, None] * omega[None, None, :]
    return jnp.concatenate([jnp.sin(angle), jnp.cos(angle)], axis=-1)


def norm_affine(hidden, gain, shift):
    center = jnp.mean(hidden, axis=-1, keepdims=True)
    offset = hidden - center
    spread = jnp.mean(offset * offset, axis=-1, keepdims=True)
    return offset * lax.rsqrt(spread + norm_eps) * gain + shift


def matmul(left, right):
    return jnp.dot(left, right, preferred_element_type=full)


def inner_rows(left, right):
    return lax.dot_general(left, right, (((0,), (0,)), ((), ())), preferred_element_type=full)


def times_transposed(left, right):
    return lax.dot_general(left, right, (((1,), (1,)), ((), ())), preferred_element_type=full)


def column_total(values):
    return jnp.sum(values.astype(full), axis=0)


def local(
    tokens,
    scale_codes,
    w_qkv,
    b_q,
    b_v,
    w_out,
    b_out,
    gain_one,
    shift_one,
    w_fc1,
    b_fc1,
    w_fc2,
    b_fc2,
    gain_two,
    shift_two,
    cotangent,
):
    n = lax.axis_size("fsdp")
    q = lax.axis_index("dp")
    f = lax.axis_index("fsdp")
    row_count, width = tokens.shape
    rows = width // n
    ff = b_fc1.shape[0] * n
    ffq = ff // n // 4
    quarter = width // 4
    n_img = scale_codes.shape[0]
    patches = row_count // n_img
    head_size = width // HEADS
    factor = 1.0 / math.sqrt(head_size)
    shard_order = jnp.asarray(masks(n), jnp.int32) ^ f
    group_order = jnp.arange(4, dtype=jnp.int32) ^ q
    order = jnp.concatenate([shard_order, group_order])

    def pick(value, axis):
        return lax.dynamic_index_in_dim(value, q, axis, keepdims=False)

    small = jnp.concatenate(
        [b_q, b_v, b_out, gain_one, shift_one, b_fc2, gain_two, shift_two, b_fc1]
    ).astype(half)
    pad = -small.shape[0] % 2048
    small_held = gather_shards(jnp.pad(small, (0, pad)).reshape(-1, 128), n).reshape(n, -1)
    inverse = jnp.zeros((n,), jnp.int32).at[shard_order].set(jnp.arange(n, dtype=jnp.int32))
    small_all = jnp.take(small_held, inverse, axis=0).astype(full)
    vectors = [small_all[:, i * rows : (i + 1) * rows].reshape(width) for i in range(8)]
    full_bq, full_bv, full_bout, gain_one_f, shift_one_f, full_bfc2, gain_two_f, shift_two_f = vectors
    bias_units = small_all[:, 8 * rows : 8 * rows + 4 * ffq].reshape(n, 4, ffq)
    bias_fc1 = jnp.take(bias_units, group_order, axis=1).transpose(1, 0, 2).reshape(ff)

    qkv_own = pick(w_qkv.reshape(rows, 3, 4, quarter), 2).reshape(rows, 3 * quarter).astype(half)
    qkv_parts = gather_quarters(qkv_own, n)
    out_own = pick(w_out.reshape(rows, 4, quarter), 1).astype(half)
    fc1_own = pick(w_fc1.reshape(rows, n, 4, ffq), 2).reshape(rows, n * ffq).astype(half)
    up_parts = gather_quarters(jnp.concatenate([fc1_own, out_own], axis=1), n)
    fc2_own = pick(w_fc2.reshape(4, ffq, width), 0).astype(half)
    column = gather_shards(fc2_own, n, 1)
    both = jnp.stack([column, x_swap(column)])
    far = swap(both, "fsdp", n, 0)
    down_own = jnp.concatenate([both[0], far[0]])
    down_across = jnp.concatenate([both[1], far[1]])
    down_parts = (down_own, core_swap(down_own), down_across, core_swap(down_across))

    hidden = n * ffq

    def plan_qkv(r, order_ref, ins, outs):
        s = order_ref[r]
        for j in range(4):
            for t in range(3):
                yield (
                    ins[j].at[r, :, pl.ds(t * quarter, quarter)],
                    outs[0].at[pl.ds(s * rows, rows), pl.ds(t * width + order_ref[n + j] * quarter, quarter)],
                )

    def plan_up(r, order_ref, ins, outs):
        s = order_ref[r]
        for j in range(4):
            yield ins[j].at[r, :, pl.ds(0, hidden)], outs[0].at[pl.ds(s * rows, rows), pl.ds(j * hidden, hidden)]
            yield (
                ins[j].at[r, :, pl.ds(hidden, quarter)],
                outs[1].at[pl.ds(s * rows, rows), pl.ds(order_ref[n + j] * quarter, quarter)],
            )

    def plan_down(r, order_ref, ins, outs):
        s = order_ref[r]
        for j in range(4):
            yield ins[j].at[r], outs[0].at[pl.ds(j * hidden + s * ffq, ffq)]

    (full_qkv,) = moved(qkv_parts, [(width, 3 * width)], n, plan_qkv, order)
    full_fc1, full_out = moved(up_parts, [(width, ff), (width, width)], n, plan_up, order)
    (full_fc2,) = moved(down_parts, [(ff, width)], n, plan_down, order)

    places = table(scale_codes, width)
    row_place = jnp.broadcast_to(places[:, :, None], (n_img, GRID, GRID, width // 2))
    col_place = jnp.broadcast_to(places[:, None], (n_img, GRID, GRID, width // 2))
    place = jnp.concatenate([row_place, col_place], axis=-1).reshape(row_count, width)
    x_zero = tokens.astype(full) + place
    normed_one = norm_affine(x_zero, gain_one_f, shift_one_f).astype(half)
    qkv_bias = jnp.concatenate([full_bq, jnp.zeros_like(full_bq), full_bv])
    projected = (
        (matmul(normed_one, full_qkv) + qkv_bias)
        .astype(half)
        .reshape(n_img, patches, 3, HEADS, head_size)
    )
    queries = projected[:, :, 0]
    keys_all = projected[:, :, 1]
    values_all = projected[:, :, 2]
    scores = (
        jnp.einsum("iqhd,ikhd->ihqk", queries, keys_all, preferred_element_type=full)
        * factor
    )
    top_score = jnp.max(scores, axis=-1, keepdims=True)
    raised = jnp.exp(scores - top_score)
    totals = jnp.sum(raised, axis=-1, keepdims=True)
    probs = raised / totals
    log_total = top_score + jnp.log(totals)
    mixed = jnp.einsum(
        "ihqk,ikhd->iqhd", probs.astype(half), values_all, preferred_element_type=full
    )
    mixed = mixed.reshape(row_count, width).astype(half)
    after_attn = x_zero + (matmul(mixed, full_out) + full_bout)
    normed_two = norm_affine(after_attn, gain_two_f, shift_two_f).astype(half)
    hidden_pre = matmul(normed_two, full_fc1) + bias_fc1
    hidden_act = jax.nn.gelu(hidden_pre, approximate=False).astype(half)
    block_out = (after_attn + (matmul(hidden_act, full_fc2) + full_bfc2)).astype(half)

    grad_w_fc2 = inner_rows(hidden_act, cotangent).astype(half)
    grad_b_fc2 = column_total(cotangent)
    grad_act = times_transposed(cotangent, full_fc2)
    unused_act, gelu_pull = jax.vjp(lambda pre: jax.nn.gelu(pre, approximate=False), hidden_pre)
    grad_pre = gelu_pull(grad_act)[0].astype(half)
    grad_w_fc1 = inner_rows(normed_two, grad_pre).astype(half)
    grad_b_fc1 = column_total(grad_pre)

    def plan_down_back(r, order_ref, ins, outs):
        s = order_ref[r]
        for j in range(4):
            yield ins[0].at[pl.ds(j * hidden + s * ffq, ffq)], outs[j].at[r]

    def plan_up_back(r, order_ref, ins, outs):
        s = order_ref[r]
        for j in range(4):
            yield ins[0].at[pl.ds(s * rows, rows), pl.ds(j * hidden, hidden)], outs[j].at[r]

    down_grads = moved([grad_w_fc2], [(n, ffq, width)] * 4, n, plan_down_back, order)
    up_grads = moved([grad_w_fc1], [(n, rows, hidden)] * 4, n, plan_up_back, order)

    middle = n // 2
    pair_low, pair_high = [], []
    for a, b in ((0, 1), (2, 3)):
        got = core_swap(down_grads[b])
        pair_low.append(add_half(down_grads[a][:middle], got[:middle]))
        pair_high.append(add_half(down_grads[a][middle:], got[middle:]))
    far = swap(jnp.stack(pair_high), "fsdp", n, 0)
    across = x_swap(add_half(pair_low[1], far[1]))
    down_low = (pair_low[0].astype(full) + far[0].astype(full) + across.astype(full)).astype(half)
    for bit in range(1, n.bit_length() - 1):
        size = down_low.shape[0] // 2
        got = swap(down_low[size:], "fsdp", n, bit)
        down_low = add_half(down_low[:size], got)
    down_pieces = spread_quarters(down_low[0], q)
    out_fc2 = jnp.concatenate(down_pieces).astype(full)
    up_pieces = spread_quarters(reduce_quarters(up_grads, n), q)
    out_fc1 = (
        jnp.stack([p.reshape(rows, n, ffq) for p in up_pieces], axis=2).reshape(rows, ff).astype(full)
    )

    grad_two_in = times_transposed(grad_pre, full_fc1)
    unused_two, norm_two_pull = jax.vjp(norm_affine, after_attn, gain_two_f, shift_two_f)
    part_two, grad_gain_two, grad_shift_two = norm_two_pull(grad_two_in)
    grad_after = cotangent.astype(full) + part_two
    branch_grad = grad_after.astype(half)
    grad_w_out = inner_rows(mixed, branch_grad).astype(half)
    grad_b_out = column_total(branch_grad)
    grad_mixed = (
        times_transposed(branch_grad, full_out)
        .astype(half)
        .reshape(n_img, patches, HEADS, head_size)
    )
    again_scores = (
        jnp.einsum("iqhd,ikhd->ihqk", queries, keys_all, preferred_element_type=full)
        * factor
    )
    again_probs = jnp.exp(again_scores - log_total)
    grad_values = jnp.einsum(
        "ihqk,iqhd->ikhd", again_probs.astype(half), grad_mixed, preferred_element_type=full
    )
    grad_probs = jnp.einsum(
        "iqhd,ikhd->ihqk", grad_mixed, values_all, preferred_element_type=full
    )
    weighted = jnp.sum(again_probs * grad_probs, axis=-1, keepdims=True)
    grad_scores = (again_probs * (grad_probs - weighted)).astype(half)
    grad_queries = (
        jnp.einsum("ihqk,ikhd->iqhd", grad_scores, keys_all, preferred_element_type=full)
        * factor
    )
    grad_keys = (
        jnp.einsum("ihqk,iqhd->ikhd", grad_scores, queries, preferred_element_type=full)
        * factor
    )
    grad_proj = (
        jnp.stack([grad_queries, grad_keys, grad_values], axis=2)
        .reshape(row_count, 3 * width)
        .astype(half)
    )
    grad_w_qkv = inner_rows(normed_one, grad_proj).astype(half)
    grad_b_q = column_total(grad_proj[:, :width])
    grad_b_v = column_total(grad_proj[:, 2 * width :])

    def plan_attn_back(r, order_ref, ins, outs):
        s = order_ref[r]
        for j in range(4):
            for t in range(3):
                yield (
                    ins[0].at[pl.ds(s * rows, rows), pl.ds(t * width + order_ref[n + j] * quarter, quarter)],
                    outs[j].at[r, :, pl.ds(t * quarter, quarter)],
                )
            yield (
                ins[1].at[pl.ds(s * rows, rows), pl.ds(order_ref[n + j] * quarter, quarter)],
                outs[j].at[r, :, pl.ds(3 * quarter, quarter)],
            )

    attn_grads = moved([grad_w_qkv, grad_w_out], [(n, rows, width)] * 4, n, plan_attn_back, order)
    attn_pieces = spread_quarters(reduce_quarters(attn_grads, n), q)
    out_qkv = (
        jnp.stack([p[:, : 3 * quarter].reshape(rows, 3, quarter) for p in attn_pieces], axis=2)
        .reshape(rows, 3 * width)
        .astype(full)
    )
    out_out = jnp.stack([p[:, 3 * quarter :] for p in attn_pieces], axis=1).reshape(rows, width).astype(full)

    grad_one_in = times_transposed(grad_proj, full_qkv)
    unused_one, norm_one_pull = jax.vjp(norm_affine, x_zero, gain_one_f, shift_one_f)
    part_one, grad_gain_one, grad_shift_one = norm_one_pull(grad_one_in)
    grad_tokens = grad_after + part_one

    sums = [
        grad_b_q, grad_b_v, grad_b_out, grad_gain_one, grad_shift_one, grad_b_fc2, grad_gain_two, grad_shift_two
    ]
    back_group = jnp.take(grad_b_fc1.reshape(4, n, ffq), group_order, axis=0).transpose(1, 0, 2)
    packed = jnp.concatenate([s.reshape(n, rows) for s in sums] + [back_group.reshape(n, 4 * ffq)], axis=1)
    packed = jnp.take(packed, shard_order, axis=0)
    pad = -packed.shape[1] % 1024
    packed = jnp.pad(packed, ((0, 0), (0, pad))).reshape(n, -1, 128)
    packed = packed + core_swap(packed)
    packed = packed + x_swap(packed)
    for bit in range(n.bit_length() - 1):
        size = packed.shape[0] // 2
        packed = packed[:size] + swap(packed[size:], "fsdp", n, bit)
    vector = packed.reshape(-1)
    small_out = [vector[i * rows : (i + 1) * rows] for i in range(8)]
    out_bfc1 = vector[8 * rows : 8 * rows + 4 * ffq]
    o_bq, o_bv, o_bout, o_gone, o_sone, o_bfc2, o_gtwo, o_stwo = small_out
    return (
        block_out,
        grad_tokens,
        out_qkv,
        o_bq,
        o_bv,
        out_out,
        o_bout,
        o_gone,
        o_sone,
        out_fc1,
        out_bfc1,
        out_fc2,
        o_bfc2,
        o_gtwo,
        o_stwo,
    )


def solution(mesh):
    rows_split = P(("dp", "fsdp"), None)
    matrix = P("fsdp", None)
    vector = P("fsdp")
    return jax.shard_map(
        local,
        mesh=mesh,
        in_specs=(
            rows_split, P(("dp", "fsdp")), matrix, vector, vector, matrix, vector, vector, vector,
            matrix, vector, matrix, vector, vector, vector, rows_split,
        ),
        out_specs=(
            rows_split, rows_split, matrix, vector, vector, matrix, vector, vector, vector,
            matrix, vector, matrix, vector, vector, vector,
        ),
        check_vma=False,
    )
```

time: 1440 us -> 2240 us (1.56)
  Pallas kernels: 0 us -> 1540 us
  waiting for transfers between devices: 858 us -> 267 us
  blocking collectives: 214 us -> 0 us
  starting transfers between devices: 0.37 us -> 44.4 us
  local copies, waits for them, and re-layouts: 84.6 us -> 112 us
    pallas_call x0 -> x6, Pallas kernels: none -> 1540 us  [moved(): pl.pallas_call(kernel, out_shape=shapes, grid_spec=pltpu.PrefetchScalarGr...]
    reduce_scatter x4 -> x0, waiting for transfers between devices: 647 us -> none  [the longest x1 284 us: local(): lax.psum_scatter(grad_w_fc1, 'fsdp', scatter_dimension=0, tiled=True)]
    ppermute x0 -> x50, waiting for transfers between devices: none -> 267 us  [swap(): return lax.ppermute(value, axis, [(i, i ^ 1 << bit) for i in range(size)])]
    all_gather x9 -> x0, blocking collectives: 171 us -> none  [the longest x1 26.3 us: local(): lax.all_gather(b_fc1.astype(half), 'fsdp', axis=0, tiled=True)]
    all_gather x4 -> x0, waiting for transfers between devices: 154 us -> none  [the longest x1 112 us: local(): lax.all_gather(w_fc2.astype(half), 'fsdp', axis=0, tiled=True)]
    psum x1 -> x0, waiting for transfers between devices: 57.3 us -> none  [local(): lax.psum(attn_shards[0].astype(jnp.bfloat16), 'dp').astype(jnp.float32)]
    ppermute x0 -> x50, starting transfers between devices: none -> 44.4 us  [swap(): return lax.ppermute(value, axis, [(i, i ^ 1 << bit) for i in range(size)])]
    unnamed x1 -> x0, blocking collectives: 36.7 us -> none
  transfers between devices with their start and end apart: 9 -> 50, of which waited for: 6 -> 24; matrix products, arithmetic and copies ran while one was open for 18% -> 7% of each run, Pallas kernels for 0% -> 32%
where the time goes in v1:
time: 2240 us; the launch traced here: 2230 us
  Pallas kernels  1540 us (69%)
  waiting for transfers between devices  267 us (12%)
  matrix products  183 us (8%)
  local copies, waits for them, and re-layouts  112 us (5%)
  other arithmetic  89.8 us (4%)
  starting transfers between devices  44.4 us (2%)
    pallas_call x6, Pallas kernels, moved(): pl.pallas_call(kernel, out_shape=shapes, grid_spec=pltpu.PrefetchScalarGr...  1540 us
    ppermute x50, waiting for transfers between devices, swap(): return lax.ppermute(value, axis, [(i, i ^ 1 << bit) for i in range(size)])  267 us
    dot_general x4, matrix products, matmul(): return jnp.dot(left, right, preferred_element_type=full)  66.8 us
    dot_general x4, matrix products, times_transposed(): lax.dot_general(left, right, (((1,), (1,)), ((), ())), preferred_element_...  49.2 us
  transfers between devices with their start and end apart: 50, of which 24 were waited for; matrix products, arithmetic and copies ran while one was open for 7% of the time, Pallas kernels for 32%

profile of v1, /device:TPU:0, one launch (start us, length us, event | category | flops | bytes accessed | tf_op | source)
XLA Modules:
  0.0 2233.9 jit_solution(4012374980890234611)
XLA Ops:
  25.9 4.7 reshape.314
  33.5 10.1 collective-permute-done.3
  47.3 10.5 collective-permute-done.4
  60.4 8.5 collective-permute-done.16
  72.9 5.4 collective-permute-done.5
  80.9 6.5 collective-permute-done.1
  101.5 26.6 %collective-permute-done.7.refs_2_ = bf16[8,128,768]{2,1,0:T(8,128)(2,1)} collective-permute-done((bf16[8,128,768]{2,1,0:T(8,128)(2,1)S(1)}, bf16[8,128,768]{2,1,0:T(8,128)(2,1)}, u32[]{:S(2)}, u32[]{:S(2)}) %collective-permute-start.7) | collective-permute-done | bytes 1572896 | tf_op jit(solution)/shard_map/ppermute | solution.py:19
  128.8 42.2 %collective-permute-done.11 = bf16[4,128,1280]{2,1,0:T(8,128)(2,1)} collective-permute-done((bf16[4,128,1280]{2,1,0:T(8,128)(2,1)}, bf16[4,128,1280]{2,1,0:T(8,128)(2,1)}, u32[]{:S(2)}, u32[]{:S(2)}) %collective-permute-start.11) | collective-permute-done | bytes 1310752 | tf_op jit(solution)/shard_map/ppermute | solution.py:19
  181.8 192.4 %moved.6 = bf16[1024,3072]{1,0:T(8,128)(2,1)} custom-call(s32[12]{0:T(128)} %pad_add_fusion.order_ref, bf16[8,128,768]{2,1,0:T(8,128)(2,1)} %copy-done.16, bf16[8,128,768]{2,1,0:T(8,128)(2,1)} %copy-done.27, bf16[8,128,768]{2,1,0:T(8,128)(2,1)} %collective-permute-done.7.refs_2_, bf16[8,128,768]{2,1,0:T(8,128)(2,1)} %collective-permute-done.8.refs_3_), custom_call_target="tpu_custom_call" | custom-call | tf_op jit(solution)/shard_map/moved/pallas_call | solution.py:103
  374.2 10.0 add_convert_fusion
  384.2 12.8 reshape.383
  396.9 6.9 fusion.62
  403.9 5.3 copy.116
  409.1 4.3 copy.117
  413.4 6.1 copy.118
  436.4 255.9 %moved.8 = bf16[4096,1024]{1,0:T(8,128)(2,1)} custom-call(s32[12]{0:T(128)} %pad_add_fusion.order_ref, bf16[8,128,1024]{2,1,0:T(8,128)(2,1)} %pad_maximum_fusion.4.refs_0_, bf16[8,128,1024]{2,1,0:T(8,128)(2,1)} %collective-permute-done.19.refs_1_, bf16[8,128,1024]{2,1,0:T(8,128)(2,1)} %pad_maximum_fusion.5.refs_2_, ...), custom_call_target="tpu_custom_call" | custom-call | tf_op jit(solution)/shard_map/moved/pallas_call | solution.py:103
  692.4 319.6 %moved.7 = (bf16[1024,4096]{1,0:T(8,128)(2,1)}, bf16[1024,1024]{1,0:T(8,128)(2,1)}) custom-call(s32[12]{0:T(128)} %pad_add_fusion.order_ref, bf16[8,128,1280]{2,1,0:T(8,128)(2,1)} %pad_maximum_fusion.2.refs_0_, bf16[8,128,1280]{2,1,0:T(8,128)(2,1)} %collective-permute-done.12.refs_1_, bf16[8,128,1280]{2,1,0:T(8,128)(2,1)} %collective-permute-done.13.refs_2_, ...), custom_call_target="tpu_custom_call" | custom-call | tf_op jit(solution)/shard_map/moved/pallas_call | solution.py:103
  1012.0 4.8 fusion.64
  1017.3 39.8 %multiply_convert_fusion.1 = (bf16[784,4096]{1,0:T(8,128)(2,1)}, f32[784,4096]{1,0:T(8,128)}, f32[784,4096]{1,0:T(8,128)}) fusion(f32[4096]{0:T(1024)S(1)} %select_bitcast_fusion, bf16[1024,4096]{1,0:T(8,128)(2,1)S(1)} %bitcast.314, f32[784,1024]{1,0:T(8,128)S(1)} %get-tuple-element.145, f32[1024]{0:T(1024)S(1)} %get-tuple-element.124, ...), kind=kOutput, calls=%fused_computation.22 | convolution fusion | flops 6792626176 | bytes 43743360 | tf_op jit(solution)/shard_map/dot_general | solution.py:134
  1057.1 19.5 convert_reduce_fusion
  1076.6 13.1 multiply_reduce_fusion.2
  1089.8 12.4 convolution_convert_fusion.refs_0_
  1112.8 5.4 reshape.384
  1118.2 4.3 copy.91
  1122.5 7.4 convert_bitcast_fusion
  1129.9 9.4 multiply_reduce_fusion
  1139.3 10.1 multiply_convert_fusion
  1152.9 4.3 pad_maximum_fusion
  1157.2 11.5 copy.96
  1168.7 12.4 convert_element_type.416
  1181.2 13.6 multiply_reduce_fusion.3
  1196.7 9.4 convolution_convert_fusion.2.refs_0_
  1206.8 256.0 %moved.10 = (bf16[8,128,1024]{2,1,0:T(8,128)(2,1)}, bf16[8,128,1024]{2,1,0:T(8,128)(2,1)}, bf16[8,128,1024]{2,1,0:T(8,128)(2,1)}, bf16[8,128,1024]{2,1,0:T(8,128)(2,1)}) custom-call(s32[12]{0:T(128)} %pad_add_fusion.order_ref, bf16[1024,4096]{1,0:T(8,128)(2,1)} %convolution_convert_fusion.refs_0_), custom_call_target="tpu_custom_call" | custom-call | tf_op jit(solution)/shard_map/moved/pallas_call | solution.py:103
  1462.9 14.1 convolution_convert_fusion.1.refs_0_
  1477.0 256.0 %moved.11 = (bf16[8,128,1024]{2,1,0:T(8,128)(2,1)}, bf16[8,128,1024]{2,1,0:T(8,128)(2,1)}, bf16[8,128,1024]{2,1,0:T(8,128)(2,1)}, bf16[8,128,1024]{2,1,0:T(8,128)(2,1)}) custom-call(s32[12]{0:T(128)} %pad_add_fusion.order_ref, bf16[4096,1024]{1,0:T(8,128)(2,1)} %convolution_convert_fusion.1.refs_0_), custom_call_target="tpu_custom_call" | custom-call | tf_op jit(solution)/shard_map/moved/pallas_call | solution.py:103
  1734.1 5.4 fusion.58
  1739.6 255.9 %moved.9 = (bf16[8,128,1024]{2,1,0:T(8,128)(2,1)}, bf16[8,128,1024]{2,1,0:T(8,128)(2,1)}, bf16[8,128,1024]{2,1,0:T(8,128)(2,1)}, bf16[8,128,1024]{2,1,0:T(8,128)(2,1)}) custom-call(s32[12]{0:T(128)} %pad_add_fusion.order_ref, bf16[1024,3072]{1,0:T(8,128)(2,1)} %convolution_convert_fusion.2.refs_0_, bf16[1024,1024]{1,0:T(8,128)(2,1)} %convolution_convert_fusion.3.refs_1_), custom_call_target="tpu_custom_call" | custom-call | tf_op jit(solution)/shard_map/moved/pallas_call | solution.py:103
  1995.6 5.3 convert_reduce_fusion.1
  2029.3 36.5 %collective-permute-done.44 = bf16[2,4,128,1024]{3,2,1,0:T(8,128)(2,1)} collective-permute-done((bf16[2,4,128,1024]{3,2,1,0:T(8,128)(2,1)}, bf16[2,4,128,1024]{3,2,1,0:T(8,128)(2,1)}, u32[]{:S(2)}, u32[]{:S(2)}) %collective-permute-start.44) | collective-permute-done | bytes 2097184 | tf_op jit(solution)/shard_map/ppermute | solution.py:19
  2072.2 4.5 add_convert_fusion.11
  2077.3 39.8 %collective-permute-done.23 = bf16[8,128,1024]{2,1,0:T(8,128)(2,1)} collective-permute-done((bf16[8,128,1024]{2,1,0:T(8,128)(2,1)}, bf16[8,128,1024]{2,1,0:T(8,128)(2,1)}, u32[]{:S(2)}, u32[]{:S(2)}) %collective-permute-start.23) | collective-permute-done | bytes 2097184 | tf_op jit(solution)/shard_map/ppermute | solution.py:19
  2121.7 12.2 add_convert_fusion.3
  2136.4 7.3 collective-permute-done.24
  2150.7 16.7 collective-permute-done.25
  2167.6 7.7 collective-permute-done.39
  2179.2 11.3 collective-permute-done.26
  2197.8 7.8 collective-permute-done.41
  2205.9 10.9 collective-permute-done.28
  (369 shorter events, 179.2 us)
Async XLA Ops:
  8.4 62.5 %collective-permute-start = (bf16[1,16,128]{2,1,0:T(8,128)(2,1)S(1)}, bf16[1,16,128]{2,1,0:T(8,128)(2,1)S(1)}, u32[]{:S(2)}, u32[]{:S(2)}) collective-permute-start(bf16[1,16,128]{2,1,0:T(8,128)(2,1)S(1)} %get-tuple-element.139), channel_id=1, source_target_pairs={{0,4},{1,5},{2,6},{3,7},{4,0},{5,1},{6,2},{7,3},{8,12},{9,13},{10,... | collective-permute-start | bytes 12296 | tf_op jit(solution)/shard_map/ppermute | solution.py:19
  12.5 32.1 %collective-permute-start.15 = (bf16[1,128,1024]{2,1,0:T(8,128)(2,1)S(1)}, bf16[1,128,1024]{2,1,0:T(8,128)(2,1)S(1)}, u32[]{:S(2)}, u32[]{:S(2)}) collective-permute-start(bf16[1,128,1024]{2,1,0:T(8,128)(2,1)S(1)} %dynamic-slice_convert_fusion), channel_id=1, source_target_pairs={{0,4},{1,5},{2,6},{3,7},{4,0},{5,1},{6,2},{7,3},{8,12},{9,13},{10,... | collective-permute-start | bytes 786440 | tf_op jit(solution)/shard_map/ppermute | solution.py:19
  14.6 29.0 %collective-permute-start.3 = (bf16[1,128,768]{2,1,0:T(8,128)(2,1)S(1)}, bf16[1,128,768]{2,1,0:T(8,128)(2,1)}, u32[]{:S(2)}, u32[]{:S(2)}) collective-permute-start(bf16[1,128,768]{2,1,0:T(8,128)(2,1)S(1)} %copy.80), channel_id=1, source_target_pairs={{0,4},{1,5},{2,6},{3,7},{4,0},{5,1},{6,2},{7,3},{8,12},{9,13},{10,... | collective-permute-start | bytes 589832 | tf_op jit(solution)/shard_map/ppermute | solution.py:19
  21.2 49.5 %collective-permute-start.9 = (bf16[1,128,1280]{2,1,0:T(8,128)(2,1)S(1)}, bf16[1,128,1280]{2,1,0:T(8,128)(2,1)S(1)}, u32[]{:S(2)}, u32[]{:S(2)}) collective-permute-start(bf16[1,128,1280]{2,1,0:T(8,128)(2,1)S(1)} %maximum_bitcast_fusion), channel_id=1, source_target_pairs={{0,4},{1,5},{2,6},{3,7},{4,0},{5,1},{6,2},{7,3},{8,12},{9,13},{10,... | collective-permute-start | bytes 983048 | tf_op jit(solution)/shard_map/ppermute | solution.py:19
  44.5 13.3 collective-permute-start.4
  44.7 24.3 %collective-permute-start.16 = (bf16[2,128,1024]{2,1,0:T(8,128)(2,1)S(1)}, bf16[2,128,1024]{2,1,0:T(8,128)(2,1)S(1)}, u32[]{:S(2)}, u32[]{:S(2)}) collective-permute-start(bf16[2,128,1024]{2,1,0:T(8,128)(2,1)S(1)} %pad_maximum_fusion.12), channel_id=1, source_target_pairs={{0,2},{1,3},{2,0},{3,1},{4,6},{5,7},{6,4},{7,5},{8,10},{9,11},{10,... | collective-permute-start | bytes 1572872 | tf_op jit(solution)/shard_map/ppermute | solution.py:19
  58.8 19.4 collective-permute-start.5
  69.1 26.1 %collective-permute-start.17 = (bf16[4,128,1024]{2,1,0:T(8,128)(2,1)S(1)}, bf16[4,128,1024]{2,1,0:T(8,128)(2,1)S(1)}, u32[]{:S(2)}, u32[]{:S(2)}) collective-permute-start(bf16[4,128,1024]{2,1,0:T(8,128)(2,1)S(1)} %get-tuple-element.121), channel_id=1, source_target_pairs={{0,16},{8,24},{16,0},{24,8},{1,17},{9,25},{17,1},{25,9},{2,18},{10... | collective-permute-start | bytes 3145736 | tf_op jit(solution)/shard_map/ppermute | solution.py:19
  70.8 27.6 %collective-permute-start.10 = (bf16[2,128,1280]{2,1,0:T(8,128)(2,1)S(1)}, bf16[2,128,1280]{2,1,0:T(8,128)(2,1)S(1)}, u32[]{:S(2)}, u32[]{:S(2)}) collective-permute-start(bf16[2,128,1280]{2,1,0:T(8,128)(2,1)S(1)} %pad_maximum_fusion.11), channel_id=1, source_target_pairs={{0,2},{1,3},{2,0},{3,1},{4,6},{5,7},{6,4},{7,5},{8,10},{9,11},{10,... | collective-permute-start | bytes 1966088 | tf_op jit(solution)/shard_map/ppermute | solution.py:19
  70.9 16.5 collective-permute-start.1
  79.4 48.7 %collective-permute-start.7 = (bf16[8,128,768]{2,1,0:T(8,128)(2,1)S(1)}, bf16[8,128,768]{2,1,0:T(8,128)(2,1)}, u32[]{:S(2)}, u32[]{:S(2)}) collective-permute-start(bf16[8,128,768]{2,1,0:T(8,128)(2,1)S(1)} %pad_maximum_fusion.7.refs_0_), channel_id=1, source_target_pairs={{0,16},{8,24},{16,0},{24,8},{1,17},{9,25},{17,1},{25,9},{2,18},{10... | collective-permute-start | bytes 4718600 | tf_op jit(solution)/shard_map/ppermute | solution.py:19
  87.4 3.7 collective-permute-start.2
  96.8 78.5 %collective-permute-start.18 = (bf16[2,4,128,1024]{3,2,1,0:T(8,128)(2,1)}, bf16[2,4,128,1024]{3,2,1,0:T(8,128)(2,1)}, u32[]{:S(2)}, u32[]{:S(2)}) collective-permute-start(bf16[2,4,128,1024]{3,2,1,0:T(8,128)(2,1)} %pad_maximum_fusion.3), channel_id=1, source_target_pairs={{0,1},{1,0},{2,3},{3,2},{4,5},{5,4},{6,7},{7,6},{8,9},{9,8},{10,11... | collective-permute-start | bytes 6291464 | tf_op jit(solution)/shard_map/ppermute | solution.py:19
  99.6 71.4 %collective-permute-start.11 = (bf16[4,128,1280]{2,1,0:T(8,128)(2,1)}, bf16[4,128,1280]{2,1,0:T(8,128)(2,1)}, u32[]{:S(2)}, u32[]{:S(2)}) collective-permute-start(bf16[4,128,1280]{2,1,0:T(8,128)(2,1)} %pad_maximum_fusion.8), channel_id=1, source_target_pairs={{0,1},{1,0},{2,3},{3,2},{4,5},{5,4},{6,7},{7,6},{8,9},{9,8},{10,11... | collective-permute-start | bytes 3932168 | tf_op jit(solution)/shard_map/ppermute | solution.py:19
  101.4 79.2 %collective-permute-start.6 = (bf16[8,128,768]{2,1,0:T(8,128)(2,1)S(1)}, bf16[8,128,768]{2,1,0:T(8,128)(2,1)S(1)}, u32[]{:S(2)}, u32[]{:S(2)}) collective-permute-start(bf16[8,128,768]{2,1,0:T(8,128)(2,1)S(1)} %pad_maximum_fusion.7.refs_0_), channel_id=1, source_target_pairs={{0,8},{8,0},{16,24},{24,16},{1,9},{9,1},{17,25},{25,17},{2,10},{10... | collective-permute-start | bytes 4718600 | tf_op jit(solution)/shard_map/ppermute | solution.py:19
  128.1 53.7 %collective-permute-start.8 = (bf16[8,128,768]{2,1,0:T(8,128)(2,1)}, bf16[8,128,768]{2,1,0:T(8,128)(2,1)}, u32[]{:S(2)}, u32[]{:S(2)}) collective-permute-start(bf16[8,128,768]{2,1,0:T(8,128)(2,1)} %collective-permute-done.7.refs_2_), channel_id=1, source_target_pairs={{0,8},{8,0},{16,24},{24,16},{1,9},{9,1},{17,25},{25,17},{2,10},{10... | collective-permute-start | bytes 4718600 | tf_op jit(solution)/shard_map/ppermute | solution.py:19
  173.9 249.2 %collective-permute-start.13 = (bf16[8,128,1280]{2,1,0:T(8,128)(2,1)}, bf16[8,128,1280]{2,1,0:T(8,128)(2,1)}, u32[]{:S(2)}, u32[]{:S(2)}) collective-permute-start(bf16[8,128,1280]{2,1,0:T(8,128)(2,1)} %pad_maximum_fusion.2.refs_0_), channel_id=1, source_target_pairs={{0,16},{8,24},{16,0},{24,8},{1,17},{9,25},{17,1},{25,9},{2,18},{10... | collective-permute-start | bytes 7864328 | tf_op jit(solution)/shard_map/ppermute | solution.py:19
  175.4 517.0 %collective-permute-start.12 = (bf16[8,128,1280]{2,1,0:T(8,128)(2,1)}, bf16[8,128,1280]{2,1,0:T(8,128)(2,1)}, u32[]{:S(2)}, u32[]{:S(2)}) collective-permute-start(bf16[8,128,1280]{2,1,0:T(8,128)(2,1)} %pad_maximum_fusion.2.refs_0_), channel_id=1, source_target_pairs={{0,8},{8,0},{16,24},{24,16},{1,9},{9,1},{17,25},{25,17},{2,10},{10... | collective-permute-start | bytes 7864328 | tf_op jit(solution)/shard_map/ppermute | solution.py:19
  178.6 257.8 %collective-permute-start.19 = (bf16[8,128,1024]{2,1,0:T(8,128)(2,1)}, bf16[8,128,1024]{2,1,0:T(8,128)(2,1)}, u32[]{:S(2)}, u32[]{:S(2)}) collective-permute-start(bf16[8,128,1024]{2,1,0:T(8,128)(2,1)} %pad_maximum_fusion.4.refs_0_), channel_id=1, source_target_pairs={{0,8},{8,0},{16,24},{24,16},{1,9},{9,1},{17,25},{25,17},{2,10},{10... | collective-permute-start | bytes 6291464 | tf_op jit(solution)/shard_map/ppermute | solution.py:19
  181.8 254.6 %collective-permute-start.20 = (bf16[8,128,1024]{2,1,0:T(8,128)(2,1)}, bf16[8,128,1024]{2,1,0:T(8,128)(2,1)}, u32[]{:S(2)}, u32[]{:S(2)}) collective-permute-start(bf16[8,128,1024]{2,1,0:T(8,128)(2,1)} %pad_maximum_fusion.5.refs_2_), channel_id=1, source_target_pairs={{0,8},{8,0},{16,24},{24,16},{1,9},{9,1},{17,25},{25,17},{2,10},{10... | collective-permute-start | bytes 6291464 | tf_op jit(solution)/shard_map/ppermute | solution.py:19
  423.1 269.3 %collective-permute-start.14 = (bf16[8,128,1280]{2,1,0:T(8,128)(2,1)}, bf16[8,128,1280]{2,1,0:T(8,128)(2,1)}, u32[]{:S(2)}, u32[]{:S(2)}) collective-permute-start(bf16[8,128,1280]{2,1,0:T(8,128)(2,1)} %collective-permute-done.13.refs_2_), channel_id=1, source_target_pairs={{0,8},{8,0},{16,24},{24,16},{1,9},{9,1},{17,25},{25,17},{2,10},{10... | collective-permute-start | bytes 7864328 | tf_op jit(solution)/shard_map/ppermute | solution.py:19
  1733.0 278.7 %collective-permute-start.42 = (bf16[8,128,1024]{2,1,0:T(8,128)(2,1)}, bf16[8,128,1024]{2,1,0:T(8,128)(2,1)}, u32[]{:S(2)}, u32[]{:S(2)}) collective-permute-start(bf16[8,128,1024]{2,1,0:T(8,128)(2,1)} %get-tuple-element.40), channel_id=1, source_target_pairs={{0,8},{8,0},{16,24},{24,16},{1,9},{9,1},{17,25},{25,17},{2,10},{10... | collective-permute-start | bytes 6291464 | tf_op jit(solution)/shard_map/ppermute | solution.py:19
  1733.6 280.7 %collective-permute-start.43 = (bf16[8,128,1024]{2,1,0:T(8,128)(2,1)}, bf16[8,128,1024]{2,1,0:T(8,128)(2,1)}, u32[]{:S(2)}, u32[]{:S(2)}) collective-permute-start(bf16[8,128,1024]{2,1,0:T(8,128)(2,1)} %get-tuple-element.42), channel_id=1, source_target_pairs={{0,8},{8,0},{16,24},{24,16},{1,9},{9,1},{17,25},{25,17},{2,10},{10... | collective-permute-start | bytes 6291464 | tf_op jit(solution)/shard_map/ppermute | solution.py:19
  1733.7 284.3 %collective-permute-start.35 = (bf16[8,128,1024]{2,1,0:T(8,128)(2,1)}, bf16[8,128,1024]{2,1,0:T(8,128)(2,1)}, u32[]{:S(2)}, u32[]{:S(2)}) collective-permute-start(bf16[8,128,1024]{2,1,0:T(8,128)(2,1)} %get-tuple-element.38), channel_id=1, source_target_pairs={{0,8},{8,0},{16,24},{24,16},{1,9},{9,1},{17,25},{25,17},{2,10},{10... | collective-permute-start | bytes 6291464 | tf_op jit(solution)/shard_map/ppermute | solution.py:19
  1995.5 27.9 %collective-permute-start.22 = (bf16[8,128,1024]{2,1,0:T(8,128)(2,1)}, bf16[8,128,1024]{2,1,0:T(8,128)(2,1)}, u32[]{:S(2)}, u32[]{:S(2)}) collective-permute-start(bf16[8,128,1024]{2,1,0:T(8,128)(2,1)} %get-tuple-element.34), channel_id=1, source_target_pairs={{0,8},{8,0},{16,24},{24,16},{1,9},{9,1},{17,25},{25,17},{2,10},{10... | collective-permute-start | bytes 6291464 | tf_op jit(solution)/shard_map/ppermute | solution.py:19
  2003.3 4.4 collective-permute-start.30
  2007.7 4.0 collective-permute-start.31
  2011.7 58.2 %collective-permute-start.34 = (bf16[8,128,1024]{2,1,0:T(8,128)(2,1)}, bf16[8,128,1024]{2,1,0:T(8,128)(2,1)}, u32[]{:S(2)}, u32[]{:S(2)}) collective-permute-start(bf16[8,128,1024]{2,1,0:T(8,128)(2,1)} %get-tuple-element.36), channel_id=1, source_target_pairs={{0,8},{8,0},{16,24},{24,16},{1,9},{9,1},{17,25},{25,17},{2,10},{10... | collective-permute-start | bytes 6291464 | tf_op jit(solution)/shard_map/ppermute | solution.py:19
  2011.7 65.6 %collective-permute-start.21 = (bf16[8,128,1024]{2,1,0:T(8,128)(2,1)}, bf16[8,128,1024]{2,1,0:T(8,128)(2,1)}, u32[]{:S(2)}, u32[]{:S(2)}) collective-permute-start(bf16[8,128,1024]{2,1,0:T(8,128)(2,1)} %get-tuple-element.32), channel_id=1, source_target_pairs={{0,8},{8,0},{16,24},{24,16},{1,9},{9,1},{17,25},{25,17},{2,10},{10... | collective-permute-start | bytes 6291464 | tf_op jit(solution)/shard_map/ppermute | solution.py:19
  2014.3 13.6 collective-permute-start.32
  2017.9 47.9 %collective-permute-start.44 = (bf16[2,4,128,1024]{3,2,1,0:T(8,128)(2,1)}, bf16[2,4,128,1024]{3,2,1,0:T(8,128)(2,1)}, u32[]{:S(2)}, u32[]{:S(2)}) collective-permute-start(bf16[2,4,128,1024]{3,2,1,0:T(8,128)(2,1)} %pad_maximum_fusion.6), channel_id=1, source_target_pairs={{0,1},{1,0},{2,3},{3,2},{4,5},{5,4},{6,7},{7,6},{8,9},{9,8},{10,11... | collective-permute-start | bytes 6291464 | tf_op jit(solution)/shard_map/ppermute | solution.py:19
  2023.3 48.9 %collective-permute-start.36 = (bf16[8,128,1024]{2,1,0:T(8,128)(2,1)}, bf16[8,128,1024]{2,1,0:T(8,128)(2,1)}, u32[]{:S(2)}, u32[]{:S(2)}) collective-permute-start(bf16[8,128,1024]{2,1,0:T(8,128)(2,1)} %add_convert_fusion.1), channel_id=1, source_target_pairs={{0,16},{8,24},{16,0},{24,8},{1,17},{9,25},{17,1},{25,9},{2,18},{10... | collective-permute-start | bytes 6291464 | tf_op jit(solution)/shard_map/ppermute | solution.py:19
  2027.8 89.3 %collective-permute-start.23 = (bf16[8,128,1024]{2,1,0:T(8,128)(2,1)}, bf16[8,128,1024]{2,1,0:T(8,128)(2,1)}, u32[]{:S(2)}, u32[]{:S(2)}) collective-permute-start(bf16[8,128,1024]{2,1,0:T(8,128)(2,1)} %add_convert_fusion.2), channel_id=1, source_target_pairs={{0,16},{8,24},{16,0},{24,8},{1,17},{9,25},{17,1},{25,9},{2,18},{10... | collective-permute-start | bytes 6291464 | tf_op jit(solution)/shard_map/ppermute | solution.py:19
  2065.8 68.1 %collective-permute-start.33 = (f32[1,16,128]{2,1,0:T(8,128)S(1)}, f32[1,16,128]{2,1,0:T(8,128)S(1)}, u32[]{:S(2)}, u32[]{:S(2)}) collective-permute-start(f32[1,16,128]{2,1,0:T(8,128)S(1)} %slice.431), channel_id=1, source_target_pairs={{0,4},{1,5},{2,6},{3,7},{4,0},{5,1},{6,2},{7,3},{8,12},{9,13},{10,... | collective-permute-start | bytes 24584 | tf_op jit(solution)/shard_map/ppermute | solution.py:19
  2069.9 75.7 %collective-permute-start.45 = (bf16[4,128,1024]{2,1,0:T(8,128)(2,1)S(1)}, bf16[4,128,1024]{2,1,0:T(8,128)(2,1)S(1)}, u32[]{:S(2)}, u32[]{:S(2)}) collective-permute-start(bf16[4,128,1024]{2,1,0:T(8,128)(2,1)S(1)} %fusion.20), channel_id=1, source_target_pairs={{0,16},{8,24},{16,0},{24,8},{1,17},{9,25},{17,1},{25,9},{2,18},{10... | collective-permute-start | bytes 3145736 | tf_op jit(solution)/shard_map/ppermute | solution.py:19
  2076.6 57.3 %collective-permute-start.37 = (bf16[4,128,1024]{2,1,0:T(8,128)(2,1)S(1)}, bf16[4,128,1024]{2,1,0:T(8,128)(2,1)S(1)}, u32[]{:S(2)}, u32[]{:S(2)}) collective-permute-start(bf16[4,128,1024]{2,1,0:T(8,128)(2,1)S(1)} %get-tuple-element.97), channel_id=1, source_target_pairs={{0,1},{1,0},{2,3},{3,2},{4,5},{5,4},{6,7},{7,6},{8,9},{9,8},{10,11... | collective-permute-start | bytes 3145736 | tf_op jit(solution)/shard_map/ppermute | solution.py:19
  2121.0 22.7 %collective-permute-start.24 = (bf16[4,128,1024]{2,1,0:T(8,128)(2,1)S(1)}, bf16[4,128,1024]{2,1,0:T(8,128)(2,1)S(1)}, u32[]{:S(2)}, u32[]{:S(2)}) collective-permute-start(bf16[4,128,1024]{2,1,0:T(8,128)(2,1)S(1)} %get-tuple-element.99), channel_id=1, source_target_pairs={{0,1},{1,0},{2,3},{3,2},{4,5},{5,4},{6,7},{7,6},{8,9},{9,8},{10,11... | collective-permute-start | bytes 3145736 | tf_op jit(solution)/shard_map/ppermute | solution.py:19
  2134.3 14.5 collective-permute-start.38
  2144.1 23.4 %collective-permute-start.25 = (bf16[2,128,1024]{2,1,0:T(8,128)(2,1)S(1)}, bf16[2,128,1024]{2,1,0:T(8,128)(2,1)S(1)}, u32[]{:S(2)}, u32[]{:S(2)}) collective-permute-start(bf16[2,128,1024]{2,1,0:T(8,128)(2,1)S(1)} %get-tuple-element.103), channel_id=1, source_target_pairs={{0,2},{1,3},{2,0},{3,1},{4,6},{5,7},{6,4},{7,5},{8,10},{9,11},{10,... | collective-permute-start | bytes 1572872 | tf_op jit(solution)/shard_map/ppermute | solution.py:19
  2148.1 28.4 %collective-permute-start.46 = (bf16[2,128,1024]{2,1,0:T(8,128)(2,1)S(1)}, bf16[2,128,1024]{2,1,0:T(8,128)(2,1)S(1)}, u32[]{:S(2)}, u32[]{:S(2)}) collective-permute-start(bf16[2,128,1024]{2,1,0:T(8,128)(2,1)S(1)} %slice.463), channel_id=1, source_target_pairs={{0,2},{1,3},{2,0},{3,1},{4,6},{5,7},{6,4},{7,5},{8,10},{9,11},{10,... | collective-permute-start | bytes 1572872 | tf_op jit(solution)/shard_map/ppermute | solution.py:19
  2148.8 26.5 %collective-permute-start.39 = (bf16[1,128,1024]{2,1,0:T(8,128)(2,1)S(1)}, bf16[1,128,1024]{2,1,0:T(8,128)(2,1)S(1)}, u32[]{:S(2)}, u32[]{:S(2)}) collective-permute-start(bf16[1,128,1024]{2,1,0:T(8,128)(2,1)S(1)} %add_convert_fusion.21), channel_id=1, source_target_pairs={{0,4},{1,5},{2,6},{3,7},{4,0},{5,1},{6,2},{7,3},{8,12},{9,13},{10,... | collective-permute-start | bytes 786440 | tf_op jit(solution)/shard_map/ppermute | solution.py:19
  2167.5 23.0 %collective-permute-start.26 = (bf16[1,128,1024]{2,1,0:T(8,128)(2,1)S(1)}, bf16[1,128,1024]{2,1,0:T(8,128)(2,1)S(1)}, u32[]{:S(2)}, u32[]{:S(2)}) collective-permute-start(bf16[1,128,1024]{2,1,0:T(8,128)(2,1)S(1)} %add_convert_fusion.24), channel_id=1, source_target_pairs={{0,4},{1,5},{2,6},{3,7},{4,0},{5,1},{6,2},{7,3},{8,12},{9,13},{10,... | collective-permute-start | bytes 786440 | tf_op jit(solution)/shard_map/ppermute | solution.py:19
  2175.4 15.3 collective-permute-start.40
  2176.8 17.3 collective-permute-start.47
  2190.7 3.5 collective-permute-start.27
  2190.8 14.8 collective-permute-start.41
  2194.2 22.6 %collective-permute-start.28 = (bf16[2,128,1024]{2,1,0:T(8,128)(2,1)S(1)}, bf16[2,128,1024]{2,1,0:T(8,128)(2,1)S(1)}, u32[]{:S(2)}, u32[]{:S(2)}) collective-permute-start(bf16[2,128,1024]{2,1,0:T(8,128)(2,1)S(1)} %pad_maximum_fusion.13), channel_id=1, source_target_pairs={{0,16},{8,24},{16,0},{24,8},{1,17},{9,25},{17,1},{25,9},{2,18},{10... | collective-permute-start | bytes 1572872 | tf_op jit(solution)/shard_map/ppermute | solution.py:19
  2196.6 34.2 %collective-permute-start.49 = (bf16[2,128,1024]{2,1,0:T(8,128)(2,1)}, bf16[2,128,1024]{2,1,0:T(8,128)(2,1)}, u32[]{:S(2)}, u32[]{:S(2)}) collective-permute-start(bf16[2,128,1024]{2,1,0:T(8,128)(2,1)} %pad_maximum_fusion.15), channel_id=1, source_target_pairs={{0,16},{8,24},{16,0},{24,8},{1,17},{9,25},{17,1},{25,9},{2,18},{10... | collective-permute-start | bytes 1572872 | tf_op jit(solution)/shard_map/ppermute | solution.py:19
  (55 other events, 2612.3 us)

commit v2 on v1

v2 whole, which is shorter than its diff:
```python
import math

import jax
import jax.numpy as jnp
from jax import lax
from jax.experimental import pallas as pl
from jax.experimental.pallas import tpu as pltpu
from jax.sharding import PartitionSpec as P

HEADS = 16
GRID = 14
NSCALE = 16
norm_eps = 1e-06
half = jnp.bfloat16
full = jnp.float32


def swap(value, axis, size, bit):
    return lax.ppermute(value, axis, [(i, i ^ (1 << bit)) for i in range(size)])


def core_swap(value):
    return swap(value, "dp", 4, 0)


def x_swap(value):
    return swap(value, "dp", 4, 1)


def masks(n):
    found = [0]
    for bit in reversed(range(n.bit_length() - 1)):
        found = found + [m | (1 << bit) for m in found]
    return found


def gather_shards(piece, n, last=0):
    held = piece[None]
    for bit in reversed(range(last, n.bit_length() - 1)):
        held = jnp.concatenate([held, swap(held, "fsdp", n, bit)])
    return held


def gather_quarters(piece, n):
    own = gather_shards(piece, n)
    beside = core_swap(own)
    across = x_swap(own)
    return own, beside, across, core_swap(across)


def add_half(a, b):
    return (a.astype(full) + b.astype(full)).astype(half)


def scatter_shards(low, high, n):
    for bit in range(n.bit_length() - 1):
        got = swap(high, "fsdp", n, bit)
        size = low.shape[0] // 2
        if size:
            low, high = add_half(low[:size], got[:size]), add_half(low[size:], got[size:])
        else:
            low = add_half(low, got)
    return low[0]


def reduce_quarters(parts, n):
    middle = n // 2
    beside = core_swap(parts[1])
    across = add_half(parts[2], core_swap(parts[3]))
    got = x_swap(across)
    total = [
        (parts[0][s].astype(full) + beside[s].astype(full) + got[s].astype(full)).astype(half)
        for s in (slice(0, middle), slice(middle, None))
    ]
    return scatter_shards(total[0], total[1], n)


def spread_quarters(piece, q):
    pair = [piece, core_swap(piece)]
    there = x_swap(jnp.stack(pair))
    pieces = pair + [there[0], there[1]]
    odd = (q & 1) == 1
    upper = q >= 2
    once = [jnp.where(odd, pieces[i ^ 1], pieces[i]) for i in range(4)]
    return [jnp.where(upper, once[i ^ 2], once[i]) for i in range(4)]


ANYWHERE = pl.BlockSpec(memory_space=pl.ANY)
ON_CHIP = pl.BlockSpec(memory_space=pltpu.VMEM)
SCALARS = pl.BlockSpec(memory_space=pltpu.SMEM)


def dot(left, right, dim_left, dim_right):
    return lax.dot_general(
        left, right, (((dim_left,), (dim_right,)), ((), ())), preferred_element_type=full
    )


def call(kernel, name, operands, in_specs, outs, out_specs, scratch, flops, moved, transcendentals=0):
    return pl.pallas_call(
        kernel,
        out_shape=[jax.ShapeDtypeStruct(shape, kind) for shape, kind in outs],
        in_specs=in_specs,
        out_specs=out_specs,
        scratch_shapes=scratch,
        compiler_params=pltpu.CompilerParams(vmem_limit_bytes=58 * 2**20),
        cost_estimate=pl.CostEstimate(
            flops=flops, bytes_accessed=moved, transcendentals=transcendentals
        ),
        name=name,
    )(*operands)


def loop(count, body):
    def step(i, carry):
        body(i)
        return carry

    lax.fori_loop(0, count, step, 0)


def tile(i, size):
    return pl.ds(pl.multiple_of(i * size, size), size)


def head_rows(s, q, n, rows, quarter):
    per = n // 4
    return pl.multiple_of(((s // per) ^ q) * quarter + (s % per) * rows, rows)


def softmax_pair(q2, k2, patches):
    lane = lax.broadcasted_iota(jnp.int32, q2.shape, 1)
    first = lane < q2.shape[1] // 2
    zero = jnp.zeros_like(q2)
    both = jnp.concatenate([jnp.where(first, q2, zero), jnp.where(first, zero, q2)])
    scores = dot(both, k2, 1, 1)
    key = lax.broadcasted_iota(jnp.int32, scores.shape, 1)
    scores = jnp.where(key < patches, scores, -1e30)
    raised = jnp.exp(scores - jnp.max(scores, axis=-1, keepdims=True))
    probs = raised * (1.0 / jnp.sum(raised, axis=-1, keepdims=True))
    return both, probs, first


def attention_forward(order, normed, bias, weights, n_img, patches, factor):
    groups = len(weights)
    n, rows, wide = weights[0].shape
    count, width = normed.shape
    padded = count // n_img
    quarter = wide // 3

    def kernel(order_ref, normed_ref, bias_ref, *refs):
        w_refs, refs = refs[:groups], refs[groups:]
        qkv_refs, mixed_refs, (w_held, sems) = refs[:groups], refs[groups : 2 * groups], refs[2 * groups :]
        for g in range(groups):

            def start(r, g=g):
                at = pl.multiple_of(order_ref[r] * rows, rows)
                pltpu.make_async_copy(w_refs[g].at[r], w_held.at[g, pl.ds(at, rows)], sems.at[g]).start()

            loop(n, start)
        for g in range(groups):
            pltpu.make_async_copy(w_held.at[g], w_held.at[g], sems.at[g]).wait()

            def project(t, g=g):
                at = tile(t, quarter)
                product = dot(normed_ref[...], w_held[g, :, at], 1, 0)
                qkv_refs[g][:, at] = (product + bias_ref[g, :, at]).astype(half)

            loop(3, project)

            def attend(i, g=g):
                at = tile(i // 2, padded)
                lanes = [pl.ds(pl.multiple_of(t * quarter + (i % 2) * 128, 128), 128) for t in range(3)]
                q2 = qkv_refs[g][at, lanes[0]] * factor
                k2 = qkv_refs[g][at, lanes[1]]
                v2 = qkv_refs[g][at, lanes[2]]
                _, probs, first = softmax_pair(q2, k2, patches)
                out = dot(probs.astype(half), v2, 1, 0)
                mixed_refs[g][at, lanes[0]] = jnp.where(first, out[:padded], out[padded:]).astype(half)

            loop(2 * n_img, attend)

    return call(
        kernel,
        "attention_forward",
        (order, normed, bias, *weights),
        [SCALARS, ON_CHIP, ON_CHIP] + [ANYWHERE] * groups,
        [((count, wide), half)] * groups + [((count, quarter), half)] * groups,
        [ON_CHIP] * (2 * groups),
        [pltpu.VMEM((groups, width, wide), half), pltpu.SemaphoreType.DMA((groups,))],
        groups * 2 * count * width * wide,
        2 * (count * width + groups * (width * wide + count * (wide + quarter))),
    )


def layer_norm(value, gain, shift):
    center = jnp.mean(value, axis=-1, keepdims=True)
    offset = value - center
    spread = jnp.mean(offset * offset, axis=-1, keepdims=True)
    return offset * lax.rsqrt(spread + norm_eps) * gain + shift


def layer_norm_back(value, grad, gain):
    center = jnp.mean(value, axis=-1, keepdims=True)
    offset = value - center
    scale = lax.rsqrt(jnp.mean(offset * offset, axis=-1, keepdims=True) + norm_eps)
    unit = offset * scale
    scaled = grad * gain
    inner = jnp.mean(scaled * unit, axis=-1, keepdims=True)
    return scale * (scaled - jnp.mean(scaled, axis=-1, keepdims=True) - unit * inner), grad * unit


def load_out(order_ref, up_refs, held, sem, n, rows, hidden, quarter):
    q = order_ref[n]

    def start(r):
        at = head_rows(order_ref[r], q, n, rows, quarter)
        for j in range(4):
            column = pl.multiple_of((q ^ j) * quarter, quarter)
            pltpu.make_async_copy(
                up_refs[j].at[r, :, pl.ds(hidden, quarter)],
                held.at[pl.ds(at, rows), pl.ds(column, quarter)],
                sem,
            ).start()

    loop(n, start)


CHUNK = 16


def attention_out(order, x_zero, mixed, ups, bias, gain, shift):
    count, width = x_zero.shape
    n, rows, _ = ups[0].shape
    quarter = mixed[0].shape[1]
    hidden = ups[0].shape[2] - quarter

    def kernel(order_ref, x_ref, bias_ref, gain_ref, shift_ref, *refs):
        mixed_refs, up_refs = refs[:4], refs[4:8]
        after_ref, normed_ref, held, sems = refs[8:]
        load_out(order_ref, up_refs, held, sems.at[0], n, rows, hidden, quarter)
        together = jnp.concatenate([m[...] for m in mixed_refs], axis=1)
        pltpu.make_async_copy(held, held, sems.at[0]).wait()
        after_ref[...] = dot(together, held[...], 1, 0)

        def finish(i):
            at = tile(i, CHUNK)
            after = x_ref[at] + (after_ref[at] + bias_ref[...])
            after_ref[at] = after
            normed_ref[at] = layer_norm(after, gain_ref[...], shift_ref[...]).astype(half)

        loop(count // CHUNK, finish)

    return call(
        kernel,
        "attention_out",
        (order, x_zero, bias, gain, shift, *mixed, *ups),
        [SCALARS] + [ON_CHIP] * 8 + [ANYWHERE] * 4,
        [((count, width), full), ((count, width), half)],
        [ON_CHIP] * 2,
        [pltpu.VMEM((width, width), half), pltpu.SemaphoreType.DMA((1,))],
        2 * count * width * width,
        14 * count * width + 2 * width * width,
    )


def mlp(order, normed, cot, bias, ups, downs, carried=None, ending=None):
    groups = len(ups)
    count, width = normed.shape
    n, rows, _ = ups[0].shape
    share = downs[0].shape[1]
    hidden = n * share
    step = min(512, hidden)
    steps = hidden // step
    more = [] if carried is None else [*carried, *ending]

    def kernel(order_ref, normed_ref, cot_ref, bias_ref, *refs):
        more_refs, refs = refs[: len(more)], refs[len(more) :]
        up_refs, down_refs, refs = refs[:groups], refs[groups : 2 * groups], refs[2 * groups :]
        g_up_refs, g_down_refs, refs = refs[:groups], refs[groups : 2 * groups], refs[2 * groups :]
        g_bias_ref, out_ref, back_ref, refs = refs[0], refs[1], refs[2], refs[3:]
        up, down, pre, act, act_half, pre_half, g_up, g_down, sems, out_sems = refs[-10:]
        for g in range(groups):

            def start(r, g=g):
                s = order_ref[r]
                pltpu.make_async_copy(
                    up_refs[g].at[r, :, pl.ds(0, hidden)],
                    up.at[g, pl.ds(pl.multiple_of(s * rows, rows), rows)],
                    sems.at[g],
                ).start()
                pltpu.make_async_copy(
                    down_refs[g].at[r],
                    down.at[g, pl.ds(pl.multiple_of(s * share, share), share)],
                    sems.at[groups + g],
                ).start()

            loop(n, start)
        if more:
            out_ref[...] = more_refs[0][...]
            back_ref[...] = more_refs[1][...]
        else:
            out_ref[...] = jnp.zeros_like(out_ref)
            back_ref[...] = jnp.zeros_like(back_ref)
        for g in range(groups):
            pltpu.make_async_copy(up.at[g], up.at[g], sems.at[g]).wait()
            pltpu.make_async_copy(down.at[g], down.at[g], sems.at[groups + g]).wait()

            def part(t, g=g):
                at = tile(t, step)
                pre[...] = dot(normed_ref[...], up[g, :, at], 1, 0)
                act[...] = dot(cot_ref[...], down[g, at, :], 1, 1)

                def gelu(i):
                    some = tile(i, CHUNK)
                    x = pre[some] + bias_ref[g, :, at]
                    below = 0.5 * (1.0 + lax.erf(x * math.sqrt(0.5)))
                    density = jnp.exp(-0.5 * x * x) * (1.0 / math.sqrt(2.0 * math.pi))
                    act_half[some] = (x * below).astype(half)
                    pre_half[some] = (act[some] * (below + x * density)).astype(half)

                loop(count // CHUNK, gelu)
                h = act_half[...]
                p = pre_half[...]
                out_ref[...] += dot(h, down[g, at, :], 1, 0)
                back_ref[...] += dot(p, up[g, :, at], 1, 1)
                g_down[g, at, :] = dot(h, cot_ref[...], 0, 0).astype(half)
                g_up[g, :, at] = dot(normed_ref[...], p, 0, 0).astype(half)
                g_bias_ref[g, :, at] = jnp.sum(p.astype(full), axis=0, keepdims=True)

            loop(steps, part)

            def send(r, g=g):
                s = order_ref[r]
                pltpu.make_async_copy(
                    g_up.at[g, pl.ds(pl.multiple_of(s * rows, rows), rows)],
                    g_up_refs[g].at[r],
                    out_sems.at[g],
                ).start()
                pltpu.make_async_copy(
                    g_down.at[g, pl.ds(pl.multiple_of(s * share, share), share)],
                    g_down_refs[g].at[r],
                    out_sems.at[groups + g],
                ).start()

            loop(n, send)
        if more:
            after_ref, end_ref, block_ref = more_refs[2], more_refs[3], refs[0]

            def finish(i):
                at = tile(i, CHUNK)
                block_ref[at] = (after_ref[at] + (out_ref[at] + end_ref[...])).astype(half)

            loop(count // CHUNK, finish)
        for g in range(groups):
            pltpu.make_async_copy(g_up_refs[g], g_up_refs[g], out_sems.at[g]).wait()
            pltpu.make_async_copy(g_down_refs[g], g_down_refs[g], out_sems.at[groups + g]).wait()

    outs = (
        [((n, rows, hidden), half)] * groups
        + [((n, share, width), half)] * groups
        + [((groups, 1, hidden), full), ((count, width), full), ((count, width), full)]
        + ([((count, width), half)] if more else [])
    )
    return call(
        kernel,
        "mlp",
        (order, normed, cot, bias, *more, *ups, *downs),
        [SCALARS] + [ON_CHIP] * (3 + len(more)) + [ANYWHERE] * (2 * groups),
        outs,
        [ANYWHERE] * (2 * groups) + [ON_CHIP] * (len(outs) - 2 * groups),
        [
            pltpu.VMEM((groups, width, hidden), half),
            pltpu.VMEM((groups, hidden, width), half),
            pltpu.VMEM((count, step), full),
            pltpu.VMEM((count, step), full),
            pltpu.VMEM((count, step), half),
            pltpu.VMEM((count, step), half),
            pltpu.VMEM((groups, width, hidden), half),
            pltpu.VMEM((groups, hidden, width), half),
            pltpu.SemaphoreType.DMA((2 * groups,)),
            pltpu.SemaphoreType.DMA((2 * groups,)),
        ],
        groups * 12 * count * width * hidden,
        groups * 8 * width * hidden + 20 * count * width,
        groups * 2 * count * hidden,
    )


def attention_out_back(order, grad, after, cot, gain, mixed, ups):
    count, width = after.shape
    n, rows, _ = ups[0].shape
    quarter = mixed[0].shape[1]
    hidden = ups[0].shape[2] - quarter

    def kernel(order_ref, grad_ref, after_ref, cot_ref, gain_ref, *refs):
        mixed_refs, up_refs, refs = refs[:4], refs[4:8], refs[8:]
        after_grad_ref, mixed_grad_refs, g_out_ref, sums_ref = refs[0], refs[1:5], refs[5], refs[6]
        held, branch, terms, sems = refs[7:]
        load_out(order_ref, up_refs, held, sems.at[0], n, rows, hidden, quarter)
        terms[...] = jnp.zeros_like(terms)

        def fold(value):
            return jnp.sum(value.reshape(CHUNK // 8, 8, width), axis=0)

        def back(i):
            at = tile(i, CHUNK)
            incoming = grad_ref[at]
            part, gain_terms = layer_norm_back(after_ref[at], incoming, gain_ref[...])
            own = cot_ref[at].astype(full)
            total = own + part
            after_grad_ref[at] = total
            rounded = total.astype(half)
            branch[at] = rounded
            terms[0] += fold(rounded.astype(full))
            terms[1] += fold(gain_terms)
            terms[2] += fold(incoming)
            terms[3] += fold(own)

        loop(count // CHUNK, back)
        for k in range(4):
            sums_ref[k] = jnp.sum(terms[k], axis=0, keepdims=True)
        pltpu.make_async_copy(held, held, sems.at[0]).wait()
        for j in range(4):
            mixed_grad_refs[j][...] = dot(branch[...], held[j * quarter : (j + 1) * quarter], 1, 1).astype(half)
            g_out_ref[j * quarter : (j + 1) * quarter] = dot(mixed_refs[j][...], branch[...], 0, 0).astype(half)

    return call(
        kernel,
        "attention_out_back",
        (order, grad, after, cot, gain, *mixed, *ups),
        [SCALARS] + [ON_CHIP] * 8 + [ANYWHERE] * 4,
        [((count, width), full)]
        + [((count, quarter), half)] * 4
        + [((width, width), half), ((4, 1, width), full)],
        [ON_CHIP] * 7,
        [
            pltpu.VMEM((width, width), half),
            pltpu.VMEM((count, width), half),
            pltpu.VMEM((4, 8, width), full),
            pltpu.SemaphoreType.DMA((1,)),
        ],
        4 * count * width * width,
        18 * count * width + 4 * width * width,
    )


def attention_back(order, normed, qkvs, mixed_grads, g_out, which, n_img, patches, factor, n):
    groups = len(qkvs)
    count, width = normed.shape
    wide = qkvs[0].shape[1]
    quarter = wide // 3
    padded = count // n_img
    rows = width // n

    def kernel(order_ref, normed_ref, g_out_ref, *refs):
        qkv_refs, mg_refs, refs = refs[:groups], refs[groups : 2 * groups], refs[2 * groups :]
        g_w_refs, proj_refs, sums_ref = refs[:groups], refs[groups : 2 * groups], refs[2 * groups]
        g_w, sems = refs[2 * groups + 1 :]
        q = order_ref[n]
        for g in range(groups):

            def send_out(r, g=g):
                at = head_rows(order_ref[r], q, n, rows, quarter)
                column = pl.multiple_of((q ^ which[g]) * quarter, quarter)
                pltpu.make_async_copy(
                    g_out_ref.at[pl.ds(at, rows), pl.ds(column, quarter)],
                    g_w_refs[g].at[r, :, pl.ds(wide, quarter)],
                    sems.at[g],
                ).start()

            loop(n, send_out)

            def attend(i, g=g):
                at = tile(i // 2, padded)
                lanes = [pl.ds(pl.multiple_of(t * quarter + (i % 2) * 128, 128), 128) for t in range(3)]
                q2 = qkv_refs[g][at, lanes[0]] * factor
                k2 = qkv_refs[g][at, lanes[1]]
                v2 = qkv_refs[g][at, lanes[2]]
                both, probs, first = softmax_pair(q2, k2, patches)
                o2 = mg_refs[g][at, lanes[0]]
                zero = jnp.zeros_like(o2)
                o_both = jnp.concatenate([jnp.where(first, o2, zero), jnp.where(first, zero, o2)])
                g_probs = dot(o_both, v2, 1, 1)
                weighted = jnp.sum(probs * g_probs, axis=-1, keepdims=True)
                g_scores = (probs * (g_probs - weighted)).astype(half)
                g_query = dot(g_scores, k2, 1, 0)
                g_query = jnp.where(first, g_query[:padded], g_query[padded:]) * factor
                proj_refs[g][at, lanes[0]] = g_query.astype(half)
                proj_refs[g][at, lanes[1]] = dot(g_scores, both, 0, 0).astype(half)
                proj_refs[g][at, lanes[2]] = dot(probs.astype(half), o_both, 0, 0).astype(half)

            loop(2 * n_img, attend)

            def weigh(t, g=g):
                at = tile(t, quarter)
                some = proj_refs[g][:, at]
                g_w[g, :, at] = dot(normed_ref[...], some, 0, 0).astype(half)
                sums_ref[g, :, at] = jnp.sum(some.astype(full), axis=0, keepdims=True)

            loop(3, weigh)

            def send(r, g=g):
                at = pl.multiple_of(order_ref[r] * rows, rows)
                pltpu.make_async_copy(
                    g_w.at[g, pl.ds(at, rows)], g_w_refs[g].at[r, :, pl.ds(0, wide)], sems.at[g]
                ).start()

            loop(n, send)
        for g in range(groups):
            pltpu.make_async_copy(g_w_refs[g], g_w_refs[g], sems.at[g]).wait()

    return call(
        kernel,
        "attention_back",
        (order, normed, g_out, *qkvs, *mixed_grads),
        [SCALARS] + [ON_CHIP] * (2 + 2 * groups),
        [((n, rows, wide + quarter), half)] * groups
        + [((count, wide), half)] * groups
        + [((groups, 1, wide), full)],
        [ANYWHERE] * groups + [ON_CHIP] * (groups + 1),
        [pltpu.VMEM((groups, width, wide), half), pltpu.SemaphoreType.DMA((groups,))],
        groups * 2 * count * width * wide * 2,
        2 * (count * width + width * width + groups * (width * wide + count * (2 * wide + quarter))),
    )


def input_back(order, x_zero, after_grad, gain, projs, weights):
    count, width = x_zero.shape
    n, rows, wide = weights[0].shape

    def kernel(order_ref, x_ref, after_ref, gain_ref, *refs):
        proj_refs, w_refs = refs[:4], refs[4:8]
        token_ref, sums_ref, held, terms, sems = refs[8:]
        for j in range(4):

            def start(r, j=j):
                at = pl.multiple_of(order_ref[r] * rows, rows)
                pltpu.make_async_copy(w_refs[j].at[r], held.at[j, pl.ds(at, rows)], sems.at[j]).start()

            loop(n, start)
        for j in range(4):
            pltpu.make_async_copy(held.at[j], held.at[j], sems.at[j]).wait()
            product = dot(proj_refs[j][...], held[j], 1, 1)
            if j == 0:
                token_ref[...] = product
            else:
                token_ref[...] += product
        terms[...] = jnp.zeros_like(terms)

        def fold(value):
            return jnp.sum(value.reshape(CHUNK // 8, 8, width), axis=0)

        def back(i):
            at = tile(i, CHUNK)
            incoming = token_ref[at]
            part, gain_terms = layer_norm_back(x_ref[at], incoming, gain_ref[...])
            token_ref[at] = after_ref[at] + part
            terms[0] += fold(gain_terms)
            terms[1] += fold(incoming)

        loop(count // CHUNK, back)
        for k in range(2):
            sums_ref[k] = jnp.sum(terms[k], axis=0, keepdims=True)

    return call(
        kernel,
        "input_back",
        (order, x_zero, after_grad, gain, *projs, *weights),
        [SCALARS] + [ON_CHIP] * 7 + [ANYWHERE] * 4,
        [((count, width), full), ((2, 1, width), full)],
        [ON_CHIP] * 2,
        [
            pltpu.VMEM((4, width, wide), half),
            pltpu.VMEM((2, 8, width), full),
            pltpu.SemaphoreType.DMA((4,)),
        ],
        8 * count * width * wide,
        12 * count * width + 8 * (width + count) * wide,
    )


def table(codes, width):
    ratio = 0.3 * jnp.exp(codes.astype(full) * (math.log(10.0 / 0.3) / (NSCALE - 1)))
    quarter = width // 4
    omega = jnp.exp(jnp.arange(quarter).astype(full) * (-math.log(10000.0) / quarter))
    steps = jnp.arange(GRID, dtype=jnp.int32).astype(full)
    angle = ratio[:, None, None] * steps[None, :, None] * omega[None, None, :]
    return jnp.concatenate([jnp.sin(angle), jnp.cos(angle)], axis=-1)


def local(
    tokens,
    scale_codes,
    w_qkv,
    b_q,
    b_v,
    w_out,
    b_out,
    gain_one,
    shift_one,
    w_fc1,
    b_fc1,
    w_fc2,
    b_fc2,
    gain_two,
    shift_two,
    cotangent,
):
    n = lax.axis_size("fsdp")
    q = lax.axis_index("dp")
    f = lax.axis_index("fsdp")
    row_count, width = tokens.shape
    rows = width // n
    ff = b_fc1.shape[0] * n
    ffq = ff // n // 4
    hidden = n * ffq
    quarter = width // 4
    n_img = scale_codes.shape[0]
    patches = row_count // n_img
    padded = -(-patches // 16) * 16
    factor = 1.0 / math.sqrt(width // HEADS)
    shard_order = jnp.asarray(masks(n), jnp.int32) ^ f
    group_order = jnp.arange(4, dtype=jnp.int32) ^ q
    order = jnp.concatenate([shard_order, q[None]])

    def pick(value, axis):
        return lax.dynamic_index_in_dim(value, q, axis, keepdims=False)

    small = jnp.concatenate(
        [b_q, b_v, b_out, gain_one, shift_one, b_fc2, gain_two, shift_two, b_fc1]
    ).astype(half)
    pad = -small.shape[0] % 2048
    small_held = gather_shards(jnp.pad(small, (0, pad)).reshape(-1, 128), n).reshape(n, -1)
    inverse = jnp.zeros((n,), jnp.int32).at[shard_order].set(jnp.arange(n, dtype=jnp.int32))
    small_all = jnp.take(small_held, inverse, axis=0).astype(full)
    vectors = [small_all[:, i * rows : (i + 1) * rows].reshape(1, width) for i in range(8)]
    full_bq, full_bv, full_bout, gain_one_f, shift_one_f, full_bfc2, gain_two_f, shift_two_f = vectors
    bias_units = small_all[:, 8 * rows : 8 * rows + 4 * ffq].reshape(n, 4, ffq)
    bias_fc1 = jnp.take(bias_units, group_order, axis=1).transpose(1, 0, 2).reshape(4, 1, hidden)
    bias_q = jnp.take(full_bq.reshape(4, quarter), group_order, axis=0)
    bias_v = jnp.take(full_bv.reshape(4, quarter), group_order, axis=0)
    bias_qkv = jnp.concatenate([bias_q, jnp.zeros_like(bias_q), bias_v], axis=1)[:, None]

    qkv_own = pick(w_qkv.reshape(rows, 3, 4, quarter), 2).reshape(rows, 3 * quarter).astype(half)
    qkv_parts = gather_quarters(qkv_own, n)
    out_own = pick(w_out.reshape(rows, 4, quarter), 1).astype(half)
    fc1_own = pick(w_fc1.reshape(rows, n, 4, ffq), 2).reshape(rows, n * ffq).astype(half)
    up_parts = gather_quarters(jnp.concatenate([fc1_own, out_own], axis=1), n)
    fc2_own = pick(w_fc2.reshape(4, ffq, width), 0).astype(half)
    column = gather_shards(fc2_own, n, 1)
    both = jnp.stack([column, x_swap(column)])
    far = swap(both, "fsdp", n, 0)
    down_own = jnp.concatenate([both[0], far[0]])
    down_across = jnp.concatenate([both[1], far[1]])
    down_parts = (down_own, core_swap(down_own), down_across, core_swap(down_across))

    def spread_rows(value):
        split = value.reshape(n_img, patches, width)
        return jnp.pad(split, ((0, 0), (0, padded - patches), (0, 0)))

    def compact(value):
        return value.reshape(n_img, padded, width)[:, :patches].reshape(row_count, width)

    places = table(scale_codes, width)
    row_place = jnp.broadcast_to(places[:, :, None], (n_img, GRID, GRID, width // 2))
    col_place = jnp.broadcast_to(places[:, None], (n_img, GRID, GRID, width // 2))
    place = jnp.concatenate([row_place, col_place], axis=-1).reshape(n_img, patches, width)
    place = jnp.pad(place, ((0, 0), (0, padded - patches), (0, 0)))
    x_zero = (spread_rows(tokens).astype(full) + place).reshape(-1, width)
    normed_one = layer_norm(x_zero, gain_one_f, shift_one_f).astype(half)
    cot = spread_rows(cotangent).reshape(-1, width)

    first = attention_forward(order, normed_one, bias_qkv[:2], qkv_parts[:2], n_img, patches, factor)
    second = attention_forward(order, normed_one, bias_qkv[2:], qkv_parts[2:], n_img, patches, factor)
    qkvs = (*first[:2], *second[:2])
    mixed = (*first[2:], *second[2:])
    after_attn, normed_two = attention_out(
        order, x_zero, mixed, up_parts, full_bout, gain_two_f, shift_two_f
    )

    g_up0, g_up1, g_down0, g_down1, g_bias_a, out_a, back_a = mlp(
        order, normed_two, cot, bias_fc1[:2], up_parts[:2], down_parts[:2]
    )
    g_up2, g_up3, g_down2, g_down3, g_bias_b, _, grad_two_in, block = mlp(
        order, normed_two, cot, bias_fc1[2:], up_parts[2:], down_parts[2:], (out_a, back_a), (after_attn, full_bfc2)
    )
    block_out = compact(block)
    up_grads = (g_up0, g_up1, g_up2, g_up3)
    down_grads = (g_down0, g_down1, g_down2, g_down3)

    middle = n // 2
    pair_low, pair_high = [], []
    for a, b in ((0, 1), (2, 3)):
        got = core_swap(down_grads[b])
        pair_low.append(add_half(down_grads[a][:middle], got[:middle]))
        pair_high.append(add_half(down_grads[a][middle:], got[middle:]))
    far = swap(jnp.stack(pair_high), "fsdp", n, 0)
    across = x_swap(add_half(pair_low[1], far[1]))
    down_low = (pair_low[0].astype(full) + far[0].astype(full) + across.astype(full)).astype(half)
    for bit in range(1, n.bit_length() - 1):
        size = down_low.shape[0] // 2
        got = swap(down_low[size:], "fsdp", n, bit)
        down_low = add_half(down_low[:size], got)
    down_pieces = spread_quarters(down_low[0], q)
    out_fc2 = jnp.concatenate(down_pieces).astype(full)
    up_pieces = spread_quarters(reduce_quarters(up_grads, n), q)
    out_fc1 = (
        jnp.stack([p.reshape(rows, n, ffq) for p in up_pieces], axis=2).reshape(rows, ff).astype(full)
    )

    after_grad, mg0, mg1, mg2, mg3, g_out, sums_two = attention_out_back(
        order, grad_two_in, after_attn, cot, gain_two_f, mixed, up_parts
    )
    g_w2, g_w3, proj2, proj3, sums_b = attention_back(
        order, normed_one, qkvs[2:], (mg2, mg3), g_out, (2, 3), n_img, patches, factor, n
    )
    g_w0, g_w1, proj0, proj1, sums_a = attention_back(
        order, normed_one, qkvs[:2], (mg0, mg1), g_out, (0, 1), n_img, patches, factor, n
    )
    attn_pieces = spread_quarters(reduce_quarters((g_w0, g_w1, g_w2, g_w3), n), q)
    out_qkv = (
        jnp.stack([p[:, : 3 * quarter].reshape(rows, 3, quarter) for p in attn_pieces], axis=2)
        .reshape(rows, 3 * width)
        .astype(full)
    )
    out_out = jnp.stack([p[:, 3 * quarter :] for p in attn_pieces], axis=1).reshape(rows, width).astype(full)
    tokens_grad, sums_one = input_back(
        order, x_zero, after_grad, gain_one_f, (proj0, proj1, proj2, proj3), qkv_parts
    )
    grad_tokens = compact(tokens_grad)

    sums_proj = jnp.take(jnp.concatenate([sums_a, sums_b])[:, 0], group_order, axis=0)
    sums = [
        sums_proj[:, :quarter],
        sums_proj[:, 2 * quarter :],
        sums_two[0],
        sums_one[0],
        sums_one[1],
        sums_two[3],
        sums_two[1],
        sums_two[2],
    ]
    units = jnp.concatenate([g_bias_a, g_bias_b]).reshape(4, n, ffq)
    units = jnp.take(units, group_order, axis=0).transpose(1, 0, 2)
    packed = jnp.concatenate([s.reshape(n, rows) for s in sums] + [units.reshape(n, 4 * ffq)], axis=1)
    packed = jnp.take(packed, shard_order, axis=0)
    pad = -packed.shape[1] % 1024
    packed = jnp.pad(packed, ((0, 0), (0, pad))).reshape(n, -1, 128)
    packed = packed + core_swap(packed)
    packed = packed + x_swap(packed)
    for bit in range(n.bit_length() - 1):
        size = packed.shape[0] // 2
        packed = packed[:size] + swap(packed[size:], "fsdp", n, bit)
    vector = packed.reshape(-1)
    small_out = [vector[i * rows : (i + 1) * rows] for i in range(8)]
    out_bfc1 = vector[8 * rows : 8 * rows + 4 * ffq]
    o_bq, o_bv, o_bout, o_gone, o_sone, o_bfc2, o_gtwo, o_stwo = small_out
    return (
        block_out,
        grad_tokens,
        out_qkv,
        o_bq,
        o_bv,
        out_out,
        o_bout,
        o_gone,
        o_sone,
        out_fc1,
        out_bfc1,
        out_fc2,
        o_bfc2,
        o_gtwo,
        o_stwo,
    )


def solution(mesh):
    rows_split = P(("dp", "fsdp"), None)
    matrix = P("fsdp", None)
    vector = P("fsdp")
    return jax.shard_map(
        local,
        mesh=mesh,
        in_specs=(
            rows_split, P(("dp", "fsdp")), matrix, vector, vector, matrix, vector, vector, vector,
            matrix, vector, matrix, vector, vector, vector, rows_split,
        ),
        out_specs=(
            rows_split, rows_split, matrix, vector, vector, matrix, vector, vector, vector,
            matrix, vector, matrix, vector, vector, vector,
        ),
        check_vma=False,
    )
```

time: 2240 us -> 678 us (0.30)
  Pallas kernels: 1540 us -> 238 us
  matrix products: 183 us -> 0 us
  local copies, waits for them, and re-layouts: 112 us -> 54.6 us
  other arithmetic: 89.8 us -> 49.1 us
    pallas_call x6 -> x9, Pallas kernels: 1540 us -> 238 us  [call(): pl.pallas_call(kernel, out_shape=[jax.ShapeDtypeStruct(shape, kind) for s...]
    dot_general x18 -> x0, matrix products: 183 us -> none  [the longest x4 66.8 us: matmul(): return jnp.dot(left, right, preferred_element_type=full)]
  transfers between devices with their start and end apart: 50 -> 50, of which waited for: 24 -> 24; matrix products, arithmetic and copies ran while one was open for 7% -> 14% of each run, Pallas kernels for 32% -> 29%
where the time goes in v2:
time: 678 us; the launch traced here: 671 us
  waiting for transfers between devices  284 us (42%)
  Pallas kernels  238 us (35%)
  local copies, waits for them, and re-layouts  54.6 us (8%)
  other arithmetic  49.1 us (7%)
  starting transfers between devices  42.7 us (6%)
    ppermute x50, waiting for transfers between devices, swap(): return lax.ppermute(value, axis, [(i, i ^ 1 << bit) for i in range(size)])  284 us
    pallas_call x9, Pallas kernels, call(): pl.pallas_call(kernel, out_shape=[jax.ShapeDtypeStruct(shape, kind) for s...  238 us
    ppermute x50, starting transfers between devices, swap(): return lax.ppermute(value, axis, [(i, i ^ 1 << bit) for i in range(size)])  42.7 us
    convert_element_type x11, other arithmetic, add_half(): return (a.astype(full) + b.astype(full)).astype(half)  13.7 us
  transfers between devices with their start and end apart: 50, of which 24 were waited for; matrix products, arithmetic and copies ran while one was open for 14% of the time, Pallas kernels for 29%

profile of v2, /device:TPU:0, one launch (start us, length us, event | category | flops | bytes accessed | tf_op | source)
XLA Modules:
  0.0 670.5 jit_solution(5721483157123114733)
XLA Ops:
  0.7 3.8 reshape.288
  4.5 2.2 constant_dynamic-slice_fusion.1
  7.2 4.1 collective-permute-start.9
  13.2 2.6 copy.58
  17.6 2.9 collective-permute-start.3
  22.8 3.6 copy.57
  26.4 2.5 reshape.281
  28.8 7.9 %collective-permute-done.9 = bf16[1,128,1280]{2,1,0:T(8,128)(2,1)S(1)} collective-permute-done((bf16[1,128,1280]{2,1,0:T(8,128)(2,1)S(1)}, bf16[1,128,1280]{2,1,0:T(8,128)(2,1)S(1)}, u32[]{:S(2)}, u32[]{:S(2)}) %collective-permute-start.9) | collective-permute-done | bytes 327712 | tf_op jit(solution)/shard_map/ppermute | solution.py:19
  37.8 22.1 %collective-permute-done.10 = bf16[2,128,1280]{2,1,0:T(8,128)(2,1)S(1)} collective-permute-done((bf16[2,128,1280]{2,1,0:T(8,128)(2,1)S(1)}, bf16[2,128,1280]{2,1,0:T(8,128)(2,1)S(1)}, u32[]{:S(2)}, u32[]{:S(2)}) %collective-permute-start.10) | collective-permute-done | bytes 655392 | tf_op jit(solution)/shard_map/ppermute | solution.py:19
  62.4 2.8 fusion.13
  65.8 10.2 %collective-permute-done.16 = bf16[2,128,1024]{2,1,0:T(8,128)(2,1)S(1)} collective-permute-done((bf16[2,128,1024]{2,1,0:T(8,128)(2,1)S(1)}, bf16[2,128,1024]{2,1,0:T(8,128)(2,1)S(1)}, u32[]{:S(2)}, u32[]{:S(2)}) %collective-permute-start.16) | collective-permute-done | bytes 524320 | tf_op jit(solution)/shard_map/ppermute | solution.py:19
  77.7 13.1 %collective-permute-done.11 = bf16[4,128,1280]{2,1,0:T(8,128)(2,1)S(1)} collective-permute-done((bf16[4,128,1280]{2,1,0:T(8,128)(2,1)S(1)}, bf16[4,128,1280]{2,1,0:T(8,128)(2,1)S(1)}, u32[]{:S(2)}, u32[]{:S(2)}) %collective-permute-start.11) | collective-permute-done | bytes 1310752 | tf_op jit(solution)/shard_map/ppermute | solution.py:19
  95.2 7.1 %collective-permute-done.17 = bf16[4,128,1024]{2,1,0:T(8,128)(2,1)S(1)} collective-permute-done((bf16[4,128,1024]{2,1,0:T(8,128)(2,1)S(1)}, bf16[4,128,1024]{2,1,0:T(8,128)(2,1)S(1)}, u32[]{:S(2)}, u32[]{:S(2)}) %collective-permute-start.17) | collective-permute-done | bytes 1048608 | tf_op jit(solution)/shard_map/ppermute | solution.py:19
  105.8 2.0 pad_maximum_fusion.9
  109.7 3.4 collective-permute-done.1
  114.3 2.5 reshape.290
  116.8 2.8 pad.22
  119.6 45.0 %collective-permute-done.2 = bf16[4,16,128]{2,1,0:T(8,128)(2,1)S(1)} collective-permute-done((bf16[4,16,128]{2,1,0:T(8,128)(2,1)S(1)}, bf16[4,16,128]{2,1,0:T(8,128)(2,1)S(1)}, u32[]{:S(2)}, u32[]{:S(2)}) %collective-permute-start.2) | collective-permute-done | bytes 16416 | tf_op jit(solution)/shard_map/ppermute | solution.py:19
  165.3 2.6 pad_maximum_fusion.6.refs_0_.refs_4_
  172.0 2.7 slice_bitcast_fusion.2
  176.6 22.8 %collective-permute-done.7.refs_0_.refs_6_ = bf16[8,128,768]{2,1,0:T(8,128)(2,1)} collective-permute-done((bf16[8,128,768]{2,1,0:T(8,128)(2,1)}, bf16[8,128,768]{2,1,0:T(8,128)(2,1)}, u32[]{:S(2)}, u32[]{:S(2)}) %collective-permute-start.7) | collective-permute-done | bytes 1572896 | tf_op jit(solution)/shard_map/ppermute | solution.py:19
  203.7 18.2 %attention_forward.2 = (bf16[832,768]{1,0:T(8,128)(2,1)}, bf16[832,768]{1,0:T(8,128)(2,1)}, bf16[832,256]{1,0:T(8,128)(2,1)}, bf16[832,256]{1,0:T(8,128)(2,1)}) custom-call(s32[9]{0:T(128)} %pad_add_fusion.1.order_ref, bf16[832,1024]{1,0:T(8,128)(2,1)} %add_convert_fusion.2.normed_ref, f32[2,1,768]{2,1,0:T(1,128)} %copy.63.bias_ref, ...), custom_call_target="tpu_custom_call" | custom-call | flops 2617245696 | bytes 8257536 | tf_op jit(solution)/shard_map/attention_forward/pallas_call | solution.py:100
  222.7 18.2 %attention_forward.3 = (bf16[832,768]{1,0:T(8,128)(2,1)}, bf16[832,768]{1,0:T(8,128)(2,1)}, bf16[832,256]{1,0:T(8,128)(2,1)}, bf16[832,256]{1,0:T(8,128)(2,1)}) custom-call(s32[9]{0:T(128)} %pad_add_fusion.1.order_ref, bf16[832,1024]{1,0:T(8,128)(2,1)} %add_convert_fusion.2.normed_ref, f32[2,1,768]{2,1,0:T(1,128)} %slice.337.bias_ref, ...), custom_call_target="tpu_custom_call" | custom-call | flops 2617245696 | bytes 8257536 | tf_op jit(solution)/shard_map/attention_forward/pallas_call | solution.py:100
  240.9 18.1 %attention_out.1 = (f32[832,1024]{1,0:T(8,128)}, bf16[832,1024]{1,0:T(8,128)(2,1)}) custom-call(s32[9]{0:T(128)} %pad_add_fusion.1.order_ref, f32[832,1024]{1,0:T(8,128)} %bitcast.188, f32[1,1024]{1,0:T(1,128)} %bitcast.230, f32[1,1024]{1,0:T(1,128)} %bitcast.223, f32[1,1024]{1,0:T(1,128)} %bitcast.229, bf16[832,256]{1,0:T(8,128)(2,1)} %get-tuple-element.59.refs_0_, ...), custom_call_target="tpu_custom_call" | custom-call | flops 1744830464 | bytes 14024704 | tf_op jit(solution)/shard_map/attention_out/pallas_call | solution.py:100
  259.0 38.4 %mlp.2 = (bf16[8,128,1024]{2,1,0:T(8,128)(2,1)}, bf16[8,128,1024]{2,1,0:T(8,128)(2,1)}, bf16[8,128,1024]{2,1,0:T(8,128)(2,1)}, bf16[8,128,1024]{2,1,0:T(8,128)(2...) custom-call(s32[9]{0:T(128)} %pad_add_fusion.1.order_ref, ...), custom_call_target="tpu_custom_call" | custom-call | flops 20937965568 | bytes 33816576 | tf_op jit(solution)/shard_map/mlp/pallas_call | solution.py:100
  298.7 42.2 %mlp.3 = (bf16[8,128,1024]{2,1,0:T(8,128)(2,1)}, bf16[8,128,1024]{2,1,0:T(8,128)(2,1)}, bf16[8,128,1024]{2,1,0:T(8,128)(2,1)}, bf16[8,128,1024]{2,1,0:T(8,128)(2...) custom-call(s32[9]{0:T(128)} %pad_add_fusion.1.order_ref, ...), custom_call_target="tpu_custom_call" | custom-call | flops 20937965568 | bytes 33816576 | tf_op jit(solution)/shard_map/mlp/pallas_call | solution.py:100
  342.1 24.6 %attention_out_back.1 = (f32[832,1024]{1,0:T(8,128)}, bf16[832,256]{1,0:T(8,128)(2,1)}, bf16[832,256]{1,0:T(8,128)(2,1)}, bf16[832,256]{1,0:T(8,128)(2,1)}, bf16...) custom-call(s32[9]{0:T(128)} %pad_add_fusion.1.order_ref, ...), custom_call_target="tpu_custom_call" | custom-call | flops 3489660928 | bytes 19529728 | tf_op jit(solution)/shard_map/attention_out_back/pallas_call | solution.py:100
  366.7 24.9 %attention_back.3 = (bf16[8,128,1024]{2,1,0:T(8,128)(2,1)}, bf16[8,128,1024]{2,1,0:T(8,128)(2,1)}, bf16[832,768]{1,0:T(8,128)(2,1)}, bf16[832,768]{1,0:T(8,128)(2,1)}, f32[2,1,768]{2,1,0:T(1,128)}) custom-call(s32[9]{0:T(128)} %pad_add_fusion.1.order_ref, bf16[832,1024]{1,0:T(8,128)(2,1)} %add_convert_fusion.2.normed_ref, ...), custom_call_target="tpu_custom_call" | custom-call | flops 5234491392 | bytes 12910592 | tf_op jit(solution)/shard_map/attention_back/pallas_call | solution.py:100
  391.7 24.9 %attention_back.2 = (bf16[8,128,1024]{2,1,0:T(8,128)(2,1)}, bf16[8,128,1024]{2,1,0:T(8,128)(2,1)}, bf16[832,768]{1,0:T(8,128)(2,1)}, bf16[832,768]{1,0:T(8,128)(2,1)}, f32[2,1,768]{2,1,0:T(1,128)}) custom-call(s32[9]{0:T(128)} %pad_add_fusion.1.order_ref, bf16[832,1024]{1,0:T(8,128)(2,1)} %add_convert_fusion.2.normed_ref, ...), custom_call_target="tpu_custom_call" | custom-call | flops 5234491392 | bytes 12910592 | tf_op jit(solution)/shard_map/attention_back/pallas_call | solution.py:100
  418.0 28.2 %input_back.1 = (f32[832,1024]{1,0:T(8,128)}, f32[2,1,1024]{2,1,0:T(1,128)}) custom-call(s32[9]{0:T(128)} %pad_add_fusion.1.order_ref, f32[832,1024]{1,0:T(8,128)} %bitcast.189, f32[832,1024]{1,0:T(8,128)} %get-tuple-element.69.after_ref, f32[1,1024]{1,0:T(1,128)} %bitcast.240, bf16[832,768]{1,0:T(8,128)(2,1)} %get-tuple-element.75.refs_0_, ...), custom_call_target="tpu_custom_call" | custom-call | flops 5234491392 | bytes 21626880 | tf_op jit(solution)/shard_map/input_back/pallas_call | solution.py:100
  450.4 3.4 add_convert_fusion
  455.3 2.7 add_convert_fusion.1
  464.7 41.9 %collective-permute-done.36 = bf16[8,128,1024]{2,1,0:T(8,128)(2,1)S(1)} collective-permute-done((bf16[8,128,1024]{2,1,0:T(8,128)(2,1)S(1)}, bf16[8,128,1024]{2,1,0:T(8,128)(2,1)S(1)}, u32[]{:S(2)}, u32[]{:S(2)}) %collective-permute-start.36) | collective-permute-done | bytes 2097184 | tf_op jit(solution)/shard_map/ppermute | solution.py:19
  506.6 2.9 add_convert_fusion.8
  510.0 40.7 %collective-permute-done.23 = bf16[8,128,1024]{2,1,0:T(8,128)(2,1)S(1)} collective-permute-done((bf16[8,128,1024]{2,1,0:T(8,128)(2,1)S(1)}, bf16[8,128,1024]{2,1,0:T(8,128)(2,1)S(1)}, u32[]{:S(2)}, u32[]{:S(2)}) %collective-permute-start.23) | collective-permute-done | bytes 2097184 | tf_op jit(solution)/shard_map/ppermute | solution.py:19
  550.7 2.9 add_convert_fusion.10
  554.1 3.6 fusion
  559.8 2.2 collective-permute-done.32
  562.0 3.7 collective-permute-start.33
  565.6 2.2 slice.466
  575.1 3.0 collective-permute-done.24
  582.0 2.5 fusion.2
  586.1 6.2 collective-permute-done.38
  593.1 16.2 %collective-permute-done.25 = bf16[2,128,1024]{2,1,0:T(8,128)(2,1)S(1)} collective-permute-done((bf16[2,128,1024]{2,1,0:T(8,128)(2,1)S(1)}, bf16[2,128,1024]{2,1,0:T(8,128)(2,1)S(1)}, u32[]{:S(2)}, u32[]{:S(2)}) %collective-permute-start.25) | collective-permute-done | bytes 524320 | tf_op jit(solution)/shard_map/ppermute | solution.py:19
  609.4 5.7 collective-permute-done.39
  619.0 11.0 %collective-permute-done.26 = bf16[1,128,1024]{2,1,0:T(8,128)(2,1)S(1)} collective-permute-done((bf16[1,128,1024]{2,1,0:T(8,128)(2,1)S(1)}, bf16[1,128,1024]{2,1,0:T(8,128)(2,1)S(1)}, u32[]{:S(2)}, u32[]{:S(2)}) %collective-permute-start.26) | collective-permute-done | bytes 262176 | tf_op jit(solution)/shard_map/ppermute | solution.py:19
  637.6 7.4 %collective-permute-done.41 = bf16[2,128,1024]{2,1,0:T(8,128)(2,1)S(1)} collective-permute-done((bf16[2,128,1024]{2,1,0:T(8,128)(2,1)S(1)}, bf16[2,128,1024]{2,1,0:T(8,128)(2,1)S(1)}, u32[]{:S(2)}, u32[]{:S(2)}) %collective-permute-start.41) | collective-permute-done | bytes 524320 | tf_op jit(solution)/shard_map/ppermute | solution.py:19
  645.4 10.9 %collective-permute-done.28 = bf16[2,128,1024]{2,1,0:T(8,128)(2,1)S(1)} collective-permute-done((bf16[2,128,1024]{2,1,0:T(8,128)(2,1)S(1)}, bf16[2,128,1024]{2,1,0:T(8,128)(2,1)S(1)}, u32[]{:S(2)}, u32[]{:S(2)}) %collective-permute-start.28) | collective-permute-done | bytes 524320 | tf_op jit(solution)/shard_map/ppermute | solution.py:19
  (351 shorter events, 93.0 us)
Async XLA Ops:
  7.2 29.6 %collective-permute-start.9 = (bf16[1,128,1280]{2,1,0:T(8,128)(2,1)S(1)}, bf16[1,128,1280]{2,1,0:T(8,128)(2,1)S(1)}, u32[]{:S(2)}, u32[]{:S(2)}) collective-permute-start(bf16[1,128,1280]{2,1,0:T(8,128)(2,1)S(1)} %maximum_bitcast_fusion), channel_id=1, source_target_pairs={{0,4},{1,5},{2,6},{3,7},{4,0},{5,1},{6,2},{7,3},{8,12},{9,13},{10,... | collective-permute-start | bytes 983048 | tf_op jit(solution)/shard_map/ppermute | solution.py:19
  13.1 96.2 %collective-permute-start = (bf16[1,16,128]{2,1,0:T(8,128)(2,1)S(1)}, bf16[1,16,128]{2,1,0:T(8,128)(2,1)S(1)}, u32[]{:S(2)}, u32[]{:S(2)}) collective-permute-start(bf16[1,16,128]{2,1,0:T(8,128)(2,1)S(1)} %get-tuple-element.192), channel_id=1, source_target_pairs={{0,4},{1,5},{2,6},{3,7},{4,0},{5,1},{6,2},{7,3},{8,12},{9,13},{10,... | collective-permute-start | bytes 12296 | tf_op jit(solution)/shard_map/ppermute | solution.py:19
  17.6 76.4 %collective-permute-start.3 = (bf16[1,128,768]{2,1,0:T(8,128)(2,1)}, bf16[1,128,768]{2,1,0:T(8,128)(2,1)}, u32[]{:S(2)}, u32[]{:S(2)}) collective-permute-start(bf16[1,128,768]{2,1,0:T(8,128)(2,1)} %copy.62), channel_id=1, source_target_pairs={{0,4},{1,5},{2,6},{3,7},{4,0},{5,1},{6,2},{7,3},{8,12},{9,13},{10,... | collective-permute-start | bytes 589832 | tf_op jit(solution)/shard_map/ppermute | solution.py:19
  20.5 41.1 %collective-permute-start.15 = (bf16[1,128,1024]{2,1,0:T(8,128)(2,1)S(1)}, bf16[1,128,1024]{2,1,0:T(8,128)(2,1)S(1)}, u32[]{:S(2)}, u32[]{:S(2)}) collective-permute-start(bf16[1,128,1024]{2,1,0:T(8,128)(2,1)S(1)} %dynamic-slice_convert_fusion), channel_id=1, source_target_pairs={{0,4},{1,5},{2,6},{3,7},{4,0},{5,1},{6,2},{7,3},{8,12},{9,13},{10,... | collective-permute-start | bytes 786440 | tf_op jit(solution)/shard_map/ppermute | solution.py:19
  36.8 23.1 %collective-permute-start.10 = (bf16[2,128,1280]{2,1,0:T(8,128)(2,1)S(1)}, bf16[2,128,1280]{2,1,0:T(8,128)(2,1)S(1)}, u32[]{:S(2)}, u32[]{:S(2)}) collective-permute-start(bf16[2,128,1280]{2,1,0:T(8,128)(2,1)S(1)} %pad_maximum_fusion.10), channel_id=1, source_target_pairs={{0,2},{1,3},{2,0},{3,1},{4,6},{5,7},{6,4},{7,5},{8,10},{9,11},{10,... | collective-permute-start | bytes 1966088 | tf_op jit(solution)/shard_map/ppermute | solution.py:19
  60.0 30.8 %collective-permute-start.11 = (bf16[4,128,1280]{2,1,0:T(8,128)(2,1)S(1)}, bf16[4,128,1280]{2,1,0:T(8,128)(2,1)S(1)}, u32[]{:S(2)}, u32[]{:S(2)}) collective-permute-start(bf16[4,128,1280]{2,1,0:T(8,128)(2,1)S(1)} %pad_maximum_fusion.7), channel_id=1, source_target_pairs={{0,1},{1,0},{2,3},{3,2},{4,5},{5,4},{6,7},{7,6},{8,9},{9,8},{10,11... | collective-permute-start | bytes 3932168 | tf_op jit(solution)/shard_map/ppermute | solution.py:19
  62.4 13.6 %collective-permute-start.16 = (bf16[2,128,1024]{2,1,0:T(8,128)(2,1)S(1)}, bf16[2,128,1024]{2,1,0:T(8,128)(2,1)S(1)}, u32[]{:S(2)}, u32[]{:S(2)}) collective-permute-start(bf16[2,128,1024]{2,1,0:T(8,128)(2,1)S(1)} %pad_maximum_fusion.11), channel_id=1, source_target_pairs={{0,2},{1,3},{2,0},{3,1},{4,6},{5,7},{6,4},{7,5},{8,10},{9,11},{10,... | collective-permute-start | bytes 1572872 | tf_op jit(solution)/shard_map/ppermute | solution.py:19
  76.1 26.2 %collective-permute-start.17 = (bf16[4,128,1024]{2,1,0:T(8,128)(2,1)S(1)}, bf16[4,128,1024]{2,1,0:T(8,128)(2,1)S(1)}, u32[]{:S(2)}, u32[]{:S(2)}) collective-permute-start(bf16[4,128,1024]{2,1,0:T(8,128)(2,1)S(1)} %get-tuple-element.159), channel_id=1, source_target_pairs={{0,16},{8,24},{16,0},{24,8},{1,17},{9,25},{17,1},{25,9},{2,18},{10... | collective-permute-start | bytes 3145736 | tf_op jit(solution)/shard_map/ppermute | solution.py:19
  92.5 79.4 %collective-permute-start.13 = (bf16[8,128,1280]{2,1,0:T(8,128)(2,1)}, bf16[8,128,1280]{2,1,0:T(8,128)(2,1)}, u32[]{:S(2)}, u32[]{:S(2)}) collective-permute-start(bf16[8,128,1280]{2,1,0:T(8,128)(2,1)} %pad_maximum_fusion.1.refs_4_.refs_0_), channel_id=1, source_target_pairs={{0,16},{8,24},{16,0},{24,8},{1,17},{9,25},{17,1},{25,9},{2,18},{10... | collective-permute-start | bytes 7864328 | tf_op jit(solution)/shard_map/ppermute | solution.py:19
  95.1 10.0 %collective-permute-start.4 = (bf16[2,128,768]{2,1,0:T(8,128)(2,1)S(1)}, bf16[2,128,768]{2,1,0:T(8,128)(2,1)S(1)}, u32[]{:S(2)}, u32[]{:S(2)}) collective-permute-start(bf16[2,128,768]{2,1,0:T(8,128)(2,1)S(1)} %pad_maximum_fusion.15), channel_id=1, source_target_pairs={{0,2},{1,3},{2,0},{3,1},{4,6},{5,7},{6,4},{7,5},{8,10},{9,11},{10,... | collective-permute-start | bytes 1179656 | tf_op jit(solution)/shard_map/ppermute | solution.py:19
  103.9 68.0 %collective-permute-start.18 = (bf16[2,4,128,1024]{3,2,1,0:T(8,128)(2,1)}, bf16[2,4,128,1024]{3,2,1,0:T(8,128)(2,1)}, u32[]{:S(2)}, u32[]{:S(2)}) collective-permute-start(bf16[2,4,128,1024]{3,2,1,0:T(8,128)(2,1)} %pad_maximum_fusion.2), channel_id=1, source_target_pairs={{0,1},{1,0},{2,3},{3,2},{4,5},{5,4},{6,7},{7,6},{8,9},{9,8},{10,11... | collective-permute-start | bytes 6291464 | tf_op jit(solution)/shard_map/ppermute | solution.py:19
  107.8 57.5 %collective-permute-start.5 = (bf16[4,128,768]{2,1,0:T(8,128)(2,1)}, bf16[4,128,768]{2,1,0:T(8,128)(2,1)}, u32[]{:S(2)}, u32[]{:S(2)}) collective-permute-start(bf16[4,128,768]{2,1,0:T(8,128)(2,1)} %pad_maximum_fusion.9), channel_id=1, source_target_pairs={{0,1},{1,0},{2,3},{3,2},{4,5},{5,4},{6,7},{7,6},{8,9},{9,8},{10,11... | collective-permute-start | bytes 2359304 | tf_op jit(solution)/shard_map/ppermute | solution.py:19
  109.3 3.7 collective-permute-start.1
  113.0 51.6 %collective-permute-start.2 = (bf16[4,16,128]{2,1,0:T(8,128)(2,1)S(1)}, bf16[4,16,128]{2,1,0:T(8,128)(2,1)S(1)}, u32[]{:S(2)}, u32[]{:S(2)}) collective-permute-start(bf16[4,16,128]{2,1,0:T(8,128)(2,1)S(1)} %pad_maximum_fusion.18), channel_id=1, source_target_pairs={{0,1},{1,0},{2,3},{3,2},{4,5},{5,4},{6,7},{7,6},{8,9},{9,8},{10,11... | collective-permute-start | bytes 49160 | tf_op jit(solution)/shard_map/ppermute | solution.py:19
  167.9 31.5 %collective-permute-start.7 = (bf16[8,128,768]{2,1,0:T(8,128)(2,1)}, bf16[8,128,768]{2,1,0:T(8,128)(2,1)}, u32[]{:S(2)}, u32[]{:S(2)}) collective-permute-start(bf16[8,128,768]{2,1,0:T(8,128)(2,1)} %pad_maximum_fusion.6.refs_0_.refs_4_), channel_id=1, source_target_pairs={{0,16},{8,24},{16,0},{24,8},{1,17},{9,25},{17,1},{25,9},{2,18},{10... | collective-permute-start | bytes 4718600 | tf_op jit(solution)/shard_map/ppermute | solution.py:19
  171.3 32.4 %collective-permute-start.6 = (bf16[8,128,768]{2,1,0:T(8,128)(2,1)}, bf16[8,128,768]{2,1,0:T(8,128)(2,1)}, u32[]{:S(2)}, u32[]{:S(2)}) collective-permute-start(bf16[8,128,768]{2,1,0:T(8,128)(2,1)} %pad_maximum_fusion.6.refs_0_.refs_4_), channel_id=1, source_target_pairs={{0,8},{8,0},{16,24},{24,16},{1,9},{9,1},{17,25},{25,17},{2,10},{10... | collective-permute-start | bytes 4718600 | tf_op jit(solution)/shard_map/ppermute | solution.py:19
  171.4 69.5 %collective-permute-start.12 = (bf16[8,128,1280]{2,1,0:T(8,128)(2,1)}, bf16[8,128,1280]{2,1,0:T(8,128)(2,1)}, u32[]{:S(2)}, u32[]{:S(2)}) collective-permute-start(bf16[8,128,1280]{2,1,0:T(8,128)(2,1)} %pad_maximum_fusion.1.refs_4_.refs_0_), channel_id=1, source_target_pairs={{0,8},{8,0},{16,24},{24,16},{1,9},{9,1},{17,25},{25,17},{2,10},{10... | collective-permute-start | bytes 7864328 | tf_op jit(solution)/shard_map/ppermute | solution.py:19
  171.9 69.0 %collective-permute-start.14 = (bf16[8,128,1280]{2,1,0:T(8,128)(2,1)}, bf16[8,128,1280]{2,1,0:T(8,128)(2,1)}, u32[]{:S(2)}, u32[]{:S(2)}) collective-permute-start(bf16[8,128,1280]{2,1,0:T(8,128)(2,1)} %collective-permute-done.13.refs_6_.refs_4_), channel_id=1, source_target_pairs={{0,8},{8,0},{16,24},{24,16},{1,9},{9,1},{17,25},{25,17},{2,10},{10... | collective-permute-start | bytes 7864328 | tf_op jit(solution)/shard_map/ppermute | solution.py:19
  176.2 82.8 %collective-permute-start.19 = (bf16[8,128,1024]{2,1,0:T(8,128)(2,1)}, bf16[8,128,1024]{2,1,0:T(8,128)(2,1)}, u32[]{:S(2)}, u32[]{:S(2)}) collective-permute-start(bf16[8,128,1024]{2,1,0:T(8,128)(2,1)} %pad_maximum_fusion.3.refs_2_), channel_id=1, source_target_pairs={{0,8},{8,0},{16,24},{24,16},{1,9},{9,1},{17,25},{25,17},{2,10},{10... | collective-permute-start | bytes 6291464 | tf_op jit(solution)/shard_map/ppermute | solution.py:19
  199.4 23.2 %collective-permute-start.8 = (bf16[8,128,768]{2,1,0:T(8,128)(2,1)}, bf16[8,128,768]{2,1,0:T(8,128)(2,1)}, u32[]{:S(2)}, u32[]{:S(2)}) collective-permute-start(bf16[8,128,768]{2,1,0:T(8,128)(2,1)} %collective-permute-done.7.refs_0_.refs_6_), channel_id=1, source_target_pairs={{0,8},{8,0},{16,24},{24,16},{1,9},{9,1},{17,25},{25,17},{2,10},{10... | collective-permute-start | bytes 4718600 | tf_op jit(solution)/shard_map/ppermute | solution.py:19
  222.1 75.3 %collective-permute-start.20 = (bf16[8,128,1024]{2,1,0:T(8,128)(2,1)S(1)}, bf16[8,128,1024]{2,1,0:T(8,128)(2,1)S(1)}, u32[]{:S(2)}, u32[]{:S(2)}) collective-permute-start(bf16[8,128,1024]{2,1,0:T(8,128)(2,1)S(1)} %pad_maximum_fusion.4.refs_6_), channel_id=1, source_target_pairs={{0,8},{8,0},{16,24},{24,16},{1,9},{9,1},{17,25},{25,17},{2,10},{10... | collective-permute-start | bytes 6291464 | tf_op jit(solution)/shard_map/ppermute | solution.py:19
  341.0 117.1 %collective-permute-start.43 = (bf16[8,128,1024]{2,1,0:T(8,128)(2,1)}, bf16[8,128,1024]{2,1,0:T(8,128)(2,1)}, u32[]{:S(2)}, u32[]{:S(2)}) collective-permute-start(bf16[8,128,1024]{2,1,0:T(8,128)(2,1)} %get-tuple-element.101), channel_id=1, source_target_pairs={{0,8},{8,0},{16,24},{24,16},{1,9},{9,1},{17,25},{25,17},{2,10},{10... | collective-permute-start | bytes 6291464 | tf_op jit(solution)/shard_map/ppermute | solution.py:19
  341.6 118.8 %collective-permute-start.42 = (bf16[8,128,1024]{2,1,0:T(8,128)(2,1)}, bf16[8,128,1024]{2,1,0:T(8,128)(2,1)S(1)}, u32[]{:S(2)}, u32[]{:S(2)}) collective-permute-start(bf16[8,128,1024]{2,1,0:T(8,128)(2,1)} %get-tuple-element.99), channel_id=1, source_target_pairs={{0,8},{8,0},{16,24},{24,16},{1,9},{9,1},{17,25},{25,17},{2,10},{10... | collective-permute-start | bytes 6291464 | tf_op jit(solution)/shard_map/ppermute | solution.py:19
  341.7 108.5 %collective-permute-start.35 = (bf16[8,128,1024]{2,1,0:T(8,128)(2,1)}, bf16[8,128,1024]{2,1,0:T(8,128)(2,1)}, u32[]{:S(2)}, u32[]{:S(2)}) collective-permute-start(bf16[8,128,1024]{2,1,0:T(8,128)(2,1)} %get-tuple-element.97), channel_id=1, source_target_pairs={{0,8},{8,0},{16,24},{24,16},{1,9},{9,1},{17,25},{25,17},{2,10},{10... | collective-permute-start | bytes 6291464 | tf_op jit(solution)/shard_map/ppermute | solution.py:19
  391.6 62.2 %collective-permute-start.22 = (bf16[8,128,1024]{2,1,0:T(8,128)(2,1)}, bf16[8,128,1024]{2,1,0:T(8,128)(2,1)}, u32[]{:S(2)}, u32[]{:S(2)}) collective-permute-start(bf16[8,128,1024]{2,1,0:T(8,128)(2,1)} %get-tuple-element.87), channel_id=1, source_target_pairs={{0,8},{8,0},{16,24},{24,16},{1,9},{9,1},{17,25},{25,17},{2,10},{10... | collective-permute-start | bytes 6291464 | tf_op jit(solution)/shard_map/ppermute | solution.py:19
  449.8 13.4 %collective-permute-start.34 = (bf16[8,128,1024]{2,1,0:T(8,128)(2,1)}, bf16[8,128,1024]{2,1,0:T(8,128)(2,1)S(1)}, u32[]{:S(2)}, u32[]{:S(2)}) collective-permute-start(bf16[8,128,1024]{2,1,0:T(8,128)(2,1)} %get-tuple-element.95), channel_id=1, source_target_pairs={{0,8},{8,0},{16,24},{24,16},{1,9},{9,1},{17,25},{25,17},{2,10},{10... | collective-permute-start | bytes 6291464 | tf_op jit(solution)/shard_map/ppermute | solution.py:19
  450.1 59.9 %collective-permute-start.21 = (bf16[8,128,1024]{2,1,0:T(8,128)(2,1)}, bf16[8,128,1024]{2,1,0:T(8,128)(2,1)S(1)}, u32[]{:S(2)}, u32[]{:S(2)}) collective-permute-start(bf16[8,128,1024]{2,1,0:T(8,128)(2,1)} %get-tuple-element.85), channel_id=1, source_target_pairs={{0,8},{8,0},{16,24},{24,16},{1,9},{9,1},{17,25},{25,17},{2,10},{10... | collective-permute-start | bytes 6291464 | tf_op jit(solution)/shard_map/ppermute | solution.py:19
  453.8 8.7 %collective-permute-start.30 = (f32[8,16,128]{2,1,0:T(8,128)S(1)}, f32[8,16,128]{2,1,0:T(8,128)S(1)}, u32[]{:S(2)}, u32[]{:S(2)}) collective-permute-start(f32[8,16,128]{2,1,0:T(8,128)S(1)} %copy_add_fusion), channel_id=1, source_target_pairs={{0,16},{8,24},{16,0},{24,8},{1,17},{9,25},{17,1},{25,9},{2,18},{10... | collective-permute-start | bytes 196616 | tf_op jit(solution)/shard_map/ppermute | solution.py:19
  458.1 48.5 %collective-permute-start.36 = (bf16[8,128,1024]{2,1,0:T(8,128)(2,1)S(1)}, bf16[8,128,1024]{2,1,0:T(8,128)(2,1)S(1)}, u32[]{:S(2)}, u32[]{:S(2)}) collective-permute-start(bf16[8,128,1024]{2,1,0:T(8,128)(2,1)S(1)} %add_convert_fusion), channel_id=1, source_target_pairs={{0,16},{8,24},{16,0},{24,8},{1,17},{9,25},{17,1},{25,9},{2,18},{10... | collective-permute-start | bytes 6291464 | tf_op jit(solution)/shard_map/ppermute | solution.py:19
  460.3 90.3 %collective-permute-start.23 = (bf16[8,128,1024]{2,1,0:T(8,128)(2,1)S(1)}, bf16[8,128,1024]{2,1,0:T(8,128)(2,1)S(1)}, u32[]{:S(2)}, u32[]{:S(2)}) collective-permute-start(bf16[8,128,1024]{2,1,0:T(8,128)(2,1)S(1)} %add_convert_fusion.1), channel_id=1, source_target_pairs={{0,16},{8,24},{16,0},{24,8},{1,17},{9,25},{17,1},{25,9},{2,18},{10... | collective-permute-start | bytes 6291464 | tf_op jit(solution)/shard_map/ppermute | solution.py:19
  462.5 91.6 %collective-permute-start.44 = (bf16[2,4,128,1024]{3,2,1,0:T(8,128)(2,1)S(1)}, bf16[2,4,128,1024]{3,2,1,0:T(8,128)(2,1)S(1)}, u32[]{:S(2)}, u32[]{:S(2)}) collective-permute-start(bf16[2,4,128,1024]{3,2,1,0:T(8,128)(2,1)S(1)} %pad_maximum_fusion.5), channel_id=1, source_target_pairs={{0,1},{1,0},{2,3},{3,2},{4,5},{5,4},{6,7},{7,6},{8,9},{9,8},{10,11... | collective-permute-start | bytes 6291464 | tf_op jit(solution)/shard_map/ppermute | solution.py:19
  463.1 95.0 %collective-permute-start.31 = (f32[4,16,128]{2,1,0:T(8,128)S(1)}, f32[4,16,128]{2,1,0:T(8,128)S(1)}, u32[]{:S(2)}, u32[]{:S(2)}) collective-permute-start(f32[4,16,128]{2,1,0:T(8,128)S(1)} %slice.488), channel_id=1, source_target_pairs={{0,1},{1,0},{2,3},{3,2},{4,5},{5,4},{6,7},{7,6},{8,9},{9,8},{10,11... | collective-permute-start | bytes 98312 | tf_op jit(solution)/shard_map/ppermute | solution.py:19
  509.5 63.3 %collective-permute-start.37 = (bf16[4,128,1024]{2,1,0:T(8,128)(2,1)}, bf16[4,128,1024]{2,1,0:T(8,128)(2,1)}, u32[]{:S(2)}, u32[]{:S(2)}) collective-permute-start(bf16[4,128,1024]{2,1,0:T(8,128)(2,1)} %get-tuple-element.137), channel_id=1, source_target_pairs={{0,1},{1,0},{2,3},{3,2},{4,5},{5,4},{6,7},{7,6},{8,9},{9,8},{10,11... | collective-permute-start | bytes 3145736 | tf_op jit(solution)/shard_map/ppermute | solution.py:19
  553.6 24.6 %collective-permute-start.24 = (bf16[4,128,1024]{2,1,0:T(8,128)(2,1)}, bf16[4,128,1024]{2,1,0:T(8,128)(2,1)}, u32[]{:S(2)}, u32[]{:S(2)}) collective-permute-start(bf16[4,128,1024]{2,1,0:T(8,128)(2,1)} %get-tuple-element.139), channel_id=1, source_target_pairs={{0,1},{1,0},{2,3},{3,2},{4,5},{5,4},{6,7},{7,6},{8,9},{9,8},{10,11... | collective-permute-start | bytes 3145736 | tf_op jit(solution)/shard_map/ppermute | solution.py:19
  557.7 24.3 %collective-permute-start.45 = (bf16[4,128,1024]{2,1,0:T(8,128)(2,1)}, bf16[4,128,1024]{2,1,0:T(8,128)(2,1)}, u32[]{:S(2)}, u32[]{:S(2)}) collective-permute-start(bf16[4,128,1024]{2,1,0:T(8,128)(2,1)} %fusion), channel_id=1, source_target_pairs={{0,16},{8,24},{16,0},{24,8},{1,17},{9,25},{17,1},{25,9},{2,18},{10... | collective-permute-start | bytes 3145736 | tf_op jit(solution)/shard_map/ppermute | solution.py:19
  558.2 3.8 collective-permute-start.32
  562.0 10.8 %collective-permute-start.33 = (f32[1,16,128]{2,1,0:T(8,128)S(1)}, f32[1,16,128]{2,1,0:T(8,128)S(1)}, u32[]{:S(2)}, u32[]{:S(2)}) collective-permute-start(f32[1,16,128]{2,1,0:T(8,128)S(1)} %slice.492), channel_id=1, source_target_pairs={{0,4},{1,5},{2,6},{3,7},{4,0},{5,1},{6,2},{7,3},{8,12},{9,13},{10,... | collective-permute-start | bytes 24584 | tf_op jit(solution)/shard_map/ppermute | solution.py:19
  574.6 17.7 %collective-permute-start.38 = (bf16[2,128,1024]{2,1,0:T(8,128)(2,1)S(1)}, bf16[2,128,1024]{2,1,0:T(8,128)(2,1)S(1)}, u32[]{:S(2)}, u32[]{:S(2)}) collective-permute-start(bf16[2,128,1024]{2,1,0:T(8,128)(2,1)S(1)} %get-tuple-element.141), channel_id=1, source_target_pairs={{0,2},{1,3},{2,0},{3,1},{4,6},{5,7},{6,4},{7,5},{8,10},{9,11},{10,... | collective-permute-start | bytes 1572872 | tf_op jit(solution)/shard_map/ppermute | solution.py:19
  579.8 29.4 %collective-permute-start.25 = (bf16[2,128,1024]{2,1,0:T(8,128)(2,1)S(1)}, bf16[2,128,1024]{2,1,0:T(8,128)(2,1)S(1)}, u32[]{:S(2)}, u32[]{:S(2)}) collective-permute-start(bf16[2,128,1024]{2,1,0:T(8,128)(2,1)S(1)} %get-tuple-element.143), channel_id=1, source_target_pairs={{0,2},{1,3},{2,0},{3,1},{4,6},{5,7},{6,4},{7,5},{8,10},{9,11},{10,... | collective-permute-start | bytes 1572872 | tf_op jit(solution)/shard_map/ppermute | solution.py:19
  584.5 32.7 %collective-permute-start.46 = (bf16[2,128,1024]{2,1,0:T(8,128)(2,1)S(1)}, bf16[2,128,1024]{2,1,0:T(8,128)(2,1)S(1)}, u32[]{:S(2)}, u32[]{:S(2)}) collective-permute-start(bf16[2,128,1024]{2,1,0:T(8,128)(2,1)S(1)} %slice.524), channel_id=1, source_target_pairs={{0,2},{1,3},{2,0},{3,1},{4,6},{5,7},{6,4},{7,5},{8,10},{9,11},{10,... | collective-permute-start | bytes 1572872 | tf_op jit(solution)/shard_map/ppermute | solution.py:19
  592.4 22.6 %collective-permute-start.39 = (bf16[1,128,1024]{2,1,0:T(8,128)(2,1)S(1)}, bf16[1,128,1024]{2,1,0:T(8,128)(2,1)S(1)}, u32[]{:S(2)}, u32[]{:S(2)}) collective-permute-start(bf16[1,128,1024]{2,1,0:T(8,128)(2,1)S(1)} %add_convert_fusion.18), channel_id=1, source_target_pairs={{0,4},{1,5},{2,6},{3,7},{4,0},{5,1},{6,2},{7,3},{8,12},{9,13},{10,... | collective-permute-start | bytes 786440 | tf_op jit(solution)/shard_map/ppermute | solution.py:19
  609.3 20.7 %collective-permute-start.26 = (bf16[1,128,1024]{2,1,0:T(8,128)(2,1)S(1)}, bf16[1,128,1024]{2,1,0:T(8,128)(2,1)S(1)}, u32[]{:S(2)}, u32[]{:S(2)}) collective-permute-start(bf16[1,128,1024]{2,1,0:T(8,128)(2,1)S(1)} %add_convert_fusion.21), channel_id=1, source_target_pairs={{0,4},{1,5},{2,6},{3,7},{4,0},{5,1},{6,2},{7,3},{8,12},{9,13},{10,... | collective-permute-start | bytes 786440 | tf_op jit(solution)/shard_map/ppermute | solution.py:19
  615.2 15.0 %collective-permute-start.40 = (bf16[128,1024]{1,0:T(8,128)(2,1)S(1)}, bf16[128,1024]{1,0:T(8,128)(2,1)S(1)}, u32[]{:S(2)}, u32[]{:S(2)}) collective-permute-start(bf16[128,1024]{1,0:T(8,128)(2,1)S(1)} %bitcast.198), channel_id=1, source_target_pairs={{0,8},{8,0},{16,24},{24,16},{1,9},{9,1},{17,25},{25,17},{2,10},{10... | collective-permute-start | bytes 786440 | tf_op jit(solution)/shard_map/ppermute | solution.py:19
  617.4 16.3 %collective-permute-start.47 = (bf16[1,128,1024]{2,1,0:T(8,128)(2,1)S(1)}, bf16[1,128,1024]{2,1,0:T(8,128)(2,1)S(1)}, u32[]{:S(2)}, u32[]{:S(2)}) collective-permute-start(bf16[1,128,1024]{2,1,0:T(8,128)(2,1)S(1)} %slice.526), channel_id=1, source_target_pairs={{0,4},{1,5},{2,6},{3,7},{4,0},{5,1},{6,2},{7,3},{8,12},{9,13},{10,... | collective-permute-start | bytes 786440 | tf_op jit(solution)/shard_map/ppermute | solution.py:19
  630.1 3.7 collective-permute-start.27
  630.3 14.8 %collective-permute-start.41 = (bf16[2,128,1024]{2,1,0:T(8,128)(2,1)S(1)}, bf16[2,128,1024]{2,1,0:T(8,128)(2,1)S(1)}, u32[]{:S(2)}, u32[]{:S(2)}) collective-permute-start(bf16[2,128,1024]{2,1,0:T(8,128)(2,1)S(1)} %pad_maximum_fusion.13), channel_id=1, source_target_pairs={{0,16},{8,24},{16,0},{24,8},{1,17},{9,25},{17,1},{25,9},{2,18},{10... | collective-permute-start | bytes 1572872 | tf_op jit(solution)/shard_map/ppermute | solution.py:19
  633.9 22.4 %collective-permute-start.28 = (bf16[2,128,1024]{2,1,0:T(8,128)(2,1)S(1)}, bf16[2,128,1024]{2,1,0:T(8,128)(2,1)S(1)}, u32[]{:S(2)}, u32[]{:S(2)}) collective-permute-start(bf16[2,128,1024]{2,1,0:T(8,128)(2,1)S(1)} %pad_maximum_fusion.12), channel_id=1, source_target_pairs={{0,16},{8,24},{16,0},{24,8},{1,17},{9,25},{17,1},{25,9},{2,18},{10... | collective-permute-start | bytes 1572872 | tf_op jit(solution)/shard_map/ppermute | solution.py:19
  636.8 30.4 %collective-permute-start.49 = (bf16[2,128,1024]{2,1,0:T(8,128)(2,1)}, bf16[2,128,1024]{2,1,0:T(8,128)(2,1)}, u32[]{:S(2)}, u32[]{:S(2)}) collective-permute-start(bf16[2,128,1024]{2,1,0:T(8,128)(2,1)} %pad_maximum_fusion.14), channel_id=1, source_target_pairs={{0,16},{8,24},{16,0},{24,8},{1,17},{9,25},{17,1},{25,9},{2,18},{10... | collective-permute-start | bytes 1572872 | tf_op jit(solution)/shard_map/ppermute | solution.py:19
  (52 other events, 795.5 us)

commit v3 on v2

--- a/solution.py
+++ b/solution.py
@@ -34,45 +34,8 @@
     return found
 
 
-def gather_shards(piece, n, last=0):
-    held = piece[None]
-    for bit in reversed(range(last, n.bit_length() - 1)):
-        held = jnp.concatenate([held, swap(held, "fsdp", n, bit)])
-    return held
-
-
-def gather_quarters(piece, n):
-    own = gather_shards(piece, n)
-    beside = core_swap(own)
-    across = x_swap(own)
-    return own, beside, across, core_swap(across)
-
-
 def add_half(a, b):
     return (a.astype(full) + b.astype(full)).astype(half)
-
-
-def scatter_shards(low, high, n):
-    for bit in range(n.bit_length() - 1):
-        got = swap(high, "fsdp", n, bit)
-        size = low.shape[0] // 2
-        if size:
-            low, high = add_half(low[:size], got[:size]), add_half(low[size:], got[size:])
-        else:
-            low = add_half(low, got)
-    return low[0]
-
-
-def reduce_quarters(parts, n):
-    middle = n // 2
-    beside = core_swap(parts[1])
-    across = add_half(parts[2], core_swap(parts[3]))
-    got = x_swap(across)
-    total = [
-        (parts[0][s].astype(full) + beside[s].astype(full) + got[s].astype(full)).astype(half)
-        for s in (slice(0, middle), slice(middle, None))
-    ]
-    return scatter_shards(total[0], total[1], n)
 
 
 def spread_quarters(piece, q):
@@ -85,6 +48,60 @@
     return [jnp.where(upper, once[i ^ 2], once[i]) for i in range(4)]
 
 
+class Order:
+    def __init__(self, value):
+        self.value = value
+
+    def at(self, value):
+        value, self.value = lax.optimization_barrier((value, self.value))
+        return value
+
+
+class Gather:
+    def __init__(self, seq, piece, n):
+        self.seq, self.held, self.n = seq, piece[None], n
+        self.bits = list(reversed(range(n.bit_length() - 1)))
+        while len(self.bits) > 3:
+            self.launch()
+            self.land()
+
+    def launch(self):
+        self.held = self.seq.at(self.held)
+        self.flight = swap(self.held, "fsdp", self.n, self.bits.pop(0))
+
+    def land(self):
+        self.held = jnp.concatenate([self.held, self.seq.at(self.flight)])
+        return self.held
+
+
+class Reduce:
+    def __init__(self, seq, terms, n):
+        self.seq, self.n, self.bits = seq, n, list(range(n.bit_length() - 1))
+        middle = n // 2
+        self.low, self.high = [
+            sum(t[part].astype(full) for t in terms).astype(half)
+            for part in (slice(0, middle), slice(middle, None))
+        ]
+
+    def launch(self):
+        self.high = self.seq.at(self.high)
+        self.flight = swap(self.high, "fsdp", self.n, self.bits.pop(0))
+
+    def land(self):
+        got = self.seq.at(self.flight)
+        size = self.low.shape[0] // 2
+        if size:
+            self.low, self.high = add_half(self.low[:size], got[:size]), add_half(self.low[size:], got[size:])
+        else:
+            self.low = add_half(self.low, got)
+
+    def rest(self):
+        while self.bits:
+            self.launch()
+            self.land()
+        return self.low[0]
+
+
 ANYWHERE = pl.BlockSpec(memory_space=pl.ANY)
 ON_CHIP = pl.BlockSpec(memory_space=pltpu.VMEM)
 SCALARS = pl.BlockSpec(memory_space=pltpu.SMEM)
@@ -96,7 +113,7 @@
     )
 
 
-def call(kernel, name, operands, in_specs, outs, out_specs, scratch, flops, moved, transcendentals=0):
+def call(kernel, name, operands, in_specs, outs, out_specs, scratch):
     return pl.pallas_call(
         kernel,
         out_shape=[jax.ShapeDtypeStruct(shape, kind) for shape, kind in outs],
@@ -104,9 +121,6 @@
         out_specs=out_specs,
         scratch_shapes=scratch,
         compiler_params=pltpu.CompilerParams(vmem_limit_bytes=58 * 2**20),
-        cost_estimate=pl.CostEstimate(
-            flops=flops, bytes_accessed=moved, transcendentals=transcendentals
-        ),
         name=name,
     )(*operands)
 
@@ -188,8 +202,6 @@
         [((count, wide), half)] * groups + [((count, quarter), half)] * groups,
         [ON_CHIP] * (2 * groups),
         [pltpu.VMEM((groups, width, wide), half), pltpu.SemaphoreType.DMA((groups,))],
-        groups * 2 * count * width * wide,
-        2 * (count * width + groups * (width * wide + count * (wide + quarter))),
     )
 
 
@@ -218,7 +230,7 @@
         for j in range(4):
             column = pl.multiple_of((q ^ j) * quarter, quarter)
             pltpu.make_async_copy(
-                up_refs[j].at[r, :, pl.ds(hidden, quarter)],
+                up_refs[j % 2].at[r, :, pl.ds(hidden + j // 2 * quarter, quarter)],
                 held.at[pl.ds(at, rows), pl.ds(column, quarter)],
                 sem,
             ).start()
@@ -233,11 +245,11 @@
     count, width = x_zero.shape
     n, rows, _ = ups[0].shape
     quarter = mixed[0].shape[1]
-    hidden = ups[0].shape[2] - quarter
+    hidden = ups[0].shape[2] - 2 * quarter
 
     def kernel(order_ref, x_ref, bias_ref, gain_ref, shift_ref, *refs):
-        mixed_refs, up_refs = refs[:4], refs[4:8]
-        after_ref, normed_ref, held, sems = refs[8:]
+        mixed_refs, up_refs = refs[:4], refs[4:6]
+        after_ref, normed_ref, held, sems = refs[6:]
         load_out(order_ref, up_refs, held, sems.at[0], n, rows, hidden, quarter)
         together = jnp.concatenate([m[...] for m in mixed_refs], axis=1)
         pltpu.make_async_copy(held, held, sems.at[0]).wait()
@@ -255,12 +267,10 @@
         kernel,
         "attention_out",
         (order, x_zero, bias, gain, shift, *mixed, *ups),
-        [SCALARS] + [ON_CHIP] * 8 + [ANYWHERE] * 4,
+        [SCALARS] + [ON_CHIP] * 8 + [ANYWHERE] * 2,
         [((count, width), full), ((count, width), half)],
         [ON_CHIP] * 2,
         [pltpu.VMEM((width, width), half), pltpu.SemaphoreType.DMA((1,))],
-        2 * count * width * width,
-        14 * count * width + 2 * width * width,
     )
 
 
@@ -381,9 +391,6 @@
             pltpu.SemaphoreType.DMA((2 * groups,)),
             pltpu.SemaphoreType.DMA((2 * groups,)),
         ],
-        groups * 12 * count * width * hidden,
-        groups * 8 * width * hidden + 20 * count * width,
-        groups * 2 * count * hidden,
     )
 
 
@@ -391,10 +398,10 @@
     count, width = after.shape
     n, rows, _ = ups[0].shape
     quarter = mixed[0].shape[1]
-    hidden = ups[0].shape[2] - quarter
+    hidden = ups[0].shape[2] - 2 * quarter
 
     def kernel(order_ref, grad_ref, after_ref, cot_ref, gain_ref, *refs):
-        mixed_refs, up_refs, refs = refs[:4], refs[4:8], refs[8:]
+        mixed_refs, up_refs, refs = refs[:4], refs[4:6], refs[6:]
         after_grad_ref, mixed_grad_refs, g_out_ref, sums_ref = refs[0], refs[1:5], refs[5], refs[6]
         held, branch, terms, sems = refs[7:]
         load_out(order_ref, up_refs, held, sems.at[0], n, rows, hidden, quarter)
@@ -429,7 +436,7 @@
         kernel,
         "attention_out_back",
         (order, grad, after, cot, gain, *mixed, *ups),
-        [SCALARS] + [ON_CHIP] * 8 + [ANYWHERE] * 4,
+        [SCALARS] + [ON_CHIP] * 8 + [ANYWHERE] * 2,
         [((count, width), full)]
         + [((count, quarter), half)] * 4
         + [((width, width), half), ((4, 1, width), full)],
@@ -440,8 +447,6 @@
             pltpu.VMEM((4, 8, width), full),
             pltpu.SemaphoreType.DMA((1,)),
         ],
-        4 * count * width * width,
-        18 * count * width + 4 * width * width,
     )
 
 
@@ -520,8 +525,6 @@
         + [((groups, 1, wide), full)],
         [ANYWHERE] * groups + [ON_CHIP] * (groups + 1),
         [pltpu.VMEM((groups, width, wide), half), pltpu.SemaphoreType.DMA((groups,))],
-        groups * 2 * count * width * wide * 2,
-        2 * (count * width + width * width + groups * (width * wide + count * (2 * wide + quarter))),
     )
 
 
@@ -575,8 +578,6 @@
             pltpu.VMEM((2, 8, width), full),
             pltpu.SemaphoreType.DMA((4,)),
         ],
-        8 * count * width * wide,
-        12 * count * width + 8 * (width + count) * wide,
     )
 
 
@@ -627,11 +628,59 @@
     def pick(value, axis):
         return lax.dynamic_index_in_dim(value, q, axis, keepdims=False)
 
+    seq = Order(q)
+
+    qkv_own = pick(w_qkv.reshape(rows, 3, 4, quarter), 2).reshape(rows, 3 * quarter).astype(half)
+    qkv = Gather(seq, qkv_own, n)
+    qkv.launch()
     small = jnp.concatenate(
         [b_q, b_v, b_out, gain_one, shift_one, b_fc2, gain_two, shift_two, b_fc1]
     ).astype(half)
     pad = -small.shape[0] % 2048
-    small_held = gather_shards(jnp.pad(small, (0, pad)).reshape(-1, 128), n).reshape(n, -1)
+    vec = Gather(seq, jnp.pad(small, (0, pad)).reshape(-1, 128), n)
+    vec.launch()
+    out_own = [
+        lax.dynamic_index_in_dim(w_out.reshape(rows, 4, quarter), g, 1, keepdims=False) for g in (q, q ^ 2)
+    ]
+    fc1_own = pick(w_fc1.reshape(rows, n, 4, ffq), 2).reshape(rows, n * ffq)
+    up = Gather(seq, jnp.concatenate([fc1_own, *out_own], axis=1).astype(half), n)
+    fc2_own, fc2_across = [
+        lax.dynamic_index_in_dim(w_fc2.reshape(4, ffq, width), g, 0, keepdims=False).astype(half)
+        for g in (q, q ^ 2)
+    ]
+    down = Gather(seq, fc2_own, n)
+    down_two = Gather(seq, fc2_across, n)
+
+    def spread_rows(value):
+        split = value.reshape(n_img, patches, width)
+        return jnp.pad(split, ((0, 0), (0, padded - patches), (0, 0)))
+
+    def compact(value):
+        return value.reshape(n_img, padded, width)[:, :patches].reshape(row_count, width)
+
+    places = table(scale_codes, width)
+    row_place = jnp.broadcast_to(places[:, :, None], (n_img, GRID, GRID, width // 2))
+    col_place = jnp.broadcast_to(places[:, None], (n_img, GRID, GRID, width // 2))
+    place = jnp.concatenate([row_place, col_place], axis=-1).reshape(n_img, patches, width)
+    place = jnp.pad(place, ((0, 0), (0, padded - patches), (0, 0)))
+    x_zero = (spread_rows(tokens).astype(full) + place).reshape(-1, width)
+    cot = spread_rows(cotangent).reshape(-1, width)
+
+    qkv.land()
+    qkv.launch()
+    vec.land()
+    vec.launch()
+    x_zero = seq.at(x_zero)
+    qkv.land()
+    qkv.launch()
+    up.launch()
+    vec.land()
+    vec.launch()
+    cot = seq.at(cot)
+    up.land()
+    up.launch()
+    down.launch()
+    small_held = vec.land().reshape(n, -1)
     inverse = jnp.zeros((n,), jnp.int32).at[shard_order].set(jnp.arange(n, dtype=jnp.int32))
     small_all = jnp.take(small_held, inverse, axis=0).astype(full)
     vectors = [small_all[:, i * rows : (i + 1) * rows].reshape(1, width) for i in range(8)]
@@ -641,94 +690,119 @@
     bias_q = jnp.take(full_bq.reshape(4, quarter), group_order, axis=0)
     bias_v = jnp.take(full_bv.reshape(4, quarter), group_order, axis=0)
     bias_qkv = jnp.concatenate([bias_q, jnp.zeros_like(bias_q), bias_v], axis=1)[:, None]
-
-    qkv_own = pick(w_qkv.reshape(rows, 3, 4, quarter), 2).reshape(rows, 3 * quarter).astype(half)
-    qkv_parts = gather_quarters(qkv_own, n)
-    out_own = pick(w_out.reshape(rows, 4, quarter), 1).astype(half)
-    fc1_own = pick(w_fc1.reshape(rows, n, 4, ffq), 2).reshape(rows, n * ffq).astype(half)
-    up_parts = gather_quarters(jnp.concatenate([fc1_own, out_own], axis=1), n)
-    fc2_own = pick(w_fc2.reshape(4, ffq, width), 0).astype(half)
-    column = gather_shards(fc2_own, n, 1)
-    both = jnp.stack([column, x_swap(column)])
-    far = swap(both, "fsdp", n, 0)
-    down_own = jnp.concatenate([both[0], far[0]])
-    down_across = jnp.concatenate([both[1], far[1]])
-    down_parts = (down_own, core_swap(down_own), down_across, core_swap(down_across))
-
-    def spread_rows(value):
-        split = value.reshape(n_img, patches, width)
-        return jnp.pad(split, ((0, 0), (0, padded - patches), (0, 0)))
-
-    def compact(value):
-        return value.reshape(n_img, padded, width)[:, :patches].reshape(row_count, width)
-
-    places = table(scale_codes, width)
-    row_place = jnp.broadcast_to(places[:, :, None], (n_img, GRID, GRID, width // 2))
-    col_place = jnp.broadcast_to(places[:, None], (n_img, GRID, GRID, width // 2))
-    place = jnp.concatenate([row_place, col_place], axis=-1).reshape(n_img, patches, width)
-    place = jnp.pad(place, ((0, 0), (0, padded - patches), (0, 0)))
-    x_zero = (spread_rows(tokens).astype(full) + place).reshape(-1, width)
-    normed_one = layer_norm(x_zero, gain_one_f, shift_one_f).astype(half)
-    cot = spread_rows(cotangent).reshape(-1, width)
-
-    first = attention_forward(order, normed_one, bias_qkv[:2], qkv_parts[:2], n_img, patches, factor)
-    second = attention_forward(order, normed_one, bias_qkv[2:], qkv_parts[2:], n_img, patches, factor)
+    normed_one = seq.at(layer_norm(x_zero, gain_one_f, shift_one_f).astype(half))
+    qkv_a = seq.at(qkv.land())
+    qkv_b, qkv_c = core_swap(qkv_a), x_swap(qkv_a)
+    qkv_b = seq.at(qkv_b)
+
+    first = attention_forward(seq.at(order), normed_one, bias_qkv[:2], (qkv_a, qkv_b), n_img, patches, factor)
+    first = (seq.at(first[0]), *first[1:])
+    up.land()
+    up.launch()
+    down.land()
+    down.launch()
+    down_two.launch()
+    qkv_c = seq.at(qkv_c)
+    qkv_d = core_swap(qkv_c)
+    qkv_d = seq.at(qkv_d)
+    down.land()
+    down.launch()
+    down_two.land()
+    down_two.launch()
+    second = attention_forward(seq.at(order), normed_one, bias_qkv[2:], (qkv_c, qkv_d), n_img, patches, factor)
+    second = (seq.at(second[0]), *second[1:])
+    qkv_parts = (qkv_a, qkv_b, qkv_c, qkv_d)
     qkvs = (*first[:2], *second[:2])
     mixed = (*first[2:], *second[2:])
+    up_a = seq.at(up.land())
+    up_b = core_swap(up_a)
+    up_c = x_swap(seq.at(up_a[:, :, :hidden]))
+    up_b = seq.at(up_b)
+    ups = (up_a, up_b)
     after_attn, normed_two = attention_out(
-        order, x_zero, mixed, up_parts, full_bout, gain_two_f, shift_two_f
-    )
+        seq.at(order), x_zero, mixed, ups, full_bout, gain_two_f, shift_two_f
+    )
+    normed_two = seq.at(normed_two)
+    down_a = seq.at(down.land())
+    down_b = core_swap(down_a)
+    down_two.land()
+    down_two.launch()
+    down_b = seq.at(down_b)
 
     g_up0, g_up1, g_down0, g_down1, g_bias_a, out_a, back_a = mlp(
-        order, normed_two, cot, bias_fc1[:2], up_parts[:2], down_parts[:2]
-    )
+        seq.at(order), normed_two, cot, bias_fc1[:2], ups, (down_a, down_b)
+    )
+    g_up1, g_down1 = seq.at((g_up1, g_down1))
+    got_up1, got_down1 = core_swap(g_up1), core_swap(g_down1)
+    up_c = seq.at(up_c)
+    up_d = core_swap(up_c)
+    down_c = seq.at(down_two.land())
+    down_d = core_swap(down_c)
+    up_d, down_d = seq.at((up_d, down_d))
     g_up2, g_up3, g_down2, g_down3, g_bias_b, _, grad_two_in, block = mlp(
-        order, normed_two, cot, bias_fc1[2:], up_parts[2:], down_parts[2:], (out_a, back_a), (after_attn, full_bfc2)
+        seq.at(order), normed_two, cot, bias_fc1[2:], (up_c, up_d), (down_c, down_d),
+        (out_a, back_a), (after_attn, full_bfc2),
     )
     block_out = compact(block)
-    up_grads = (g_up0, g_up1, g_up2, g_up3)
-    down_grads = (g_down0, g_down1, g_down2, g_down3)
-
-    middle = n // 2
-    pair_low, pair_high = [], []
-    for a, b in ((0, 1), (2, 3)):
-        got = core_swap(down_grads[b])
-        pair_low.append(add_half(down_grads[a][:middle], got[:middle]))
-        pair_high.append(add_half(down_grads[a][middle:], got[middle:]))
-    far = swap(jnp.stack(pair_high), "fsdp", n, 0)
-    across = x_swap(add_half(pair_low[1], far[1]))
-    down_low = (pair_low[0].astype(full) + far[0].astype(full) + across.astype(full)).astype(half)
-    for bit in range(1, n.bit_length() - 1):
-        size = down_low.shape[0] // 2
-        got = swap(down_low[size:], "fsdp", n, bit)
-        down_low = add_half(down_low[:size], got)
-    down_pieces = spread_quarters(down_low[0], q)
-    out_fc2 = jnp.concatenate(down_pieces).astype(full)
-    up_pieces = spread_quarters(reduce_quarters(up_grads, n), q)
-    out_fc1 = (
-        jnp.stack([p.reshape(rows, n, ffq) for p in up_pieces], axis=2).reshape(rows, ff).astype(full)
-    )
+    got_up1, got_down1 = seq.at((got_up1, got_down1))
+    g_up3, g_down3 = seq.at((g_up3, g_down3))
+    got_up3, got_down3 = core_swap(g_up3), core_swap(g_down3)
+    red_down = Reduce(seq, (g_down0, got_down1), n)
+    red_down.launch()
+    got_up3 = seq.at(got_up3)
+    up_across = x_swap(seq.at(add_half(g_up2, got_up3)))
+    got_down3 = seq.at(got_down3)
+    red_down_two = Reduce(seq, (g_down2, got_down3), n)
+    red_down_two.launch()
 
     after_grad, mg0, mg1, mg2, mg3, g_out, sums_two = attention_out_back(
-        order, grad_two_in, after_attn, cot, gain_two_f, mixed, up_parts
-    )
+        seq.at(order), grad_two_in, after_attn, cot, gain_two_f, mixed, ups
+    )
+    mg2 = seq.at(mg2)
+    red_down.land()
+    red_down.launch()
     g_w2, g_w3, proj2, proj3, sums_b = attention_back(
-        order, normed_one, qkvs[2:], (mg2, mg3), g_out, (2, 3), n_img, patches, factor, n
-    )
+        seq.at(order), normed_one, qkvs[2:], (mg2, mg3), g_out, (2, 3), n_img, patches, factor, n
+    )
+    g_w3 = seq.at(g_w3)
+    red_down.land()
+    red_down_two.land()
+    up_across = seq.at(up_across)
+    got_w3 = core_swap(seq.at(g_w3))
+    red_up = Reduce(seq, (g_up0, got_up1, up_across), n)
+    red_up.launch()
+    red_down.launch()
+    red_down_two.launch()
+    got_w3 = seq.at(got_w3)
+    red_w_two = Reduce(seq, (g_w2, got_w3), n)
+    red_w_two.launch()
     g_w0, g_w1, proj0, proj1, sums_a = attention_back(
-        order, normed_one, qkvs[:2], (mg0, mg1), g_out, (0, 1), n_img, patches, factor, n
-    )
-    attn_pieces = spread_quarters(reduce_quarters((g_w0, g_w1, g_w2, g_w3), n), q)
-    out_qkv = (
-        jnp.stack([p[:, : 3 * quarter].reshape(rows, 3, quarter) for p in attn_pieces], axis=2)
-        .reshape(rows, 3 * width)
-        .astype(full)
-    )
-    out_out = jnp.stack([p[:, 3 * quarter :] for p in attn_pieces], axis=1).reshape(rows, width).astype(full)
+        seq.at(order), normed_one, qkvs[:2], (mg0, mg1), g_out, (0, 1), n_img, patches, factor, n
+    )
+    g_w1 = seq.at(g_w1)
+    red_down.land()
+    red_down_two.land()
+    red_up.land()
+    red_w_two.land()
+    got_w1 = core_swap(seq.at(g_w1))
+    red_down_two.launch()
+    red_up.launch()
+    red_w_two.launch()
+    got_w1 = seq.at(got_w1)
+    red_w = Reduce(seq, (g_w0, got_w1), n)
+    red_w.launch()
     tokens_grad, sums_one = input_back(
-        order, x_zero, after_grad, gain_one_f, (proj0, proj1, proj2, proj3), qkv_parts
-    )
+        seq.at(order), x_zero, after_grad, gain_one_f, (proj0, proj1, proj2, proj3), qkv_parts
+    )
+    tokens_grad = seq.at(tokens_grad)
     grad_tokens = compact(tokens_grad)
+    red_w.land()
+    red_w.launch()
+    red_down_two.land()
+    red_up.land()
+    red_w_two.land()
+    red_up.launch()
+    red_w_two.launch()
 
     sums_proj = jnp.take(jnp.concatenate([sums_a, sums_b])[:, 0], group_order, axis=0)
     sums = [
@@ -747,12 +821,33 @@
     packed = jnp.take(packed, shard_order, axis=0)
     pad = -packed.shape[1] % 1024
     packed = jnp.pad(packed, ((0, 0), (0, pad))).reshape(n, -1, 128)
-    packed = packed + core_swap(packed)
-    packed = packed + x_swap(packed)
+    packed = packed + seq.at(core_swap(seq.at(packed)))
+    packed = packed + seq.at(x_swap(packed))
     for bit in range(n.bit_length() - 1):
         size = packed.shape[0] // 2
         packed = packed[:size] + swap(packed[size:], "fsdp", n, bit)
     vector = packed.reshape(-1)
+
+    down_shard = add_half(red_down.rest(), x_swap(red_down_two.rest()))
+    down_pieces = spread_quarters(down_shard, q)
+    out_fc2 = jnp.concatenate(down_pieces).astype(full)
+    red_up.land()
+    up_pieces = spread_quarters(red_up.rest(), q)
+    out_fc1 = (
+        jnp.stack([p.reshape(rows, n, ffq) for p in up_pieces], axis=2).reshape(rows, ff).astype(full)
+    )
+    red_w.land()
+    red_w.launch()
+    red_w_two.land()
+    two_shard = x_swap(seq.at(red_w_two.rest()))
+    red_w.land()
+    attn_pieces = spread_quarters(add_half(red_w.rest(), two_shard), seq.value)
+    out_qkv = (
+        jnp.stack([p[:, : 3 * quarter].reshape(rows, 3, quarter) for p in attn_pieces], axis=2)
+        .reshape(rows, 3 * width)
+        .astype(full)
+    )
+    out_out = jnp.stack([p[:, 3 * quarter :] for p in attn_pieces], axis=1).reshape(rows, width).astype(full)
     small_out = [vector[i * rows : (i + 1) * rows] for i in range(8)]
     out_bfc1 = vector[8 * rows : 8 * rows + 4 * ffq]
     o_bq, o_bv, o_bout, o_gone, o_sone, o_bfc2, o_gtwo, o_stwo = small_out

time: 678 us -> 546 us (0.81)
  waiting for transfers between devices: 284 us -> 123 us
  starting transfers between devices: 42.7 us -> 59.9 us
  other arithmetic: 49.1 us -> 65 us
    ppermute x50 -> x58, waiting for transfers between devices: 284 us -> 123 us  [swap(): return lax.ppermute(value, axis, [(i, i ^ 1 << bit) for i in range(size)])]
    ppermute x50 -> x58, starting transfers between devices: 42.7 us -> 59.9 us  [swap(): return lax.ppermute(value, axis, [(i, i ^ 1 << bit) for i in range(size)])]
    convert_element_type x5 -> x6, other arithmetic: 10 us -> 16.1 us  [the longest x5 14.3 us: __init__(): sum((t[part].astype(full) for t in terms)).astype(half)]
    convert_element_type x11 -> x14, other arithmetic: 13.7 us -> 18.7 us  [add_half(): return (a.astype(full) + b.astype(full)).astype(half)]
  transfers between devices with their start and end apart: 50 -> 58, of which waited for: 24 -> 23; matrix products, arithmetic and copies ran while one was open for 14% -> 18% of each run, Pallas kernels for 29% -> 36%
where the time goes in v3:
time: 546 us; the launch traced here: 540 us
  Pallas kernels  237 us (43%)
  waiting for transfers between devices  123 us (23%)
  other arithmetic  65 us (12%)
  starting transfers between devices  59.9 us (11%)
  local copies, waits for them, and re-layouts  52.1 us (10%)
    pallas_call x9, Pallas kernels, call(): pl.pallas_call(kernel, out_shape=[jax.ShapeDtypeStruct(shape, kind) for s...  237 us
    ppermute x58, waiting for transfers between devices, swap(): return lax.ppermute(value, axis, [(i, i ^ 1 << bit) for i in range(size)])  123 us
    ppermute x58, starting transfers between devices, swap(): return lax.ppermute(value, axis, [(i, i ^ 1 << bit) for i in range(size)])  59.9 us
    convert_element_type x14, other arithmetic, add_half(): return (a.astype(full) + b.astype(full)).astype(half)  18.7 us
    convert_element_type x5, other arithmetic, __init__(): sum((t[part].astype(full) for t in terms)).astype(half)  14.3 us
    unnamed x152, local copies, waits for them, and re-layouts  12 us
    concatenate x14, other arithmetic, land(): self.held = jnp.concatenate([self.held, self.seq.at(self.flight)])  11.5 us
  transfers between devices with their start and end apart: 58, of which 23 were waited for; matrix products, arithmetic and copies ran while one was open for 18% of the time, Pallas kernels for 36%

profile of v3, /device:TPU:0, one launch (start us, length us, event | category | flops | bytes accessed | tf_op | source)
XLA Modules:
  0.0 539.7 jit_solution(10264723773077452315)
XLA Ops:
  3.5 4.0 collective-permute-start
  12.8 3.6 copy.63
  18.3 2.7 reshape.306
  21.7 2.1 dynamic-slice_convert_fusion
  24.6 2.9 pad_add_fusion
  27.5 2.3 pad_maximum_fusion.16
  29.8 1.9 collective-permute-start.1
  31.7 2.5 reshape.312
  34.1 2.8 pad.22
  37.4 3.4 collective-permute-done.1
  40.8 2.1 pad_maximum_fusion.8
  42.9 2.6 collective-permute-start.3
  48.1 13.9 %collective-permute-done.3 = bf16[1,128,1536]{2,1,0:T(8,128)(2,1)S(1)} collective-permute-done((bf16[1,128,1536]{2,1,0:T(8,128)(2,1)}, bf16[1,128,1536]{2,1,0:T(8,128)(2,1)S(1)}, u32[]{:S(2)}, u32[]{:S(2)}) %collective-permute-start.3) | collective-permute-done | bytes 393248 | tf_op jit(solution)/shard_map/ppermute | solution.py:19
  72.5 3.1 collective-permute-start.10
  76.7 18.1 %attention_forward.2 = (bf16[832,768]{1,0:T(8,128)(2,1)}, bf16[832,768]{1,0:T(8,128)(2,1)}, bf16[832,256]{1,0:T(8,128)(2,1)}, bf16[832,256]{1,0:T(8,128)(2,1)}) custom-call(s32[9]{0:T(128)} %pad_add_fusion.1.order_ref, bf16[832,1024]{1,0:T(8,128)(2,1)} %add_convert_fusion.1.normed_ref, f32[2,1,768]{2,1,0:T(1,128)} %copy.64.bias_ref, ...), custom_call_target="tpu_custom_call" | custom-call | tf_op jit(solution)/shard_map/attention_forward/pallas_call | solution.py:117
  96.4 8.2 %collective-permute-done.13.refs_0_.refs_6_ = bf16[8,128,768]{2,1,0:T(8,128)(2,1)} collective-permute-done((bf16[8,128,768]{2,1,0:T(8,128)(2,1)S(1)}, bf16[8,128,768]{2,1,0:T(8,128)(2,1)}, u32[]{:S(2)}, u32[]{:S(2)}) %collective-permute-start.13) | collective-permute-done | bytes 1572896 | tf_op jit(solution)/shard_map/ppermute | solution.py:19
  106.6 3.3 collective-permute-start.11
  110.5 15.0 %collective-permute-done.12 = bf16[2,128,1024]{2,1,0:T(8,128)(2,1)S(1)} collective-permute-done((bf16[2,128,1024]{2,1,0:T(8,128)(2,1)S(1)}, bf16[2,128,1024]{2,1,0:T(8,128)(2,1)S(1)}, u32[]{:S(2)}, u32[]{:S(2)}) %collective-permute-start.12) | collective-permute-done | bytes 524320 | tf_op jit(solution)/shard_map/ppermute | solution.py:19
  126.5 18.1 %attention_forward.3 = (bf16[832,768]{1,0:T(8,128)(2,1)}, bf16[832,768]{1,0:T(8,128)(2,1)}, bf16[832,256]{1,0:T(8,128)(2,1)}, bf16[832,256]{1,0:T(8,128)(2,1)}) custom-call(s32[9]{0:T(128)} %pad_add_fusion.1.order_ref, bf16[832,1024]{1,0:T(8,128)(2,1)} %add_convert_fusion.1.normed_ref, f32[2,1,768]{2,1,0:T(1,128)} %slice.391.bias_ref, ...), custom_call_target="tpu_custom_call" | custom-call | tf_op jit(solution)/shard_map/attention_forward/pallas_call | solution.py:117
  147.4 3.2 collective-permute-done.17.refs_5_.refs_1_
  152.3 18.0 %attention_out.1 = (f32[832,1024]{1,0:T(8,128)}, bf16[832,1024]{1,0:T(8,128)(2,1)}) custom-call(s32[9]{0:T(128)} %pad_add_fusion.1.order_ref, f32[832,1024]{1,0:T(8,128)} %bitcast.166, f32[1,1024]{1,0:T(1,128)} %bitcast.207, f32[1,1024]{1,0:T(1,128)} %bitcast.200, f32[1,1024]{1,0:T(1,128)} %bitcast.206, bf16[832,256]{1,0:T(8,128)(2,1)} %get-tuple-element.353.refs_0_, ...), custom_call_target="tpu_custom_call" | custom-call | tf_op jit(solution)/shard_map/attention_out/pallas_call | solution.py:117
  172.4 2.2 collective-permute-start.19
  174.5 12.3 %collective-permute-done.19 = bf16[2,128,1024]{2,1,0:T(8,128)(2,1)S(1)} collective-permute-done((bf16[2,128,1024]{2,1,0:T(8,128)(2,1)S(1)}, bf16[2,128,1024]{2,1,0:T(8,128)(2,1)S(1)}, u32[]{:S(2)}, u32[]{:S(2)}) %collective-permute-start.19) | collective-permute-done | bytes 524320 | tf_op jit(solution)/shard_map/ppermute | solution.py:19
  189.3 38.2 %mlp.2 = (bf16[8,128,1024]{2,1,0:T(8,128)(2,1)}, bf16[8,128,1024]{2,1,0:T(8,128)(2,1)}, bf16[8,128,1024]{2,1,0:T(8,128)(2,1)}, bf16[8,128,1024]{2,1,0:T(8,128)(2...) custom-call(s32[9]{0:T(128)} %pad_add_fusion.1.order_ref, ...), custom_call_target="tpu_custom_call" | custom-call | tf_op jit(solution)/shard_map/mlp/pallas_call | solution.py:117
  230.3 5.3 collective-permute-done.22.refs_7_
  235.6 6.6 %collective-permute-done.20.refs_5_ = bf16[8,128,1024]{2,1,0:T(8,128)(2,1)S(1)} collective-permute-done((bf16[8,128,1024]{2,1,0:T(8,128)(2,1)}, bf16[8,128,1024]{2,1,0:T(8,128)(2,1)S(1)}, u32[]{:S(2)}, u32[]{:S(2)}) %collective-permute-start.20) | collective-permute-done | bytes 2097184 | tf_op jit(solution)/shard_map/ppermute | solution.py:19
  244.2 42.3 %mlp.3 = (bf16[8,128,1024]{2,1,0:T(8,128)(2,1)}, bf16[8,128,1024]{2,1,0:T(8,128)(2,1)}, bf16[8,128,1024]{2,1,0:T(8,128)(2,1)}, bf16[8,128,1024]{2,1,0:T(8,128)(2...) custom-call(s32[9]{0:T(128)} %pad_add_fusion.1.order_ref, ...), custom_call_target="tpu_custom_call" | custom-call | tf_op jit(solution)/shard_map/mlp/pallas_call | solution.py:117
  287.1 3.7 add_convert_fusion.10
  294.2 2.0 add_convert_fusion.8
  297.5 24.3 %attention_out_back.1 = (f32[832,1024]{1,0:T(8,128)}, bf16[832,256]{1,0:T(8,128)(2,1)}, bf16[832,256]{1,0:T(8,128)(2,1)}, bf16[832,256]{1,0:T(8,128)(2,1)}, bf16...) custom-call(s32[9]{0:T(128)} %pad_add_fusion.1.order_ref, ...), custom_call_target="tpu_custom_call" | custom-call | tf_op jit(solution)/shard_map/attention_out_back/pallas_call | solution.py:117
  321.8 2.4 add_convert_fusion.19
  326.0 24.8 %attention_back.2 = (bf16[8,128,1024]{2,1,0:T(8,128)(2,1)}, bf16[8,128,1024]{2,1,0:T(8,128)(2,1)}, bf16[832,768]{1,0:T(8,128)(2,1)}, bf16[832,768]{1,0:T(8,128)(2,1)}, f32[2,1,768]{2,1,0:T(1,128)}) custom-call(s32[9]{0:T(128)} %pad_add_fusion.1.order_ref, bf16[832,1024]{1,0:T(8,128)(2,1)} %add_convert_fusion.1.normed_ref, ...), custom_call_target="tpu_custom_call" | custom-call | tf_op jit(solution)/shard_map/attention_back/pallas_call | solution.py:117
  353.8 4.0 add_convert_fusion.4
  363.1 24.8 %attention_back.3 = (bf16[8,128,1024]{2,1,0:T(8,128)(2,1)}, bf16[8,128,1024]{2,1,0:T(8,128)(2,1)}, bf16[832,768]{1,0:T(8,128)(2,1)}, bf16[832,768]{1,0:T(8,128)(2,1)}, f32[2,1,768]{2,1,0:T(1,128)}) custom-call(s32[9]{0:T(128)} %pad_add_fusion.1.order_ref, bf16[832,1024]{1,0:T(8,128)(2,1)} %add_convert_fusion.1.normed_ref, ...), custom_call_target="tpu_custom_call" | custom-call | tf_op jit(solution)/shard_map/attention_back/pallas_call | solution.py:117
  388.0 17.6 %collective-permute-done.32 = bf16[4,128,1024]{2,1,0:T(8,128)(2,1)} collective-permute-done((bf16[4,128,1024]{2,1,0:T(8,128)(2,1)S(1)}, bf16[4,128,1024]{2,1,0:T(8,128)(2,1)}, u32[]{:S(2)}, u32[]{:S(2)}) %collective-permute-start.32) | collective-permute-done | bytes 1048608 | tf_op jit(solution)/shard_map/ppermute | solution.py:19
  409.0 2.4 add_convert_fusion.13
  411.4 2.6 add_convert_fusion.12
  417.9 3.5 add_convert_fusion.2
  422.1 28.2 %input_back.1 = (f32[832,1024]{1,0:T(8,128)}, f32[2,1,1024]{2,1,0:T(1,128)}) custom-call(s32[9]{0:T(128)} %pad_add_fusion.1.order_ref, f32[832,1024]{1,0:T(8,128)} %bitcast.167, f32[832,1024]{1,0:T(8,128)} %get-tuple-element.482.after_ref, f32[1,1024]{1,0:T(1,128)} %bitcast.204, bf16[832,768]{1,0:T(8,128)(2,1)} %get-tuple-element.483.refs_0_, ...), custom_call_target="tpu_custom_call" | custom-call | tf_op jit(solution)/shard_map/input_back/pallas_call | solution.py:117
  452.0 2.6 add_convert_fusion.14
  454.6 1.9 add_convert_fusion.34
  460.2 2.8 collective-permute-done.44
  464.4 2.6 collective-permute-done.50
  470.7 2.2 slice.548
  484.0 5.1 collective-permute-done.52
  493.5 8.2 %collective-permute-done.38 = bf16[2,128,1024]{2,1,0:T(8,128)(2,1)S(1)} collective-permute-done((bf16[2,128,1024]{2,1,0:T(8,128)(2,1)}, bf16[2,128,1024]{2,1,0:T(8,128)(2,1)S(1)}, u32[]{:S(2)}, u32[]{:S(2)}) %collective-permute-start.38) | collective-permute-done | bytes 524320 | tf_op jit(solution)/shard_map/ppermute | solution.py:19
  507.7 8.3 %collective-permute-done.45 = bf16[1,128,1024]{2,1,0:T(8,128)(2,1)S(1)} collective-permute-done((bf16[1,128,1024]{2,1,0:T(8,128)(2,1)S(1)}, bf16[1,128,1024]{2,1,0:T(8,128)(2,1)S(1)}, u32[]{:S(2)}, u32[]{:S(2)}) %collective-permute-start.45) | collective-permute-done | bytes 262176 | tf_op jit(solution)/shard_map/ppermute | solution.py:19
  526.4 7.7 %collective-permute-done.49 = bf16[2,128,1024]{2,1,0:T(8,128)(2,1)} collective-permute-done((bf16[2,128,1024]{2,1,0:T(8,128)(2,1)}, bf16[2,128,1024]{2,1,0:T(8,128)(2,1)}, u32[]{:S(2)}, u32[]{:S(2)}) %collective-permute-start.49) | collective-permute-done | bytes 524320 | tf_op jit(solution)/shard_map/ppermute | solution.py:19
  (390 shorter events, 115.0 us)
Async XLA Ops:
  3.5 24.1 %collective-permute-start = (bf16[1,128,768]{2,1,0:T(8,128)(2,1)}, bf16[1,128,768]{2,1,0:T(8,128)(2,1)}, u32[]{:S(2)}, u32[]{:S(2)}) collective-permute-start(bf16[1,128,768]{2,1,0:T(8,128)(2,1)} %copy.62), channel_id=1, source_target_pairs={{0,4},{1,5},{2,6},{3,7},{4,0},{5,1},{6,2},{7,3},{8,12},{9,13},{10,... | collective-permute-start | bytes 589832 | tf_op jit(solution)/shard_map/ppermute | solution.py:19
  9.4 27.6 %collective-permute-start.2 = (bf16[1,16,128]{2,1,0:T(8,128)(2,1)S(1)}, bf16[1,16,128]{2,1,0:T(8,128)(2,1)S(1)}, u32[]{:S(2)}, u32[]{:S(2)}) collective-permute-start(bf16[1,16,128]{2,1,0:T(8,128)(2,1)S(1)} %pad_bitcast_fusion.1), channel_id=1, source_target_pairs={{0,4},{1,5},{2,6},{3,7},{4,0},{5,1},{6,2},{7,3},{8,12},{9,13},{10,... | collective-permute-start | bytes 12296 | tf_op jit(solution)/shard_map/ppermute | solution.py:19
  29.8 11.0 %collective-permute-start.1 = (bf16[2,128,768]{2,1,0:T(8,128)(2,1)}, bf16[2,128,768]{2,1,0:T(8,128)(2,1)}, u32[]{:S(2)}, u32[]{:S(2)}) collective-permute-start(bf16[2,128,768]{2,1,0:T(8,128)(2,1)} %pad_maximum_fusion.16), channel_id=1, source_target_pairs={{0,2},{1,3},{2,0},{3,1},{4,6},{5,7},{6,4},{7,5},{8,10},{9,11},{10,... | collective-permute-start | bytes 1179656 | tf_op jit(solution)/shard_map/ppermute | solution.py:19
  36.9 9.0 %collective-permute-start.4 = (bf16[2,16,128]{2,1,0:T(8,128)(2,1)S(1)}, bf16[2,16,128]{2,1,0:T(8,128)(2,1)S(1)}, u32[]{:S(2)}, u32[]{:S(2)}) collective-permute-start(bf16[2,16,128]{2,1,0:T(8,128)(2,1)S(1)} %pad_maximum_fusion.22), channel_id=1, source_target_pairs={{0,2},{1,3},{2,0},{3,1},{4,6},{5,7},{6,4},{7,5},{8,10},{9,11},{10,... | collective-permute-start | bytes 24584 | tf_op jit(solution)/shard_map/ppermute | solution.py:19
  42.9 19.1 %collective-permute-start.3 = (bf16[1,128,1536]{2,1,0:T(8,128)(2,1)}, bf16[1,128,1536]{2,1,0:T(8,128)(2,1)S(1)}, u32[]{:S(2)}, u32[]{:S(2)}) collective-permute-start(bf16[1,128,1536]{2,1,0:T(8,128)(2,1)} %pad_maximum_fusion.15), channel_id=1, source_target_pairs={{0,4},{1,5},{2,6},{3,7},{4,0},{5,1},{6,2},{7,3},{8,12},{9,13},{10,... | collective-permute-start | bytes 1179656 | tf_op jit(solution)/shard_map/ppermute | solution.py:19
  46.0 16.9 %collective-permute-start.7 = (bf16[4,16,128]{2,1,0:T(8,128)(2,1)S(1)}, bf16[4,16,128]{2,1,0:T(8,128)(2,1)S(1)}, u32[]{:S(2)}, u32[]{:S(2)}) collective-permute-start(bf16[4,16,128]{2,1,0:T(8,128)(2,1)S(1)} %pad_maximum_fusion.18), channel_id=1, source_target_pairs={{0,1},{1,0},{2,3},{3,2},{4,5},{5,4},{6,7},{7,6},{8,9},{9,8},{10,11... | collective-permute-start | bytes 49160 | tf_op jit(solution)/shard_map/ppermute | solution.py:19
  47.6 18.5 %collective-permute-start.6 = (bf16[4,128,768]{2,1,0:T(8,128)(2,1)}, bf16[4,128,768]{2,1,0:T(8,128)(2,1)}, u32[]{:S(2)}, u32[]{:S(2)}) collective-permute-start(bf16[4,128,768]{2,1,0:T(8,128)(2,1)} %pad_maximum_fusion.8), channel_id=1, source_target_pairs={{0,1},{1,0},{2,3},{3,2},{4,5},{5,4},{6,7},{7,6},{8,9},{9,8},{10,11... | collective-permute-start | bytes 2359304 | tf_op jit(solution)/shard_map/ppermute | solution.py:19
  67.6 7.9 %collective-permute-start.8 = (bf16[8,128,768]{2,1,0:T(8,128)(2,1)S(1)}, bf16[8,128,768]{2,1,0:T(8,128)(2,1)S(1)}, u32[]{:S(2)}, u32[]{:S(2)}) collective-permute-start(bf16[8,128,768]{2,1,0:T(8,128)(2,1)S(1)} %pad_maximum_fusion.4.refs_0_.refs_4_), channel_id=1, source_target_pairs={{0,8},{8,0},{16,24},{24,16},{1,9},{9,1},{17,25},{25,17},{2,10},{10... | collective-permute-start | bytes 4718600 | tf_op jit(solution)/shard_map/ppermute | solution.py:19
  67.7 36.9 %collective-permute-start.13 = (bf16[8,128,768]{2,1,0:T(8,128)(2,1)S(1)}, bf16[8,128,768]{2,1,0:T(8,128)(2,1)}, u32[]{:S(2)}, u32[]{:S(2)}) collective-permute-start(bf16[8,128,768]{2,1,0:T(8,128)(2,1)S(1)} %pad_maximum_fusion.4.refs_0_.refs_4_), channel_id=1, source_target_pairs={{0,16},{8,24},{16,0},{24,8},{1,17},{9,25},{17,1},{25,9},{2,18},{10... | collective-permute-start | bytes 4718600 | tf_op jit(solution)/shard_map/ppermute | solution.py:19
  69.0 25.8 %collective-permute-start.5 = (bf16[2,128,1536]{2,1,0:T(8,128)(2,1)}, bf16[2,128,1536]{2,1,0:T(8,128)(2,1)}, u32[]{:S(2)}, u32[]{:S(2)}) collective-permute-start(bf16[2,128,1536]{2,1,0:T(8,128)(2,1)} %pad_maximum_fusion.9), channel_id=1, source_target_pairs={{0,2},{1,3},{2,0},{3,1},{4,6},{5,7},{6,4},{7,5},{8,10},{9,11},{10,... | collective-permute-start | bytes 2359304 | tf_op jit(solution)/shard_map/ppermute | solution.py:19
  72.5 23.9 %collective-permute-start.10 = (bf16[1,128,1024]{2,1,0:T(8,128)(2,1)S(1)}, bf16[1,128,1024]{2,1,0:T(8,128)(2,1)S(1)}, u32[]{:S(2)}, u32[]{:S(2)}) collective-permute-start(bf16[1,128,1024]{2,1,0:T(8,128)(2,1)S(1)} %copy-done.29), channel_id=1, source_target_pairs={{0,4},{1,5},{2,6},{3,7},{4,0},{5,1},{6,2},{7,3},{8,12},{9,13},{10,... | collective-permute-start | bytes 786440 | tf_op jit(solution)/shard_map/ppermute | solution.py:19
  104.6 39.9 %collective-permute-start.9 = (bf16[4,128,1536]{2,1,0:T(8,128)(2,1)S(1)}, bf16[4,128,1536]{2,1,0:T(8,128)(2,1)S(1)}, u32[]{:S(2)}, u32[]{:S(2)}) collective-permute-start(bf16[4,128,1536]{2,1,0:T(8,128)(2,1)S(1)} %pad_maximum_fusion.5), channel_id=1, source_target_pairs={{0,1},{1,0},{2,3},{3,2},{4,5},{5,4},{6,7},{7,6},{8,9},{9,8},{10,11... | collective-permute-start | bytes 4718600 | tf_op jit(solution)/shard_map/ppermute | solution.py:19
  105.9 19.7 %collective-permute-start.12 = (bf16[2,128,1024]{2,1,0:T(8,128)(2,1)S(1)}, bf16[2,128,1024]{2,1,0:T(8,128)(2,1)S(1)}, u32[]{:S(2)}, u32[]{:S(2)}) collective-permute-start(bf16[2,128,1024]{2,1,0:T(8,128)(2,1)S(1)} %pad_maximum_fusion.10), channel_id=1, source_target_pairs={{0,2},{1,3},{2,0},{3,1},{4,6},{5,7},{6,4},{7,5},{8,10},{9,11},{10,... | collective-permute-start | bytes 1572872 | tf_op jit(solution)/shard_map/ppermute | solution.py:19
  106.6 19.0 %collective-permute-start.11 = (bf16[1,128,1024]{2,1,0:T(8,128)(2,1)S(1)}, bf16[1,128,1024]{2,1,0:T(8,128)(2,1)S(1)}, u32[]{:S(2)}, u32[]{:S(2)}) collective-permute-start(bf16[1,128,1024]{2,1,0:T(8,128)(2,1)S(1)} %copy-done.28), channel_id=1, source_target_pairs={{0,4},{1,5},{2,6},{3,7},{4,0},{5,1},{6,2},{7,3},{8,12},{9,13},{10,... | collective-permute-start | bytes 786440 | tf_op jit(solution)/shard_map/ppermute | solution.py:19
  145.0 25.6 %collective-permute-start.16 = (bf16[4,128,1024]{2,1,0:T(8,128)(2,1)S(1)}, bf16[4,128,1024]{2,1,0:T(8,128)(2,1)S(1)}, u32[]{:S(2)}, u32[]{:S(2)}) collective-permute-start(bf16[4,128,1024]{2,1,0:T(8,128)(2,1)S(1)} %pad_maximum_fusion.6), channel_id=1, source_target_pairs={{0,1},{1,0},{2,3},{3,2},{4,5},{5,4},{6,7},{7,6},{8,9},{9,8},{10,11... | collective-permute-start | bytes 3145736 | tf_op jit(solution)/shard_map/ppermute | solution.py:19
  170.7 18.6 %collective-permute-start.18 = (bf16[8,128,1024]{2,1,0:T(8,128)(2,1)S(1)}, bf16[8,128,1024]{2,1,0:T(8,128)(2,1)}, u32[]{:S(2)}, u32[]{:S(2)}) collective-permute-start(bf16[8,128,1024]{2,1,0:T(8,128)(2,1)S(1)} %pad_maximum_fusion.2.refs_2_), channel_id=1, source_target_pairs={{0,8},{8,0},{16,24},{24,16},{1,9},{9,1},{17,25},{25,17},{2,10},{10... | collective-permute-start | bytes 6291464 | tf_op jit(solution)/shard_map/ppermute | solution.py:19
  170.8 56.8 %collective-permute-start.15 = (bf16[8,128,1024]{2,1,0:T(8,128)(2,1)}, bf16[8,128,1024]{2,1,0:T(8,128)(2,1)}, u32[]{:S(2)}, u32[]{:S(2)}) collective-permute-start(bf16[8,128,1024]{2,1,0:T(8,128)(2,1)} %slice.392), channel_id=1, source_target_pairs={{0,16},{8,24},{16,0},{24,8},{1,17},{9,25},{17,1},{25,9},{2,18},{10... | collective-permute-start | bytes 6291464 | tf_op jit(solution)/shard_map/ppermute | solution.py:19
  172.4 14.4 %collective-permute-start.19 = (bf16[2,128,1024]{2,1,0:T(8,128)(2,1)S(1)}, bf16[2,128,1024]{2,1,0:T(8,128)(2,1)S(1)}, u32[]{:S(2)}, u32[]{:S(2)}) collective-permute-start(bf16[2,128,1024]{2,1,0:T(8,128)(2,1)S(1)} %copy-done.22), channel_id=1, source_target_pairs={{0,2},{1,3},{2,0},{3,1},{4,6},{5,7},{6,4},{7,5},{8,10},{9,11},{10,... | collective-permute-start | bytes 1572872 | tf_op jit(solution)/shard_map/ppermute | solution.py:19
  186.9 40.7 %collective-permute-start.21 = (bf16[4,128,1024]{2,1,0:T(8,128)(2,1)S(1)}, bf16[4,128,1024]{2,1,0:T(8,128)(2,1)}, u32[]{:S(2)}, u32[]{:S(2)}) collective-permute-start(bf16[4,128,1024]{2,1,0:T(8,128)(2,1)S(1)} %pad_maximum_fusion.7), channel_id=1, source_target_pairs={{0,1},{1,0},{2,3},{3,2},{4,5},{5,4},{6,7},{7,6},{8,9},{9,8},{10,11... | collective-permute-start | bytes 3145736 | tf_op jit(solution)/shard_map/ppermute | solution.py:19
  229.2 13.0 %collective-permute-start.20 = (bf16[8,128,1024]{2,1,0:T(8,128)(2,1)}, bf16[8,128,1024]{2,1,0:T(8,128)(2,1)S(1)}, u32[]{:S(2)}, u32[]{:S(2)}) collective-permute-start(bf16[8,128,1024]{2,1,0:T(8,128)(2,1)} %collective-permute-done.15.refs_4_), channel_id=1, source_target_pairs={{0,8},{8,0},{16,24},{24,16},{1,9},{9,1},{17,25},{25,17},{2,10},{10... | collective-permute-start | bytes 6291464 | tf_op jit(solution)/shard_map/ppermute | solution.py:19
  229.7 12.6 %collective-permute-start.23 = (bf16[8,128,1024]{2,1,0:T(8,128)(2,1)S(1)}, bf16[8,128,1024]{2,1,0:T(8,128)(2,1)S(1)}, u32[]{:S(2)}, u32[]{:S(2)}) collective-permute-start(bf16[8,128,1024]{2,1,0:T(8,128)(2,1)S(1)} %copy-done.52), channel_id=1, source_target_pairs={{0,8},{8,0},{16,24},{24,16},{1,9},{9,1},{17,25},{25,17},{2,10},{10... | collective-permute-start | bytes 6291464 | tf_op jit(solution)/shard_map/ppermute | solution.py:19
  230.1 12.4 %collective-permute-start.24 = (bf16[8,128,1024]{2,1,0:T(8,128)(2,1)S(1)}, bf16[8,128,1024]{2,1,0:T(8,128)(2,1)}, u32[]{:S(2)}, u32[]{:S(2)}) collective-permute-start(bf16[8,128,1024]{2,1,0:T(8,128)(2,1)S(1)} %copy-done.51), channel_id=1, source_target_pairs={{0,8},{8,0},{16,24},{24,16},{1,9},{9,1},{17,25},{25,17},{2,10},{10... | collective-permute-start | bytes 6291464 | tf_op jit(solution)/shard_map/ppermute | solution.py:19
  292.0 58.9 %collective-permute-start.28 = (bf16[8,128,1024]{2,1,0:T(8,128)(2,1)S(1)}, bf16[8,128,1024]{2,1,0:T(8,128)(2,1)}, u32[]{:S(2)}, u32[]{:S(2)}) collective-permute-start(bf16[8,128,1024]{2,1,0:T(8,128)(2,1)S(1)} %add_convert_fusion), channel_id=1, source_target_pairs={{0,16},{8,24},{16,0},{24,8},{1,17},{9,25},{17,1},{25,9},{2,18},{10... | collective-permute-start | bytes 6291464 | tf_op jit(solution)/shard_map/ppermute | solution.py:19
  292.6 29.2 %collective-permute-start.25 = (bf16[4,128,1024]{2,1,0:T(8,128)(2,1)}, bf16[4,128,1024]{2,1,0:T(8,128)(2,1)}, u32[]{:S(2)}, u32[]{:S(2)}) collective-permute-start(bf16[4,128,1024]{2,1,0:T(8,128)(2,1)} %get-tuple-element.402), channel_id=1, source_target_pairs={{0,1},{1,0},{2,3},{3,2},{4,5},{5,4},{6,7},{7,6},{8,9},{9,8},{10,11... | collective-permute-start | bytes 3145736 | tf_op jit(solution)/shard_map/ppermute | solution.py:19
  296.2 54.7 %collective-permute-start.29 = (bf16[4,128,1024]{2,1,0:T(8,128)(2,1)}, bf16[4,128,1024]{2,1,0:T(8,128)(2,1)S(1)}, u32[]{:S(2)}, u32[]{:S(2)}) collective-permute-start(bf16[4,128,1024]{2,1,0:T(8,128)(2,1)} %get-tuple-element.433), channel_id=1, source_target_pairs={{0,1},{1,0},{2,3},{3,2},{4,5},{5,4},{6,7},{7,6},{8,9},{9,8},{10,11... | collective-permute-start | bytes 3145736 | tf_op jit(solution)/shard_map/ppermute | solution.py:19
  324.2 26.6 %collective-permute-start.30 = (bf16[2,128,1024]{2,1,0:T(8,128)(2,1)}, bf16[2,128,1024]{2,1,0:T(8,128)(2,1)S(1)}, u32[]{:S(2)}, u32[]{:S(2)}) collective-permute-start(bf16[2,128,1024]{2,1,0:T(8,128)(2,1)} %get-tuple-element.434), channel_id=1, source_target_pairs={{0,2},{1,3},{2,0},{3,1},{4,6},{5,7},{6,4},{7,5},{8,10},{9,11},{10,... | collective-permute-start | bytes 1572872 | tf_op jit(solution)/shard_map/ppermute | solution.py:19
  350.9 7.6 %collective-permute-start.31 = (bf16[8,128,1024]{2,1,0:T(8,128)(2,1)}, bf16[8,128,1024]{2,1,0:T(8,128)(2,1)S(1)}, u32[]{:S(2)}, u32[]{:S(2)}) collective-permute-start(bf16[8,128,1024]{2,1,0:T(8,128)(2,1)} %get-tuple-element.439), channel_id=1, source_target_pairs={{0,8},{8,0},{16,24},{24,16},{1,9},{9,1},{17,25},{25,17},{2,10},{10... | collective-permute-start | bytes 6291464 | tf_op jit(solution)/shard_map/ppermute | solution.py:19
  357.8 30.2 %collective-permute-start.33 = (bf16[4,128,1024]{2,1,0:T(8,128)(2,1)S(1)}, bf16[4,128,1024]{2,1,0:T(8,128)(2,1)}, u32[]{:S(2)}, u32[]{:S(2)}) collective-permute-start(bf16[4,128,1024]{2,1,0:T(8,128)(2,1)S(1)} %get-tuple-element.462), channel_id=1, source_target_pairs={{0,1},{1,0},{2,3},{3,2},{4,5},{5,4},{6,7},{7,6},{8,9},{9,8},{10,11... | collective-permute-start | bytes 3145736 | tf_op jit(solution)/shard_map/ppermute | solution.py:19
  359.6 46.0 %collective-permute-start.32 = (bf16[4,128,1024]{2,1,0:T(8,128)(2,1)S(1)}, bf16[4,128,1024]{2,1,0:T(8,128)(2,1)}, u32[]{:S(2)}, u32[]{:S(2)}) collective-permute-start(bf16[4,128,1024]{2,1,0:T(8,128)(2,1)S(1)} %get-tuple-element.461), channel_id=1, source_target_pairs={{0,1},{1,0},{2,3},{3,2},{4,5},{5,4},{6,7},{7,6},{8,9},{9,8},{10,11... | collective-permute-start | bytes 3145736 | tf_op jit(solution)/shard_map/ppermute | solution.py:19
  361.0 27.0 %collective-permute-start.34 = (bf16[2,128,1024]{2,1,0:T(8,128)(2,1)S(1)}, bf16[2,128,1024]{2,1,0:T(8,128)(2,1)S(1)}, u32[]{:S(2)}, u32[]{:S(2)}) collective-permute-start(bf16[2,128,1024]{2,1,0:T(8,128)(2,1)S(1)} %get-tuple-element.463), channel_id=1, source_target_pairs={{0,2},{1,3},{2,0},{3,1},{4,6},{5,7},{6,4},{7,5},{8,10},{9,11},{10,... | collective-permute-start | bytes 1572872 | tf_op jit(solution)/shard_map/ppermute | solution.py:19
  361.3 26.7 %collective-permute-start.35 = (bf16[1,128,1024]{2,1,0:T(8,128)(2,1)}, bf16[1,128,1024]{2,1,0:T(8,128)(2,1)S(1)}, u32[]{:S(2)}, u32[]{:S(2)}) collective-permute-start(bf16[1,128,1024]{2,1,0:T(8,128)(2,1)} %add_convert_fusion.36), channel_id=1, source_target_pairs={{0,4},{1,5},{2,6},{3,7},{4,0},{5,1},{6,2},{7,3},{8,12},{9,13},{10,... | collective-permute-start | bytes 786440 | tf_op jit(solution)/shard_map/ppermute | solution.py:19
  405.6 12.3 %collective-permute-start.36 = (bf16[8,128,1024]{2,1,0:T(8,128)(2,1)}, bf16[8,128,1024]{2,1,0:T(8,128)(2,1)}, u32[]{:S(2)}, u32[]{:S(2)}) collective-permute-start(bf16[8,128,1024]{2,1,0:T(8,128)(2,1)} %get-tuple-element.470), channel_id=1, source_target_pairs={{0,8},{8,0},{16,24},{24,16},{1,9},{9,1},{17,25},{25,17},{2,10},{10... | collective-permute-start | bytes 6291464 | tf_op jit(solution)/shard_map/ppermute | solution.py:19
  414.1 40.5 %collective-permute-start.40 = (bf16[1,128,1024]{2,1,0:T(8,128)(2,1)}, bf16[1,128,1024]{2,1,0:T(8,128)(2,1)S(1)}, u32[]{:S(2)}, u32[]{:S(2)}) collective-permute-start(bf16[1,128,1024]{2,1,0:T(8,128)(2,1)} %add_convert_fusion.35), channel_id=1, source_target_pairs={{0,4},{1,5},{2,6},{3,7},{4,0},{5,1},{6,2},{7,3},{8,12},{9,13},{10,... | collective-permute-start | bytes 786440 | tf_op jit(solution)/shard_map/ppermute | solution.py:19
  415.9 38.6 %collective-permute-start.39 = (bf16[2,128,1024]{2,1,0:T(8,128)(2,1)}, bf16[2,128,1024]{2,1,0:T(8,128)(2,1)}, u32[]{:S(2)}, u32[]{:S(2)}) collective-permute-start(bf16[2,128,1024]{2,1,0:T(8,128)(2,1)} %get-tuple-element.495), channel_id=1, source_target_pairs={{0,2},{1,3},{2,0},{3,1},{4,6},{5,7},{6,4},{7,5},{8,10},{9,11},{10,... | collective-permute-start | bytes 1572872 | tf_op jit(solution)/shard_map/ppermute | solution.py:19
  416.2 38.4 %collective-permute-start.41 = (bf16[2,128,1024]{2,1,0:T(8,128)(2,1)}, bf16[2,128,1024]{2,1,0:T(8,128)(2,1)S(1)}, u32[]{:S(2)}, u32[]{:S(2)}) collective-permute-start(bf16[2,128,1024]{2,1,0:T(8,128)(2,1)} %get-tuple-element.500), channel_id=1, source_target_pairs={{0,2},{1,3},{2,0},{3,1},{4,6},{5,7},{6,4},{7,5},{8,10},{9,11},{10,... | collective-permute-start | bytes 1572872 | tf_op jit(solution)/shard_map/ppermute | solution.py:19
  421.4 30.5 %collective-permute-start.37 = (bf16[4,128,1024]{2,1,0:T(8,128)(2,1)}, bf16[4,128,1024]{2,1,0:T(8,128)(2,1)}, u32[]{:S(2)}, u32[]{:S(2)}) collective-permute-start(bf16[4,128,1024]{2,1,0:T(8,128)(2,1)} %get-tuple-element.490), channel_id=1, source_target_pairs={{0,1},{1,0},{2,3},{3,2},{4,5},{5,4},{6,7},{7,6},{8,9},{9,8},{10,11... | collective-permute-start | bytes 3145736 | tf_op jit(solution)/shard_map/ppermute | solution.py:19
  467.6 8.3 %collective-permute-start.51 = (f32[2,16,128]{2,1,0:T(8,128)}, f32[2,16,128]{2,1,0:T(8,128)S(1)}, u32[]{:S(2)}, u32[]{:S(2)}) collective-permute-start(f32[2,16,128]{2,1,0:T(8,128)} %slice.569), channel_id=1, source_target_pairs={{0,2},{1,3},{2,0},{3,1},{4,6},{5,7},{6,4},{7,5},{8,10},{9,11},{10,... | collective-permute-start | bytes 49160 | tf_op jit(solution)/shard_map/ppermute | solution.py:19
  474.8 14.3 %collective-permute-start.42 = (bf16[1,128,1024]{2,1,0:T(8,128)(2,1)}, bf16[1,128,1024]{2,1,0:T(8,128)(2,1)S(1)}, u32[]{:S(2)}, u32[]{:S(2)}) collective-permute-start(bf16[1,128,1024]{2,1,0:T(8,128)(2,1)} %add_convert_fusion.34), channel_id=1, source_target_pairs={{0,4},{1,5},{2,6},{3,7},{4,0},{5,1},{6,2},{7,3},{8,12},{9,13},{10,... | collective-permute-start | bytes 786440 | tf_op jit(solution)/shard_map/ppermute | solution.py:19
  476.6 12.5 %collective-permute-start.52 = (f32[1,16,128]{2,1,0:T(8,128)S(1)}, f32[1,16,128]{2,1,0:T(8,128)S(1)}, u32[]{:S(2)}, u32[]{:S(2)}) collective-permute-start(f32[1,16,128]{2,1,0:T(8,128)S(1)} %slice.571), channel_id=1, source_target_pairs={{0,4},{1,5},{2,6},{3,7},{4,0},{5,1},{6,2},{7,3},{8,12},{9,13},{10,... | collective-permute-start | bytes 24584 | tf_op jit(solution)/shard_map/ppermute | solution.py:19
  479.6 11.4 %collective-permute-start.55 = (bf16[128,1024]{1,0:T(8,128)(2,1)S(1)}, bf16[128,1024]{1,0:T(8,128)(2,1)S(1)}, u32[]{:S(2)}, u32[]{:S(2)}) collective-permute-start(bf16[128,1024]{1,0:T(8,128)(2,1)S(1)} %fusion.5), channel_id=1, source_target_pairs={{0,16},{8,24},{16,0},{24,8},{1,17},{9,25},{17,1},{25,9},{2,18},{10... | collective-permute-start | bytes 786440 | tf_op jit(solution)/shard_map/ppermute | solution.py:19
  481.1 20.5 %collective-permute-start.38 = (bf16[2,128,1024]{2,1,0:T(8,128)(2,1)}, bf16[2,128,1024]{2,1,0:T(8,128)(2,1)S(1)}, u32[]{:S(2)}, u32[]{:S(2)}) collective-permute-start(bf16[2,128,1024]{2,1,0:T(8,128)(2,1)} %get-tuple-element.494), channel_id=1, source_target_pairs={{0,2},{1,3},{2,0},{3,1},{4,6},{5,7},{6,4},{7,5},{8,10},{9,11},{10,... | collective-permute-start | bytes 1572872 | tf_op jit(solution)/shard_map/ppermute | solution.py:19
  482.9 18.8 %collective-permute-start.46 = (bf16[1,128,1024]{2,1,0:T(8,128)(2,1)}, bf16[1,128,1024]{2,1,0:T(8,128)(2,1)S(1)}, u32[]{:S(2)}, u32[]{:S(2)}) collective-permute-start(bf16[1,128,1024]{2,1,0:T(8,128)(2,1)} %add_convert_fusion.33), channel_id=1, source_target_pairs={{0,4},{1,5},{2,6},{3,7},{4,0},{5,1},{6,2},{7,3},{8,12},{9,13},{10,... | collective-permute-start | bytes 786440 | tf_op jit(solution)/shard_map/ppermute | solution.py:19
  491.1 14.2 %collective-permute-start.56 = (bf16[128,1024]{1,0:T(8,128)(2,1)S(1)}, bf16[128,1024]{1,0:T(8,128)(2,1)S(1)}, u32[]{:S(2)}, u32[]{:S(2)}) collective-permute-start(bf16[128,1024]{1,0:T(8,128)(2,1)S(1)} %fusion), channel_id=1, source_target_pairs={{0,8},{8,0},{16,24},{24,16},{1,9},{9,1},{17,25},{25,17},{2,10},{10... | collective-permute-start | bytes 786440 | tf_op jit(solution)/shard_map/ppermute | solution.py:19
  491.9 24.2 %collective-permute-start.54 = (bf16[2,128,1024]{2,1,0:T(8,128)(2,1)S(1)}, bf16[2,128,1024]{2,1,0:T(8,128)(2,1)}, u32[]{:S(2)}, u32[]{:S(2)}) collective-permute-start(bf16[2,128,1024]{2,1,0:T(8,128)(2,1)S(1)} %pad_maximum_fusion.13), channel_id=1, source_target_pairs={{0,16},{8,24},{16,0},{24,8},{1,17},{9,25},{17,1},{25,9},{2,18},{10... | collective-permute-start | bytes 1572872 | tf_op jit(solution)/shard_map/ppermute | solution.py:19
  502.6 13.4 %collective-permute-start.47 = (bf16[128,1024]{1,0:T(8,128)(2,1)}, bf16[128,1024]{1,0:T(8,128)(2,1)S(1)}, u32[]{:S(2)}, u32[]{:S(2)}) collective-permute-start(bf16[128,1024]{1,0:T(8,128)(2,1)} %fusion.2), channel_id=1, source_target_pairs={{0,16},{8,24},{16,0},{24,8},{1,17},{9,25},{17,1},{25,9},{2,18},{10... | collective-permute-start | bytes 786440 | tf_op jit(solution)/shard_map/ppermute | solution.py:19
  503.5 12.4 %collective-permute-start.45 = (bf16[1,128,1024]{2,1,0:T(8,128)(2,1)S(1)}, bf16[1,128,1024]{2,1,0:T(8,128)(2,1)S(1)}, u32[]{:S(2)}, u32[]{:S(2)}) collective-permute-start(bf16[1,128,1024]{2,1,0:T(8,128)(2,1)S(1)} %add_convert_fusion.32), channel_id=1, source_target_pairs={{0,4},{1,5},{2,6},{3,7},{4,0},{5,1},{6,2},{7,3},{8,12},{9,13},{10,... | collective-permute-start | bytes 786440 | tf_op jit(solution)/shard_map/ppermute | solution.py:19
  506.2 17.6 %collective-permute-start.57 = (bf16[2,128,1024]{2,1,0:T(8,128)(2,1)}, bf16[2,128,1024]{2,1,0:T(8,128)(2,1)}, u32[]{:S(2)}, u32[]{:S(2)}) collective-permute-start(bf16[2,128,1024]{2,1,0:T(8,128)(2,1)} %pad_maximum_fusion.14), channel_id=1, source_target_pairs={{0,16},{8,24},{16,0},{24,8},{1,17},{9,25},{17,1},{25,9},{2,18},{10... | collective-permute-start | bytes 1572872 | tf_op jit(solution)/shard_map/ppermute | solution.py:19
  518.6 15.6 %collective-permute-start.49 = (bf16[2,128,1024]{2,1,0:T(8,128)(2,1)}, bf16[2,128,1024]{2,1,0:T(8,128)(2,1)}, u32[]{:S(2)}, u32[]{:S(2)}) collective-permute-start(bf16[2,128,1024]{2,1,0:T(8,128)(2,1)} %pad_maximum_fusion.12), channel_id=1, source_target_pairs={{0,16},{8,24},{16,0},{24,8},{1,17},{9,25},{17,1},{25,9},{2,18},{10... | collective-permute-start | bytes 1572872 | tf_op jit(solution)/shard_map/ppermute | solution.py:19
  (72 other events, 1339.4 us)

commit v4 on v2

v4 whole, which is shorter than its diff:
```python
import math

import jax
import jax.numpy as jnp
from jax import lax
from jax.experimental import pallas as pl
from jax.experimental.pallas import tpu as pltpu
from jax.sharding import PartitionSpec as P

HEADS = 16
GRID = 14
NSCALE = 16
norm_eps = 1e-06
half = jnp.bfloat16
full = jnp.float32


def xor_swap(value, axis, size, mask):
    return lax.ppermute(value, axis, [(i, i ^ mask) for i in range(size)])


def core_swap(value):
    return xor_swap(value, "dp", 4, 1)


def x_swap(value):
    return xor_swap(value, "dp", 4, 2)


def masks(bits):
    found = [0]
    for bit in bits:
        found = found + [m | (1 << bit) for m in found]
    return found


class Order:
    def __init__(self, value):
        self.value = value

    def at(self, value):
        value, self.value = lax.optimization_barrier((value, self.value))
        return value

    def land(self, value, *sent):
        value, flights = self.at((value, [s.flight for s in sent]))
        for s, flight in zip(sent, flights, strict=True):
            s.accept(flight)
        return value


class Sent:
    def __init__(self, flight):
        self.flight = flight

    def accept(self, value):
        self.value = value


class Gather:
    def __init__(self, seq, piece, n, bits):
        self.seq, self.held, self.n, self.bits = seq, piece[None], n, list(bits)

    def launch(self):
        self.held = self.seq.at(self.held)
        self.flight = xor_swap(self.held, "fsdp", self.n, 1 << self.bits.pop(0))

    def accept(self, value):
        self.got = value

    def join(self):
        self.held = jnp.concatenate([self.held, self.got])
        return self.held


def rounded_sum(terms, kind=half):
    return sum(t.astype(full) for t in terms).astype(kind)


class Reduce:
    def __init__(self, seq, terms, n, kind=half):
        self.kind = kind
        self.seq, self.n, self.axes = seq, n, list(range(n.bit_length() - 1))
        self.terms = [t.reshape((2,) * len(self.axes) + t.shape[1:]) for t in terms]

    def launch(self, bit=None, more=()):
        bit = self.axes[0] if bit is None else bit
        axis = self.axes.index(bit)
        self.axes.pop(axis)
        low, high = [
            [lax.index_in_dim(t, side, axis, keepdims=False) for t in self.terms] for side in (0, 1)
        ]
        self.terms = low
        self.flight = xor_swap(self.seq.at(rounded_sum([*high, *more], self.kind)), "fsdp", self.n, 1 << bit)

    def accept(self, value):
        self.terms = [*self.terms, value]

    def rest(self):
        while self.axes:
            self.launch()
            self.seq.land((), self)
        return self

    def piece(self):
        return rounded_sum(self.terms, self.kind)


class Spread:
    def __init__(self, seq, piece):
        self.seq, self.own = seq, seq.at(piece)
        self.flight = core_swap(self.own)

    def cross(self):
        self.pair = jnp.stack([self.own, self.got])
        self.flight = x_swap(self.seq.at(self.pair))

    def accept(self, value):
        self.got = value


ANYWHERE = pl.BlockSpec(memory_space=pl.ANY)
ON_CHIP = pl.BlockSpec(memory_space=pltpu.VMEM)
SCALARS = pl.BlockSpec(memory_space=pltpu.SMEM)


def dot(left, right, dim_left, dim_right):
    return lax.dot_general(
        left, right, (((dim_left,), (dim_right,)), ((), ())), preferred_element_type=full
    )


def call(kernel, name, operands, in_specs, outs, out_specs, scratch):
    return pl.pallas_call(
        kernel,
        out_shape=[jax.ShapeDtypeStruct(shape, kind) for shape, kind in outs],
        in_specs=in_specs,
        out_specs=out_specs,
        scratch_shapes=scratch,
        compiler_params=pltpu.CompilerParams(vmem_limit_bytes=58 * 2**20),
        name=name,
    )(*operands)


def loop(count, body, unroll=1):
    def step(i, carry):
        body(i)
        return carry

    lax.fori_loop(0, count, step, 0, unroll=unroll)


def tile(i, size):
    return pl.ds(pl.multiple_of(i * size, size), size)


def fetch(parts, order_ref, place, sem):
    base = 0
    for part in parts:

        def start(r, part=part, base=base):
            shard = r if order_ref is None else order_ref[base + r]
            pltpu.make_async_copy(part.at[r], place(shard), sem).start()

        loop(part.shape[0], start)
        base += part.shape[0]


def head_rows(s, q, n, rows, quarter):
    per = n // 4
    return pl.multiple_of(((s // per) ^ q) * quarter + (s % per) * rows, rows)


def pair_scores(q2, k2):
    first = lax.broadcasted_iota(jnp.int32, q2.shape, 1) < q2.shape[1] // 2
    both = apart(q2, first)
    return both, dot(k2, both, 1, 1), first


def apart(value, first):
    zero = jnp.zeros_like(value)
    return jnp.concatenate([jnp.where(first, value, zero), jnp.where(first, zero, value)])


def attention_forward(order, normed, bias, weights, n_img, patches, factor):
    groups, n_parts = len(weights), len(weights[0])
    wide = weights[0][0].shape[2]
    count, width = normed.shape
    rows = width // sum(part.shape[0] for part in weights[0])
    padded = count // n_img
    quarter = wide // 3

    def kernel(order_ref, normed_ref, bias_ref, *refs):
        w_refs, refs = refs[: groups * n_parts], refs[groups * n_parts :]
        qkv_refs, mixed_refs, refs = refs[:groups], refs[groups : 2 * groups], refs[2 * groups :]
        lse_refs, (w_held, sems) = refs[:groups], refs[groups:]
        for g in range(groups):
            fetch(
                [w.at[:, pl.ds(0, rows)] for w in w_refs[g * n_parts : (g + 1) * n_parts]],
                order_ref,
                lambda s, g=g: w_held.at[g, pl.ds(pl.multiple_of(s * rows, rows), rows)],
                sems.at[g],
            )
        for g in range(groups):
            pltpu.make_async_copy(w_held.at[g], w_held.at[g], sems.at[g]).wait()

            def project(t, g=g):
                at = tile(t, quarter)
                product = dot(normed_ref[...], w_held[g, :, at], 1, 0)
                qkv_refs[g][:, at] = (product + bias_ref[g, :, at]).astype(half)

            loop(3, project)

            def attend(i, g=g):
                at = tile(i // 2, padded)
                lanes = [pl.ds(pl.multiple_of(t * quarter + (i % 2) * 128, 128), 128) for t in range(3)]
                q2 = qkv_refs[g][at, lanes[0]] * factor
                k2 = qkv_refs[g][at, lanes[1]]
                v2 = qkv_refs[g][at, lanes[2]]
                _, scores, first = pair_scores(q2, k2)
                key = lax.broadcasted_iota(jnp.int32, scores.shape, 0)
                scores = jnp.where(key < patches, scores, -1e30)
                top = jnp.max(scores, axis=0, keepdims=True)
                raised = jnp.exp(scores - top)
                total = jnp.sum(raised, axis=0, keepdims=True)
                lse_refs[g][i] = top + jnp.log(total)
                out = dot((raised * (1.0 / total)).astype(half), v2, 0, 0)
                mixed_refs[g][at, lanes[0]] = jnp.where(first, out[:padded], out[padded:]).astype(half)

            loop(2 * n_img, attend, 2 * n_img)

    return call(
        kernel,
        "attention_forward",
        (order, normed, bias, *(part for w in weights for part in w)),
        [SCALARS, ON_CHIP, ON_CHIP] + [ANYWHERE] * (groups * n_parts),
        [((count, wide), half)] * groups
        + [((count, quarter), half)] * groups
        + [((2 * n_img, 1, 2 * padded), full)] * groups,
        [ON_CHIP] * (3 * groups),
        [pltpu.VMEM((groups, width, wide), half), pltpu.SemaphoreType.DMA((groups,))],
    )


def layer_norm(value, gain, shift):
    center = jnp.mean(value, axis=-1, keepdims=True)
    offset = value - center
    spread = jnp.mean(offset * offset, axis=-1, keepdims=True)
    return offset * lax.rsqrt(spread + norm_eps) * gain + shift


def layer_norm_back(value, grad, gain):
    center = jnp.mean(value, axis=-1, keepdims=True)
    offset = value - center
    scale = lax.rsqrt(jnp.mean(offset * offset, axis=-1, keepdims=True) + norm_eps)
    unit = offset * scale
    scaled = grad * gain
    inner = jnp.mean(scaled * unit, axis=-1, keepdims=True)
    return scale * (scaled - jnp.mean(scaled, axis=-1, keepdims=True) - unit * inner), grad * unit


def load_out(order_ref, out_refs, held, sem, n, rows, quarter):
    q = order_ref[n]
    for j in range(4):
        column = pl.multiple_of((q ^ j) * quarter, quarter)
        fetch(
            [out_refs[j % 2].at[:, :, pl.ds(j // 2 * quarter, quarter)]],
            order_ref,
            lambda s, column=column: held.at[
                pl.ds(head_rows(s, q, n, rows, quarter), rows), pl.ds(column, quarter)
            ],
            sem,
        )


CHUNK = 16
ROWS = 64


def attention_out(order, x_zero, mixed, outs, bias, gain, shift):
    count, width = x_zero.shape
    n, rows, _ = outs[0].shape
    quarter = mixed[0].shape[1]

    def kernel(order_ref, x_ref, bias_ref, gain_ref, shift_ref, *refs):
        mixed_refs, out_refs = refs[:4], refs[4:6]
        after_ref, normed_ref, held, sems = refs[6:]
        load_out(order_ref, out_refs, held, sems.at[0], n, rows, quarter)
        together = jnp.concatenate([m[...] for m in mixed_refs], axis=1)
        pltpu.make_async_copy(held, held, sems.at[0]).wait()
        after_ref[...] = dot(together, held[...], 1, 0)

        def finish(i):
            at = tile(i, CHUNK)
            after = x_ref[at] + (after_ref[at] + bias_ref[...])
            after_ref[at] = after
            normed_ref[at] = layer_norm(after, gain_ref[...], shift_ref[...]).astype(half)

        loop(count // CHUNK, finish, 13)

    return call(
        kernel,
        "attention_out",
        (order, x_zero, bias, gain, shift, *mixed, *outs),
        [SCALARS] + [ON_CHIP] * 8 + [ANYWHERE] * 2,
        [((count, width), full), ((count, width), half)],
        [ON_CHIP] * 2,
        [pltpu.VMEM((width, width), half), pltpu.SemaphoreType.DMA((1,))],
    )


def mlp(order, normed, cot, bias, ups, downs, down_start, carried=None, ending=None):
    groups = len(ups)
    count, width = normed.shape
    n, rows, _ = ups[0].shape
    hidden = bias.shape[2]
    share = hidden // n
    step = min(512, hidden)
    steps = hidden // step
    more = [] if carried is None else [*carried, *ending]

    def kernel(order_ref, normed_ref, cot_ref, bias_ref, *refs):
        more_refs, refs = refs[: len(more)], refs[len(more) :]
        up_refs, down_refs, refs = refs[:groups], refs[groups : 2 * groups], refs[2 * groups :]
        g_up_refs, g_down_refs, refs = refs[:groups], refs[groups : 2 * groups], refs[2 * groups :]
        g_bias_ref, out_ref, back_ref, refs = refs[0], refs[1], refs[2], refs[3:]
        up, down, pre, act, act_half, pre_half, g_up, g_down, sems, out_sems = refs[-10:]
        for g in range(groups):
            fetch(
                [up_refs[g].at[:, :, pl.ds(0, hidden)]],
                None,
                lambda s, g=g: up.at[g, pl.ds(pl.multiple_of(s * rows, rows), rows)],
                sems.at[g],
            )
            fetch(
                [down_refs[g].at[:, :, pl.ds(down_start, width)]],
                None,
                lambda s, g=g: down.at[g, pl.ds(pl.multiple_of(s * share, share), share)],
                sems.at[groups + g],
            )
        if more:
            out_ref[...] = more_refs[0][...]
            back_ref[...] = more_refs[1][...]
        else:
            out_ref[...] = jnp.zeros_like(out_ref)
            back_ref[...] = jnp.zeros_like(back_ref)
        for g in range(groups):
            pltpu.make_async_copy(up.at[g], up.at[g], sems.at[g]).wait()
            pltpu.make_async_copy(down.at[g], down.at[g], sems.at[groups + g]).wait()

            def part(t, g=g):
                at = tile(t, step)
                pre[...] = dot(normed_ref[...], up[g, :, at], 1, 0)
                act[...] = dot(cot_ref[...], down[g, at, :], 1, 1)

                def gelu(i):
                    some = tile(i, 2 * CHUNK)
                    x = pre[some] + bias_ref[g, :, at]
                    below = 0.5 * (1.0 + lax.erf(x * math.sqrt(0.5)))
                    density = jnp.exp(-0.5 * x * x) * (1.0 / math.sqrt(2.0 * math.pi))
                    act_half[some] = (x * below).astype(half)
                    pre_half[some] = (act[some] * (below + x * density)).astype(half)

                loop(count // CHUNK // 2, gelu)
                h = act_half[...]
                p = pre_half[...]
                out_ref[...] += dot(h, down[g, at, :], 1, 0)
                back_ref[...] += dot(p, up[g, :, at], 1, 1)
                g_down[g, at, :] = dot(h, cot_ref[...], 0, 0).astype(half)
                g_up[g, :, at] = dot(normed_ref[...], p, 0, 0).astype(half)
                g_bias_ref[g, :, at] = jnp.sum(p.astype(full), axis=0, keepdims=True)

            loop(steps, part)

            def send(r, g=g):
                s = order_ref[r]
                pltpu.make_async_copy(
                    g_up.at[g, pl.ds(pl.multiple_of(s * rows, rows), rows)],
                    g_up_refs[g].at[r],
                    out_sems.at[g],
                ).start()
                pltpu.make_async_copy(
                    g_down.at[g, pl.ds(pl.multiple_of(s * share, share), share)],
                    g_down_refs[g].at[r],
                    out_sems.at[groups + g],
                ).start()

            loop(n, send)
        if more:
            after_ref, end_ref, block_ref = more_refs[2], more_refs[3], refs[0]

            def finish(i):
                at = tile(i, CHUNK)
                block_ref[at] = (after_ref[at] + (out_ref[at] + end_ref[...])).astype(half)

            loop(count // CHUNK, finish)
        for g in range(groups):
            pltpu.make_async_copy(g_up_refs[g], g_up_refs[g], out_sems.at[g]).wait()
            pltpu.make_async_copy(g_down_refs[g], g_down_refs[g], out_sems.at[groups + g]).wait()

    outs = (
        [((n, rows, hidden), half)] * groups
        + [((n, share, width), half)] * groups
        + [((groups, 1, hidden), full), ((count, width), full), ((count, width), full)]
        + ([((count, width), half)] if more else [])
    )
    return call(
        kernel,
        "mlp",
        (order, normed, cot, bias, *more, *ups, *downs),
        [SCALARS] + [ON_CHIP] * (3 + len(more)) + [ANYWHERE] * (2 * groups),
        outs,
        [ANYWHERE] * (2 * groups) + [ON_CHIP] * (len(outs) - 2 * groups),
        [
            pltpu.VMEM((groups, width, hidden), half),
            pltpu.VMEM((groups, hidden, width), half),
            pltpu.VMEM((count, step), full),
            pltpu.VMEM((count, step), full),
            pltpu.VMEM((count, step), half),
            pltpu.VMEM((count, step), half),
            pltpu.VMEM((groups, width, hidden), half),
            pltpu.VMEM((groups, hidden, width), half),
            pltpu.SemaphoreType.DMA((2 * groups,)),
            pltpu.SemaphoreType.DMA((2 * groups,)),
        ],
    )


def attention_out_back(order, grad, after, cot, gain, mixed, outs):
    count, width = after.shape
    n, rows, _ = outs[0].shape
    quarter = mixed[0].shape[1]

    def kernel(order_ref, grad_ref, after_ref, cot_ref, gain_ref, *refs):
        mixed_refs, out_refs, refs = refs[:4], refs[4:6], refs[6:]
        after_grad_ref, mixed_grad_refs, g_out_ref, sums_ref = refs[0], refs[1:5], refs[5], refs[6]
        held, branch, terms, sems = refs[7:]
        load_out(order_ref, out_refs, held, sems.at[0], n, rows, quarter)
        terms[...] = jnp.zeros_like(terms)

        def fold(value):
            return jnp.sum(value.reshape(CHUNK // 8, 8, width), axis=0)

        def back(i):
            at = tile(i, CHUNK)
            incoming = grad_ref[at]
            part, gain_terms = layer_norm_back(after_ref[at], incoming, gain_ref[...])
            own = cot_ref[at].astype(full)
            total = own + part
            after_grad_ref[at] = total
            rounded = total.astype(half)
            branch[at] = rounded
            terms[0] += fold(rounded.astype(full))
            terms[1] += fold(gain_terms)
            terms[2] += fold(incoming)
            terms[3] += fold(own)

        loop(count // CHUNK, back, 13)
        for k in range(4):
            sums_ref[k] = jnp.sum(terms[k], axis=0, keepdims=True)
        pltpu.make_async_copy(held, held, sems.at[0]).wait()
        for j in range(4):
            mixed_grad_refs[j][...] = dot(branch[...], held[j * quarter : (j + 1) * quarter], 1, 1).astype(half)
            g_out_ref[j * quarter : (j + 1) * quarter] = dot(mixed_refs[j][...], branch[...], 0, 0).astype(half)

    return call(
        kernel,
        "attention_out_back",
        (order, grad, after, cot, gain, *mixed, *outs),
        [SCALARS] + [ON_CHIP] * 8 + [ANYWHERE] * 2,
        [((count, width), full)]
        + [((count, quarter), half)] * 4
        + [((width, width), half), ((4, 1, width), full)],
        [ON_CHIP] * 7,
        [
            pltpu.VMEM((width, width), half),
            pltpu.VMEM((count, width), half),
            pltpu.VMEM((4, 8, width), full),
            pltpu.SemaphoreType.DMA((1,)),
        ],
    )


def attention_back(order, normed, qkvs, lses, mixed_grads, g_out, which, n_img, patches, factor, n):
    groups = len(qkvs)
    count, width = normed.shape
    wide = qkvs[0].shape[1]
    quarter = wide // 3
    padded = count // n_img
    rows = width // n

    def kernel(order_ref, normed_ref, g_out_ref, *refs):
        qkv_refs, mg_refs, refs = refs[:groups], refs[groups : 2 * groups], refs[2 * groups :]
        lse_refs, refs = refs[:groups], refs[groups:]
        g_w_refs, proj_refs, sums_ref = refs[:groups], refs[groups : 2 * groups], refs[2 * groups]
        g_w, sems = refs[2 * groups + 1 :]
        q = order_ref[n]
        for g in range(groups):

            def send_out(r, g=g):
                at = head_rows(order_ref[r], q, n, rows, quarter)
                column = pl.multiple_of((q ^ which[g]) * quarter, quarter)
                pltpu.make_async_copy(
                    g_out_ref.at[pl.ds(at, rows), pl.ds(column, quarter)],
                    g_w_refs[g].at[r, :, pl.ds(wide, quarter)],
                    sems.at[g],
                ).start()

            loop(n, send_out)

            def attend(i, g=g):
                at = tile(i // 2, padded)
                lanes = [pl.ds(pl.multiple_of(t * quarter + (i % 2) * 128, 128), 128) for t in range(3)]
                q2 = qkv_refs[g][at, lanes[0]] * factor
                k2 = qkv_refs[g][at, lanes[1]]
                v2 = qkv_refs[g][at, lanes[2]]
                both, scores, first = pair_scores(q2, k2)
                key = lax.broadcasted_iota(jnp.int32, scores.shape, 0)
                probs = jnp.where(key < patches, jnp.exp(scores - lse_refs[g][i]), 0.0)
                o_both = apart(mg_refs[g][at, lanes[0]], first)
                g_probs = dot(v2, o_both, 1, 1)
                weighted = jnp.sum(probs * g_probs, axis=0, keepdims=True)
                g_scores = (probs * (g_probs - weighted)).astype(half)
                g_query = dot(g_scores, k2, 0, 0)
                g_query = jnp.where(first, g_query[:padded], g_query[padded:]) * factor
                proj_refs[g][at, lanes[0]] = g_query.astype(half)
                proj_refs[g][at, lanes[1]] = dot(g_scores, both, 1, 0).astype(half)
                proj_refs[g][at, lanes[2]] = dot(probs.astype(half), o_both, 1, 0).astype(half)

            loop(2 * n_img, attend, 4)

            def weigh(t, g=g):
                at = tile(t, quarter)
                some = proj_refs[g][:, at]
                g_w[g, :, at] = dot(normed_ref[...], some, 0, 0).astype(half)
                sums_ref[g, :, at] = jnp.sum(some.astype(full), axis=0, keepdims=True)

            loop(3, weigh)

            def send(r, g=g):
                at = pl.multiple_of(order_ref[r] * rows, rows)
                pltpu.make_async_copy(
                    g_w.at[g, pl.ds(at, rows)], g_w_refs[g].at[r, :, pl.ds(0, wide)], sems.at[g]
                ).start()

            loop(n, send)
        for g in range(groups):
            pltpu.make_async_copy(g_w_refs[g], g_w_refs[g], sems.at[g]).wait()

    return call(
        kernel,
        "attention_back",
        (order, normed, g_out, *qkvs, *mixed_grads, *lses),
        [SCALARS] + [ON_CHIP] * (2 + 3 * groups),
        [((n, rows, wide + quarter), half)] * groups
        + [((count, wide), half)] * groups
        + [((groups, 1, wide), full)],
        [ANYWHERE] * groups + [ON_CHIP] * (groups + 1),
        [pltpu.VMEM((groups, width, wide), half), pltpu.SemaphoreType.DMA((groups,))],
    )


def input_back(order, x_zero, after_grad, gain, projs, weights):
    count, width = x_zero.shape
    wide = weights[0][0].shape[2]
    rows = width // sum(part.shape[0] for part in weights[0])
    parts = [part for w in weights for part in w]
    n_parts = len(weights[0])

    def kernel(order_ref, x_ref, after_ref, gain_ref, *refs):
        proj_refs, w_refs = refs[:4], refs[4 : 4 + len(parts)]
        token_ref, sums_ref, held, terms, sems = refs[4 + len(parts) :]
        for j in range(4):
            fetch(
                [w.at[:, pl.ds(0, rows)] for w in w_refs[j * n_parts : (j + 1) * n_parts]],
                order_ref,
                lambda s, j=j: held.at[j, pl.ds(pl.multiple_of(s * rows, rows), rows)],
                sems.at[j],
            )
        for j in range(4):
            pltpu.make_async_copy(held.at[j], held.at[j], sems.at[j]).wait()
            product = dot(proj_refs[j][...], held[j], 1, 1)
            if j == 0:
                token_ref[...] = product
            else:
                token_ref[...] += product
        terms[...] = jnp.zeros_like(terms)

        def fold(value):
            return jnp.sum(value.reshape(ROWS // 8, 8, width), axis=0)

        def back(i):
            at = tile(i, ROWS)
            incoming = token_ref[at]
            part, gain_terms = layer_norm_back(x_ref[at], incoming, gain_ref[...])
            token_ref[at] = after_ref[at] + part
            terms[0] += fold(gain_terms)
            terms[1] += fold(incoming)

        loop(count // ROWS, back)
        for k in range(2):
            sums_ref[k] = jnp.sum(terms[k], axis=0, keepdims=True)

    return call(
        kernel,
        "input_back",
        (order, x_zero, after_grad, gain, *projs, *parts),
        [SCALARS] + [ON_CHIP] * 7 + [ANYWHERE] * len(parts),
        [((count, width), full), ((2, 1, width), full)],
        [ON_CHIP] * 2,
        [
            pltpu.VMEM((4, width, wide), half),
            pltpu.VMEM((2, 8, width), full),
            pltpu.SemaphoreType.DMA((4,)),
        ],
    )


def payloads(which, w_fc1, w_fc2):
    rows, ff = w_fc1.shape
    full_share, width = w_fc2.shape
    share = full_share // 4
    n = ff // full_share
    hidden = n * share
    own, across = which
    if share % 128:
        fc1 = [lax.dynamic_slice(w_fc1, (0, (4 * s + own) * share), (rows, share)) for s in range(n)]
        fc2 = [lax.dynamic_slice(w_fc2, (g * share, 0), (share, width)).astype(half) for g in which]
        rest = jnp.concatenate([*fc1, fc2[0].reshape(rows, -1).astype(full)], axis=1)
        return rest.astype(half), fc2[1]

    def kernel(which_ref, fc1_ref, fc2_ref, rest_ref, two_ref):
        for s in range(n):
            at = pl.ds(pl.multiple_of((4 * s + which_ref[0]) * share, share), share)
            rest_ref[:, s * share : (s + 1) * share] = fc1_ref[:, at].astype(half)
        rest_ref[:, hidden : hidden + width] = fc2_ref[tile(which_ref[0], share), :].astype(half)
        two_ref[...] = fc2_ref[tile(which_ref[1], share), :].astype(half)

    return call(
        kernel,
        "payloads",
        (jnp.stack(which), w_fc1, w_fc2),
        [SCALARS] + [ON_CHIP] * 2,
        [((rows, hidden + width), half), ((share, width), half)],
        [ON_CHIP] * 2,
        [],
    )


def finish_mlp(q, pair, there, n):
    _, _, rows, width = pair.shape
    hidden = width
    share = hidden // n
    if share % 128:
        pieces = natural_quarters(q, pair, there)
        fc1 = jnp.stack([p[0].reshape(rows, n, share) for p in pieces], axis=2).reshape(rows, 4 * hidden)
        return fc1.astype(full), jnp.concatenate([p[1] for p in pieces]).astype(full)

    def kernel(q_ref, pair_ref, there_ref, fc1_ref, fc2_ref):
        for j in range(4):
            g = q_ref[0] ^ j
            held = pair_ref if j < 2 else there_ref
            for s in range(n):
                at = pl.ds(pl.multiple_of((4 * s + g) * share, share), share)
                fc1_ref[:, at] = held[j % 2, 0, :, s * share : (s + 1) * share].astype(full)
            fc2_ref[tile(g, rows), :] = held[j % 2, 1].astype(full)

    return call(
        kernel,
        "finish_mlp",
        (q[None], pair, there),
        [SCALARS, ON_CHIP, ON_CHIP],
        [((rows, 4 * hidden), full), ((4 * rows, width), full)],
        [ON_CHIP] * 2,
        [],
    )


def natural_quarters(q, pair, there):
    pieces = [pair[0], pair[1], there[0], there[1]]
    once = [jnp.where((q & 1) == 1, pieces[i ^ 1], pieces[i]) for i in range(4)]
    return [jnp.where(q >= 2, once[i ^ 2], once[i]) for i in range(4)]


def finish_attention(q, pair, there):
    _, rows, width = pair.shape
    quarter = width // 4

    def kernel(q_ref, pair_ref, there_ref, qkv_ref, out_ref):
        for j in range(4):
            g = q_ref[0] ^ j
            held = pair_ref if j < 2 else there_ref
            for t in range(3):
                at = pl.ds(pl.multiple_of(t * width + g * quarter, quarter), quarter)
                qkv_ref[:, at] = held[j % 2, :, t * quarter : (t + 1) * quarter].astype(full)
            out_ref[:, tile(g, quarter)] = held[j % 2, :, 3 * quarter :].astype(full)

    return call(
        kernel,
        "finish_attention",
        (q[None], pair, there),
        [SCALARS, ON_CHIP, ON_CHIP],
        [((rows, 3 * width), full), ((rows, width), full)],
        [ON_CHIP] * 2,
        [],
    )


def table(codes, width):
    ratio = 0.3 * jnp.exp(codes.astype(full) * (math.log(10.0 / 0.3) / (NSCALE - 1)))
    quarter = width // 4
    omega = jnp.exp(jnp.arange(quarter).astype(full) * (-math.log(10000.0) / quarter))
    steps = jnp.arange(GRID, dtype=jnp.int32).astype(full)
    angle = ratio[:, None, None] * steps[None, :, None] * omega[None, None, :]
    return jnp.concatenate([jnp.sin(angle), jnp.cos(angle)], axis=-1)


def local(
    tokens,
    scale_codes,
    w_qkv,
    b_q,
    b_v,
    w_out,
    b_out,
    gain_one,
    shift_one,
    w_fc1,
    b_fc1,
    w_fc2,
    b_fc2,
    gain_two,
    shift_two,
    cotangent,
):
    n = lax.axis_size("fsdp")
    q = lax.axis_index("dp")
    f = lax.axis_index("fsdp")
    row_count, width = tokens.shape
    rows = width // n
    ff = b_fc1.shape[0] * n
    ffq = ff // n // 4
    hidden = n * ffq
    quarter = width // 4
    n_img = scale_codes.shape[0]
    patches = row_count // n_img
    padded = -(-patches // 16) * 16
    factor = 1.0 / math.sqrt(width // HEADS)
    seq = Order(q)
    bits = list(reversed(range(n.bit_length() - 1)))
    near = min(1, len(bits) - 1)
    shard_order = jnp.asarray(masks(bits), jnp.int32) ^ f
    group_order = jnp.arange(4, dtype=jnp.int32) ^ q
    order = jnp.concatenate([shard_order, q[None]])

    def last_three(chain):
        while len(chain.bits) > 3:
            chain.launch()
            seq.land((), chain)
            chain.join()
        return chain

    small = jnp.concatenate(
        [b_q, b_v, b_out, gain_one, shift_one, b_fc2, gain_two, shift_two, b_fc1]
    )
    below = -(-small.shape[0] // (3 * quarter * 16)) * 16
    small = jnp.pad(small, (0, below * 3 * quarter - small.shape[0])).reshape(below, 3 * quarter)
    qkv_own = jnp.concatenate(
        [lax.dynamic_slice(w_qkv, (0, t * width + q * quarter), (rows, quarter)) for t in range(3)], axis=1
    )
    qkv = last_three(Gather(seq, jnp.concatenate([qkv_own, small]).astype(half), n, bits))
    qkv.launch()
    rest_own, two_own = payloads([seq.at(q), q ^ 2], w_fc1, w_fc2)
    rest_own, two_own = seq.land((rest_own, two_own), qkv)
    rest = Sent(lax.all_gather(rest_own, "fsdp", axis=0, tiled=False))
    two = Sent(lax.all_gather(two_own, "fsdp", axis=0, tiled=False))
    out_own = [lax.dynamic_slice(w_out, (0, g * quarter), (rows, quarter)) for g in (q, q ^ 2)]
    out = last_three(Gather(seq, jnp.concatenate(out_own, axis=1).astype(half), n, bits))

    def spread_rows(value):
        split = value.reshape(n_img, patches, width)
        return jnp.pad(split, ((0, 0), (0, padded - patches), (0, 0)))

    def compact(value):
        return value.reshape(n_img, padded, width)[:, :patches].reshape(row_count, width)

    qkv.join()
    qkv.launch()
    out.launch()
    spread_tokens = seq.land(spread_rows(seq.at(tokens)), qkv)
    qkv_near = qkv.join()
    qkv.launch()
    near_b, near_c = Sent(core_swap(qkv.held)), Sent(x_swap(qkv.held))
    seq.land((), out)
    out.join()
    out.launch()
    places = table(scale_codes, width)
    row_place = jnp.broadcast_to(places[:, :, None], (n_img, GRID, GRID, width // 2))
    col_place = jnp.broadcast_to(places[:, None], (n_img, GRID, GRID, width // 2))
    place = jnp.concatenate([row_place, col_place], axis=-1).reshape(n_img, patches, width)
    place = jnp.pad(place, ((0, 0), (0, padded - patches), (0, 0)))
    x_zero = (seq.at(spread_tokens).astype(full) + place).reshape(-1, width)
    x_zero = seq.land(x_zero, qkv, near_b)
    qkv_far = seq.at(qkv.got)
    far_b, far_c = Sent(core_swap(qkv_far)), Sent(x_swap(qkv_far))
    small_held = jnp.concatenate([qkv_near[:, rows:], qkv_far[:, rows:]]).reshape(n, -1)
    inverse = jnp.zeros((n,), jnp.int32).at[shard_order].set(jnp.arange(n, dtype=jnp.int32))
    small_all = jnp.take(small_held, inverse, axis=0).astype(full)
    vectors = [small_all[:, i * rows : (i + 1) * rows].reshape(1, width) for i in range(8)]
    full_bq, full_bv, full_bout, gain_one_f, shift_one_f, full_bfc2, gain_two_f, shift_two_f = vectors
    bias_units = small_all[:, 8 * rows : 8 * rows + 4 * ffq].reshape(n, 4, ffq)
    bias_fc1 = jnp.take(bias_units, group_order, axis=1).transpose(1, 0, 2).reshape(4, 1, hidden)
    bias_q = jnp.take(full_bq.reshape(4, quarter), group_order, axis=0)
    bias_v = jnp.take(full_bv.reshape(4, quarter), group_order, axis=0)
    bias_qkv = jnp.concatenate([bias_q, jnp.zeros_like(bias_q), bias_v], axis=1)[:, None]
    normed_one = layer_norm(x_zero, gain_one_f, shift_one_f).astype(half)
    normed_one = seq.land(normed_one, far_b, out)
    out.join()
    out.launch()

    first = attention_forward(
        seq.at(order), normed_one, bias_qkv[:2], ((qkv_near, qkv_far), (near_b.value, far_b.value)),
        n_img, patches, factor,
    )
    first = (seq.land(first[0], near_c, far_c), *first[1:])
    near_c, far_c = seq.at((near_c.value, far_c.value))
    near_d, far_d = Sent(core_swap(near_c)), Sent(core_swap(far_c))
    cot = seq.land(spread_rows(cotangent).reshape(-1, width), near_d, far_d, out)
    out_a = seq.at(out.join())
    out_b = Sent(core_swap(out_a))
    second = attention_forward(
        seq.at(order), normed_one, bias_qkv[2:], ((near_c, far_c), (near_d.value, far_d.value)),
        n_img, patches, factor,
    )
    second = (seq.land(second[0], out_b), *second[1:])
    outs = (out_a, out_b.value)
    qkv_parts = (
        (qkv_near, qkv_far), (near_b.value, far_b.value), (near_c, far_c), (near_d.value, far_d.value)
    )
    qkvs = (*first[:2], *second[:2])
    mixed = (*first[2:4], *second[2:4])
    lses = (*first[4:], *second[4:])
    after_attn, normed_two = attention_out(
        seq.at(order), x_zero, mixed, outs, full_bout, gain_two_f, shift_two_f
    )
    normed_two = seq.land(normed_two, rest)
    rest_a = seq.at(rest.value)
    rest_b = Sent(core_swap(rest_a))
    up_c = Sent(x_swap(seq.at(rest_a[:, :, :hidden])))
    seq.land((), rest_b)
    rests = (rest_a, rest_b.value)

    g_up0, g_up1, g_down0, g_down1, g_bias_a, out_sum, back_sum = mlp(
        seq.at(order), normed_two, cot, bias_fc1[:2], rests, rests, hidden
    )
    g_up1, g_down1 = seq.land((g_up1, g_down1), up_c, two)
    up_c, two = seq.at((up_c.value, two.value))
    up_d, two_d = Sent(core_swap(up_c)), Sent(core_swap(two))
    up_1, down_1 = Sent(core_swap(g_up1)), Sent(core_swap(g_down1))
    seq.land((), up_d, two_d, up_1, down_1)
    red_up = Reduce(seq, (g_up0, up_1.value), n)
    red_up.launch()
    red_down = Reduce(seq, (g_down0, down_1.value), n)
    red_down.launch(near)
    g_up2, g_up3, g_down2, g_down3, g_bias_b, _, grad_two_in, block = mlp(
        seq.at(order), normed_two, cot, bias_fc1[2:], (up_c, up_d.value), (two, two_d.value), 0,
        (out_sum, back_sum), (after_attn, full_bfc2),
    )
    block_out = compact(block)
    g_up3, g_down3 = seq.land((g_up3, g_down3), red_up, red_down)
    up_3, down_3 = Sent(core_swap(g_up3)), Sent(core_swap(g_down3))
    red_up.launch()
    red_down.launch()
    seq.land((), up_3, down_3)
    red_up_two = Reduce(seq, (g_up2, up_3.value), n)
    red_up_two.launch()
    red_down_two = Reduce(seq, (g_down2, down_3.value), n)
    red_down_two.launch(near)

    after_grad, mg0, mg1, mg2, mg3, g_out, sums_two = attention_out_back(
        seq.at(order), grad_two_in, after_attn, cot, gain_two_f, mixed, outs
    )
    mg2 = seq.land(mg2, red_up, red_down)
    red_up.launch()
    red_down.launch()
    g_w2, g_w3, proj2, proj3, sums_b = attention_back(
        seq.at(order), normed_one, qkvs[2:], lses[2:], (mg2, mg3), g_out, (2, 3), n_img, patches, factor, n
    )
    g_w3 = seq.land(g_w3, red_up, red_down, red_up_two, red_down_two)
    w_3 = Sent(core_swap(g_w3))
    red_up_two.launch()
    red_down_two.launch()
    seq.land((), w_3)
    middle = n // 2
    half_shape = (2,) * (len(bits) - 1)
    w_high = Sent(x_swap(seq.at(rounded_sum([g_w2[middle:], w_3.value[middle:]]))))
    g_w0, g_w1, proj0, proj1, sums_a = attention_back(
        seq.at(order), normed_one, qkvs[:2], lses[:2], (mg0, mg1), g_out, (0, 1), n_img, patches, factor, n
    )
    g_w1 = seq.land(g_w1, red_up_two, red_down_two, w_high)
    w_1 = Sent(core_swap(g_w1))
    red_up_two.launch()
    red_down_two.launch()
    seq.land((), w_1)
    red_w = Reduce(seq, (g_w0, w_1.value), n)
    red_w.launch(0, [w_high.value.reshape(half_shape + w_high.value.shape[1:])])
    w_low = Sent(x_swap(seq.at(rounded_sum([g_w2[:middle], w_3.value[:middle]]))))
    tokens_grad, sums_one = input_back(
        seq.at(order), x_zero, after_grad, gain_one_f, (proj0, proj1, proj2, proj3), qkv_parts
    )
    sums_one = seq.land(sums_one, red_up_two, red_down_two, red_w, w_low)
    red_w.terms = [*red_w.terms, w_low.value.reshape(half_shape + w_low.value.shape[1:])]
    while len(red_w.axes) > 2:
        red_w.launch()
        seq.land((), red_w)
    red_w.launch()
    for chain in (red_up, red_up_two, red_down, red_down_two):
        chain.rest()
    cross = Sent(x_swap(seq.at(jnp.stack([red_up_two.piece(), red_down_two.piece()]))))

    sums_proj = jnp.take(jnp.concatenate([sums_a, sums_b])[:, 0], group_order, axis=0)
    sums = [
        sums_proj[:, :quarter],
        sums_proj[:, 2 * quarter :],
        sums_two[0],
        sums_one[0],
        sums_one[1],
        sums_two[3],
        sums_two[1],
        sums_two[2],
    ]
    units = jnp.concatenate([g_bias_a, g_bias_b]).reshape(4, n, ffq)
    units = jnp.take(units, group_order, axis=0).transpose(1, 0, 2)
    packed = jnp.concatenate([s.reshape(n, rows) for s in sums] + [units.reshape(n, 4 * ffq)], axis=1)
    packed = jnp.take(packed, shard_order, axis=0)
    pad = -packed.shape[1] % 1024
    packed = jnp.pad(packed, ((0, 0), (0, pad))).reshape(n, -1, 128)
    small_sum = Reduce(seq, (packed,), n, full)
    stage = 0
    while small_sum.axes:
        small_sum.launch()
        if small_sum.axes:
            seq.land((), small_sum)
            if stage == 1:
                seq.land((), red_w)
                red_w.launch()
        else:
            seq.land((), small_sum, cross)
        stage += 1
    packed = seq.at(small_sum.piece())
    peers = Sent([xor_swap(packed, "dp", 4, m) for m in (1, 2, 3)])
    mlp_spread = Spread(
        seq,
        jnp.stack([rounded_sum([*red_up.terms, cross.value[0]]), rounded_sum([*red_down.terms, cross.value[1]])]),
    )
    seq.land((), mlp_spread, peers)
    vector = (packed + sum(peers.value)).reshape(-1)
    mlp_spread.cross()
    block_out, tokens_grad = seq.at((block_out, tokens_grad))
    grad_tokens = compact(tokens_grad)
    if len(bits) < 3:
        red_w.rest()
    else:
        seq.land((), red_w)
    w_spread = Spread(seq, red_w.piece())
    seq.land((), w_spread)
    w_spread.cross()
    seq.land((), mlp_spread)
    out_fc1, out_fc2 = finish_mlp(q, mlp_spread.pair, mlp_spread.got, n)
    out_fc2 = seq.land(out_fc2, w_spread)
    out_qkv, out_out = finish_attention(seq.value, w_spread.pair, w_spread.got)
    small_out = [vector[i * rows : (i + 1) * rows] for i in range(8)]
    out_bfc1 = vector[8 * rows : 8 * rows + 4 * ffq]
    o_bq, o_bv, o_bout, o_gone, o_sone, o_bfc2, o_gtwo, o_stwo = small_out
    return (
        block_out,
        grad_tokens,
        out_qkv,
        o_bq,
        o_bv,
        out_out,
        o_bout,
        o_gone,
        o_sone,
        out_fc1,
        out_bfc1,
        out_fc2,
        o_bfc2,
        o_gtwo,
        o_stwo,
    )


def solution(mesh):
    rows_split = P(("dp", "fsdp"), None)
    matrix = P("fsdp", None)
    vector = P("fsdp")
    return jax.shard_map(
        local,
        mesh=mesh,
        in_specs=(
            rows_split, P(("dp", "fsdp")), matrix, vector, vector, matrix, vector, vector, vector,
            matrix, vector, matrix, vector, vector, vector, rows_split,
        ),
        out_specs=(
            rows_split, rows_split, matrix, vector, vector, matrix, vector, vector, vector,
            matrix, vector, matrix, vector, vector, vector,
        ),
        check_vma=False,
    )
```

time: 678 us -> 485 us (0.72)
  waiting for transfers between devices: 284 us -> 117 us
  Pallas kernels: 238 us -> 191 us
  local copies, waits for them, and re-layouts: 54.6 us -> 39.1 us
  other arithmetic: 49.1 us -> 63.9 us
  between operations: 2.48 us -> 15.4 us
  starting transfers between devices: 42.7 us -> 50.3 us
    ppermute x50 -> x51, waiting for transfers between devices: 284 us -> 111 us  [xor_swap(): return lax.ppermute(value, axis, [(i, i ^ mask) for i in range(size)])]
    pallas_call x9 -> x12, Pallas kernels: 238 us -> 191 us  [call(): pl.pallas_call(kernel, out_shape=[jax.ShapeDtypeStruct(shape, kind) for s...]
    convert_element_type x19 -> x17, other arithmetic: 24.7 us -> 33.4 us  [rounded_sum(): return sum((t.astype(full) for t in terms)).astype(kind)]
    another operation x16, other arithmetic: 4.98 us -> 13.4 us  [the longest x3 2.24 us: local(): far = swap(jnp.stack(pair_high), 'fsdp', n, 0)]
    ppermute x50 -> x51, starting transfers between devices: 42.7 us -> 50.3 us  [xor_swap(): return lax.ppermute(value, axis, [(i, i ^ mask) for i in range(size)])]
  transfers between devices with their start and end apart: 50 -> 53, of which waited for: 24 -> 26; matrix products, arithmetic and copies ran while one was open for 14% -> 15% of each run, Pallas kernels for 29% -> 39%
where the time goes in v4:
time: 485 us; the launch traced here: 476 us
  Pallas kernels  191 us (39%)
  waiting for transfers between devices  117 us (24%)
  other arithmetic  63.9 us (13%)
  starting transfers between devices  50.3 us (10%)
  local copies, waits for them, and re-layouts  39.1 us (8%)
  between operations  15.4 us (3%)
    pallas_call x12, Pallas kernels, call(): pl.pallas_call(kernel, out_shape=[jax.ShapeDtypeStruct(shape, kind) for s...  191 us
    ppermute x51, waiting for transfers between devices, xor_swap(): return lax.ppermute(value, axis, [(i, i ^ mask) for i in range(size)])  111 us
    ppermute x51, starting transfers between devices, xor_swap(): return lax.ppermute(value, axis, [(i, i ^ mask) for i in range(size)])  50.3 us
    convert_element_type x17, other arithmetic, rounded_sum(): return sum((t.astype(full) for t in terms)).astype(kind)  33.4 us
  transfers between devices with their start and end apart: 53, of which 26 were waited for; matrix products, arithmetic and copies ran while one was open for 15% of the time, Pallas kernels for 39%

profile of v4, /device:TPU:0, one launch (start us, length us, event | category | flops | bytes accessed | tf_op | source)
XLA Modules:
  0.0 476.4 jit_solution(14778935360816779673)
XLA Ops:
  16.0 4.1 collective-permute-start
  24.3 3.2 payloads.1
  27.5 2.7 collective-permute-done
  34.8 6.9 %collective-permute-done.2 = bf16[2,144,768]{2,1,0:T(8,128)(2,1)S(1)} collective-permute-done((bf16[2,144,768]{2,1,0:T(8,128)(2,1)S(1)}, bf16[2,144,768]{2,1,0:T(8,128)(2,1)S(1)}, u32[]{:S(2)}, u32[]{:S(2)}) %collective-permute-start.2) | collective-permute-done | bytes 442400 | tf_op jit(solution)/shard_map/ppermute | solution.py:19
  45.3 3.4 collective-permute-start.1
  49.3 3.6 copy.33
  57.9 3.3 pad_add_fusion
  61.2 6.4 %collective-permute-done.3.refs_1_.refs_5_ = bf16[4,144,768]{2,1,0:T(8,128)(2,1)} collective-permute-done((bf16[4,144,768]{2,1,0:T(8,128)(2,1)}, bf16[4,144,768]{2,1,0:T(8,128)(2,1)}, u32[]{:S(2)}, u32[]{:S(2)}) %collective-permute-start.3) | collective-permute-done | bytes 884768 | tf_op jit(solution)/shard_map/ppermute | solution.py:19
  72.1 2.5 gather_fusion
  83.0 10.7 %attention_forward.2 = (bf16[832,768]{1,0:T(8,128)(2,1)}, bf16[832,768]{1,0:T(8,128)(2,1)}, bf16[832,256]{1,0:T(8,128)(2,1)}, bf16[832,256]{1,0:T(8,128)(2,1)}, ...) custom-call(s32[9]{0:T(128)} %pad_add_fusion.1.order_ref, bf16[832,1024]{1,0:T(8,128)(2,1)} %add_convert_fusion.normed_ref, ...), custom_call_target="tpu_custom_call" | custom-call | tf_op jit(solution)/shard_map/attention_forward/pallas_call | solution.py:134
  99.8 21.5 %collective-permute-done.11 = bf16[4,128,512]{2,1,0:T(8,128)(2,1)} collective-permute-done((bf16[4,128,512]{2,1,0:T(8,128)(2,1)}, bf16[4,128,512]{2,1,0:T(8,128)(2,1)}, u32[]{:S(2)}, u32[]{:S(2)}) %collective-permute-start.11) | collective-permute-done | bytes 524320 | tf_op jit(solution)/shard_map/ppermute | solution.py:19
  124.1 10.6 %attention_forward.3 = (bf16[832,768]{1,0:T(8,128)(2,1)}, bf16[832,768]{1,0:T(8,128)(2,1)}, bf16[832,256]{1,0:T(8,128)(2,1)}, bf16[832,256]{1,0:T(8,128)(2,1)}, ...) custom-call(s32[9]{0:T(128)} %pad_add_fusion.1.order_ref, bf16[832,1024]{1,0:T(8,128)(2,1)} %add_convert_fusion.normed_ref, ...), custom_call_target="tpu_custom_call" | custom-call | tf_op jit(solution)/shard_map/attention_forward/pallas_call | solution.py:134
  135.7 9.7 %attention_out.1 = (f32[832,1024]{1,0:T(8,128)}, bf16[832,1024]{1,0:T(8,128)(2,1)}) custom-call(s32[9]{0:T(128)} %pad_add_fusion.1.order_ref, f32[832,1024]{1,0:T(8,128)} %bitcast.241, f32[1,1024]{1,0:T(1,128)} %bitcast.288, f32[1,1024]{1,0:T(1,128)} %bitcast.278, f32[1,1024]{1,0:T(1,128)} %bitcast.287, bf16[832,256]{1,0:T(8,128)(2,1)} %get-tuple-element.331.refs_0_, ...), custom_call_target="tpu_custom_call" | custom-call | tf_op jit(solution)/shard_map/attention_out/pallas_call | solution.py:134
  145.8 3.2 slice.560
  153.0 37.9 %mlp.2 = (bf16[8,128,1024]{2,1,0:T(8,128)(2,1)}, bf16[8,128,1024]{2,1,0:T(8,128)(2,1)}, bf16[8,128,1024]{2,1,0:T(8,128)(2,1)}, bf16[8,128,1024]{2,1,0:T(8,128)(2...) custom-call(s32[9]{0:T(128)} %pad_add_fusion.1.order_ref, ...), custom_call_target="tpu_custom_call" | custom-call | tf_op jit(solution)/shard_map/mlp/pallas_call | solution.py:134
  190.9 6.5 %all-gather.7.cloned.1.call-done = bf16[1024,1024]{1,0:T(8,128)(2,1)} async-done(((bf16[128,1024]{1,0:T(8,128)(2,1)}), bf16[1024,1024]{1,0:T(8,128)(2,1)}) %all-gather.7.cloned.1.call-update) | async-done | bytes 2097168 | tf_op jit(solution)/shard_map/all_gather | solution.py:776
  198.5 3.3 collective-permute-done.15.refs_5_
  201.8 3.0 collective-permute-done.16.refs_7_
  204.8 3.0 collective-permute-done.17
  207.8 3.0 collective-permute-done.18
  210.8 3.5 add_convert_fusion.6
  218.7 41.5 %mlp.3 = (bf16[8,128,1024]{2,1,0:T(8,128)(2,1)}, bf16[8,128,1024]{2,1,0:T(8,128)(2,1)}, bf16[8,128,1024]{2,1,0:T(8,128)(2,1)}, bf16[8,128,1024]{2,1,0:T(8,128)(2...) custom-call(s32[9]{0:T(128)} %pad_add_fusion.1.order_ref, ...), custom_call_target="tpu_custom_call" | custom-call | tf_op jit(solution)/shard_map/mlp/pallas_call | solution.py:134
  260.8 2.2 fusion.6
  263.0 2.3 fusion.7
  272.5 13.3 %attention_out_back.1 = (f32[832,1024]{1,0:T(8,128)}, bf16[832,256]{1,0:T(8,128)(2,1)}, bf16[832,256]{1,0:T(8,128)(2,1)}, bf16[832,256]{1,0:T(8,128)(2,1)}, bf16...) custom-call(s32[9]{0:T(128)} %pad_add_fusion.1.order_ref, ...), custom_call_target="tpu_custom_call" | custom-call | tf_op jit(solution)/shard_map/attention_out_back/pallas_call | solution.py:134
  288.4 3.1 collective-permute-start.26
  291.6 19.3 %attention_back.2 = (bf16[8,128,1024]{2,1,0:T(8,128)(2,1)}, bf16[8,128,1024]{2,1,0:T(8,128)(2,1)}, bf16[832,768]{1,0:T(8,128)(2,1)}, bf16[832,768]{1,0:T(8,128)(2,1)}, f32[2,1,768]{2,1,0:T(1,128)}) custom-call(s32[9]{0:T(128)} %pad_add_fusion.1.order_ref, bf16[832,1024]{1,0:T(8,128)(2,1)} %add_convert_fusion.normed_ref, ...), custom_call_target="tpu_custom_call" | custom-call | tf_op jit(solution)/shard_map/attention_back/pallas_call | solution.py:134
  311.3 2.0 collective-permute-done.28
  315.1 2.4 fusion.5
  317.7 2.0 add_convert_fusion.2
  321.8 3.9 collective-permute-start.30
  325.7 19.5 %attention_back.3 = (bf16[8,128,1024]{2,1,0:T(8,128)(2,1)}, bf16[8,128,1024]{2,1,0:T(8,128)(2,1)}, bf16[832,768]{1,0:T(8,128)(2,1)}, bf16[832,768]{1,0:T(8,128)(2,1)}, f32[2,1,768]{2,1,0:T(1,128)}) custom-call(s32[9]{0:T(128)} %pad_add_fusion.1.order_ref, bf16[832,1024]{1,0:T(8,128)(2,1)} %add_convert_fusion.normed_ref, ...), custom_call_target="tpu_custom_call" | custom-call | tf_op jit(solution)/shard_map/attention_back/pallas_call | solution.py:134
  348.2 2.1 fusion.20
  350.6 3.2 add_convert_fusion.1
  359.6 18.2 %input_back.1 = (f32[832,1024]{1,0:T(8,128)}, f32[2,1,1024]{2,1,0:T(1,128)}) custom-call(s32[9]{0:T(128)} %pad_add_fusion.1.order_ref, f32[832,1024]{1,0:T(8,128)} %bitcast.242, f32[832,1024]{1,0:T(8,128)} %get-tuple-element.455.after_ref, f32[1,1024]{1,0:T(1,128)} %bitcast.285, bf16[832,768]{1,0:T(8,128)(2,1)} %get-tuple-element.456.refs_0_, ...), custom_call_target="tpu_custom_call" | custom-call | tf_op jit(solution)/shard_map/input_back/pallas_call | solution.py:134
  378.3 4.2 collective-permute-done.34
  383.9 2.1 fusion.23
  393.2 10.1 %collective-permute-done.39 = f32[2,16,128]{2,1,0:T(8,128)S(1)} collective-permute-done((f32[2,16,128]{2,1,0:T(8,128)S(1)}, f32[2,16,128]{2,1,0:T(8,128)S(1)}, u32[]{:S(2)}, u32[]{:S(2)}) %collective-permute-start.39) | collective-permute-done | bytes 16416 | tf_op jit(solution)/shard_map/ppermute | solution.py:19
  403.4 2.3 fusion.13
  405.7 2.6 collective-permute-start.41
  408.3 1.9 collective-permute-done.41
  410.2 2.0 fusion.25
  412.4 2.7 collective-permute-start.48
  420.1 7.7 %collective-permute-done.48 = bf16[128,1024]{1,0:T(8,128)(2,1)S(1)} collective-permute-done((bf16[128,1024]{1,0:T(8,128)(2,1)}, bf16[128,1024]{1,0:T(8,128)(2,1)S(1)}, u32[]{:S(2)}, u32[]{:S(2)}) %collective-permute-start.48) | collective-permute-done | bytes 262176 | tf_op jit(solution)/shard_map/ppermute | solution.py:19
  435.7 20.0 %collective-permute-done.47.there_ref = bf16[2,2,128,1024]{3,2,1,0:T(8,128)(2,1)} collective-permute-done((bf16[2,2,128,1024]{3,2,1,0:T(8,128)(2,1)}, bf16[2,2,128,1024]{3,2,1,0:T(8,128)(2,1)}, u32[]{:S(2)}, u32[]{:S(2)}) %collective-permute-start.47) | collective-permute-done | bytes 1048608 | tf_op jit(solution)/shard_map/ppermute | solution.py:19
  455.7 3.9 finish_mlp.1
  459.6 6.9 %collective-permute-done.50.there_ref = bf16[2,128,1024]{2,1,0:T(8,128)(2,1)} collective-permute-done((bf16[2,128,1024]{2,1,0:T(8,128)(2,1)}, bf16[2,128,1024]{2,1,0:T(8,128)(2,1)}, u32[]{:S(2)}, u32[]{:S(2)}) %collective-permute-start.50) | collective-permute-done | bytes 524320 | tf_op jit(solution)/shard_map/ppermute | solution.py:19
  466.5 2.7 finish_attention.1
  (299 shorter events, 105.0 us)
Async XLA Ops:
  7.2 138.2 %all-gather.5.cloned.1.call-start = ((), (), s32[]{:S(2)}) async-start(), calls=%async_computation | async-start | bytes 4718592 | tf_op jit(solution)/shard_map/all_gather | solution.py:775
  16.0 14.3 %collective-permute-start = (bf16[1,144,768]{2,1,0:T(8,128)(2,1)S(1)}, bf16[1,144,768]{2,1,0:T(8,128)(2,1)S(1)}, u32[]{:S(2)}, u32[]{:S(2)}) collective-permute-start(bf16[1,144,768]{2,1,0:T(8,128)(2,1)S(1)} %pad_maximum_fusion.9), channel_id=1, source_target_pairs={{0,4},{1,5},{2,6},{3,7},{4,0},{5,1},{6,2},{7,3},{8,12},{9,13},{10,... | collective-permute-start | bytes 663560 | tf_op jit(solution)/shard_map/ppermute | solution.py:19
  30.3 11.4 %collective-permute-start.2 = (bf16[2,144,768]{2,1,0:T(8,128)(2,1)S(1)}, bf16[2,144,768]{2,1,0:T(8,128)(2,1)S(1)}, u32[]{:S(2)}, u32[]{:S(2)}) collective-permute-start(bf16[2,144,768]{2,1,0:T(8,128)(2,1)S(1)} %pad_maximum_fusion.7), channel_id=1, source_target_pairs={{0,2},{1,3},{2,0},{3,1},{4,6},{5,7},{6,4},{7,5},{8,10},{9,11},{10,... | collective-permute-start | bytes 1327112 | tf_op jit(solution)/shard_map/ppermute | solution.py:19
  42.5 18.7 %collective-permute-start.4 = (bf16[4,144,768]{2,1,0:T(8,128)(2,1)}, bf16[4,144,768]{2,1,0:T(8,128)(2,1)}, u32[]{:S(2)}, u32[]{:S(2)}) collective-permute-start(bf16[4,144,768]{2,1,0:T(8,128)(2,1)} %constant_dynamic-update-slice_fusion.refs_0_.refs_4_), channel_id=1, source_target_pairs={{0,8},{8,0},{16,24},{24,16},{1,9},{9,1},{17,25},{25,17},{2,10},{10... | collective-permute-start | bytes 2654216 | tf_op jit(solution)/shard_map/ppermute | solution.py:19
  42.5 25.1 %collective-permute-start.3 = (bf16[4,144,768]{2,1,0:T(8,128)(2,1)}, bf16[4,144,768]{2,1,0:T(8,128)(2,1)}, u32[]{:S(2)}, u32[]{:S(2)}) collective-permute-start(bf16[4,144,768]{2,1,0:T(8,128)(2,1)} %constant_dynamic-update-slice_fusion.refs_0_.refs_4_), channel_id=1, source_target_pairs={{0,1},{1,0},{2,3},{3,2},{4,5},{5,4},{6,7},{7,6},{8,9},{9,8},{10,11... | collective-permute-start | bytes 2654216 | tf_op jit(solution)/shard_map/ppermute | solution.py:19
  45.3 10.1 %collective-permute-start.1 = (bf16[1,128,512]{2,1,0:T(8,128)(2,1)S(1)}, bf16[1,128,512]{2,1,0:T(8,128)(2,1)S(1)}, u32[]{:S(2)}, u32[]{:S(2)}) collective-permute-start(bf16[1,128,512]{2,1,0:T(8,128)(2,1)S(1)} %pad_maximum_fusion.10), channel_id=1, source_target_pairs={{0,4},{1,5},{2,6},{3,7},{4,0},{5,1},{6,2},{7,3},{8,12},{9,13},{10,... | collective-permute-start | bytes 393224 | tf_op jit(solution)/shard_map/ppermute | solution.py:19
  53.0 144.5 %all-gather.7.cloned.1.call-start = ((), (), s32[]{:S(2)}) async-start(), calls=%async_computation.1 | async-start | bytes 2359296 | tf_op jit(solution)/shard_map/all_gather | solution.py:776
  53.9 39.8 %collective-permute-start.7 = (bf16[4,144,768]{2,1,0:T(8,128)(2,1)}, bf16[4,144,768]{2,1,0:T(8,128)(2,1)}, u32[]{:S(2)}, u32[]{:S(2)}) collective-permute-start(bf16[4,144,768]{2,1,0:T(8,128)(2,1)} %constant_dynamic-update-slice_fusion.refs_0_.refs_4_), channel_id=1, source_target_pairs={{0,16},{8,24},{16,0},{24,8},{1,17},{9,25},{17,1},{25,9},{2,18},{10... | collective-permute-start | bytes 2654216 | tf_op jit(solution)/shard_map/ppermute | solution.py:19
  56.2 25.0 %collective-permute-start.6 = (bf16[2,128,512]{2,1,0:T(8,128)(2,1)}, bf16[2,128,512]{2,1,0:T(8,128)(2,1)}, u32[]{:S(2)}, u32[]{:S(2)}) collective-permute-start(bf16[2,128,512]{2,1,0:T(8,128)(2,1)} %pad_maximum_fusion.8), channel_id=1, source_target_pairs={{0,2},{1,3},{2,0},{3,1},{4,6},{5,7},{6,4},{7,5},{8,10},{9,11},{10,... | collective-permute-start | bytes 786440 | tf_op jit(solution)/shard_map/ppermute | solution.py:19
  69.1 25.6 %collective-permute-start.8 = (bf16[4,144,768]{2,1,0:T(8,128)(2,1)}, bf16[4,144,768]{2,1,0:T(8,128)(2,1)}, u32[]{:S(2)}, u32[]{:S(2)}) collective-permute-start(bf16[4,144,768]{2,1,0:T(8,128)(2,1)} %collective-permute-done.3.refs_1_.refs_5_), channel_id=1, source_target_pairs={{0,16},{8,24},{16,0},{24,8},{1,17},{9,25},{17,1},{25,9},{2,18},{10... | collective-permute-start | bytes 2654216 | tf_op jit(solution)/shard_map/ppermute | solution.py:19
  70.2 11.0 %collective-permute-start.5 = (bf16[4,144,768]{2,1,0:T(8,128)(2,1)}, bf16[4,144,768]{2,1,0:T(8,128)(2,1)}, u32[]{:S(2)}, u32[]{:S(2)}) collective-permute-start(bf16[4,144,768]{2,1,0:T(8,128)(2,1)} %collective-permute-done.3.refs_1_.refs_5_), channel_id=1, source_target_pairs={{0,8},{8,0},{16,24},{24,16},{1,9},{9,1},{17,25},{25,17},{2,10},{10... | collective-permute-start | bytes 2654216 | tf_op jit(solution)/shard_map/ppermute | solution.py:19
  94.7 26.6 %collective-permute-start.9 = (bf16[4,144,768]{2,1,0:T(8,128)(2,1)}, bf16[4,144,768]{2,1,0:T(8,128)(2,1)S(1)}, u32[]{:S(2)}, u32[]{:S(2)}) collective-permute-start(bf16[4,144,768]{2,1,0:T(8,128)(2,1)} %collective-permute-done.7.refs_0_.refs_8_), channel_id=1, source_target_pairs={{0,8},{8,0},{16,24},{24,16},{1,9},{9,1},{17,25},{25,17},{2,10},{10... | collective-permute-start | bytes 2654216 | tf_op jit(solution)/shard_map/ppermute | solution.py:19
  94.7 26.6 %collective-permute-start.10 = (bf16[4,144,768]{2,1,0:T(8,128)(2,1)}, bf16[4,144,768]{2,1,0:T(8,128)(2,1)S(1)}, u32[]{:S(2)}, u32[]{:S(2)}) collective-permute-start(bf16[4,144,768]{2,1,0:T(8,128)(2,1)} %collective-permute-done.8.refs_1_.refs_9_), channel_id=1, source_target_pairs={{0,8},{8,0},{16,24},{24,16},{1,9},{9,1},{17,25},{25,17},{2,10},{10... | collective-permute-start | bytes 2654216 | tf_op jit(solution)/shard_map/ppermute | solution.py:19
  95.2 26.1 %collective-permute-start.11 = (bf16[4,128,512]{2,1,0:T(8,128)(2,1)}, bf16[4,128,512]{2,1,0:T(8,128)(2,1)}, u32[]{:S(2)}, u32[]{:S(2)}) collective-permute-start(bf16[4,128,512]{2,1,0:T(8,128)(2,1)} %pad_maximum_fusion.3), channel_id=1, source_target_pairs={{0,1},{1,0},{2,3},{3,2},{4,5},{5,4},{6,7},{7,6},{8,9},{9,8},{10,11... | collective-permute-start | bytes 1572872 | tf_op jit(solution)/shard_map/ppermute | solution.py:19
  123.3 11.4 %collective-permute-start.12 = (bf16[8,128,512]{2,1,0:T(8,128)(2,1)S(1)}, bf16[8,128,512]{2,1,0:T(8,128)(2,1)S(1)}, u32[]{:S(2)}, u32[]{:S(2)}) collective-permute-start(bf16[8,128,512]{2,1,0:T(8,128)(2,1)S(1)} %pad_maximum_fusion.1.refs_4_), channel_id=1, source_target_pairs={{0,8},{8,0},{16,24},{24,16},{1,9},{9,1},{17,25},{25,17},{2,10},{10... | collective-permute-start | bytes 3145736 | tf_op jit(solution)/shard_map/ppermute | solution.py:19
  145.4 7.6 %collective-permute-start.13 = (bf16[8,128,2048]{2,1,0:T(8,128)(2,1)}, bf16[8,128,2048]{2,1,0:T(8,128)(2,1)}, u32[]{:S(2)}, u32[]{:S(2)}) collective-permute-start(bf16[8,128,2048]{2,1,0:T(8,128)(2,1)} %bitcast.246), channel_id=1, source_target_pairs={{0,8},{8,0},{16,24},{24,16},{1,9},{9,1},{17,25},{25,17},{2,10},{10... | collective-permute-start | bytes 12582920 | tf_op jit(solution)/shard_map/ppermute | solution.py:19
  148.9 48.5 %collective-permute-start.14 = (bf16[8,128,1024]{2,1,0:T(8,128)(2,1)}, bf16[8,128,1024]{2,1,0:T(8,128)(2,1)}, u32[]{:S(2)}, u32[]{:S(2)}) collective-permute-start(bf16[8,128,1024]{2,1,0:T(8,128)(2,1)} %slice.560), channel_id=1, source_target_pairs={{0,16},{8,24},{16,0},{24,8},{1,17},{9,25},{17,1},{25,9},{2,18},{10... | collective-permute-start | bytes 6291464 | tf_op jit(solution)/shard_map/ppermute | solution.py:19
  197.4 4.4 collective-permute-start.15
  197.4 7.4 %collective-permute-start.16 = (bf16[8,128,1024]{2,1,0:T(8,128)(2,1)}, bf16[8,128,1024]{2,1,0:T(8,128)(2,1)S(1)}, u32[]{:S(2)}, u32[]{:S(2)}) collective-permute-start(bf16[8,128,1024]{2,1,0:T(8,128)(2,1)} %bitcast.261), channel_id=1, source_target_pairs={{0,8},{8,0},{16,24},{24,16},{1,9},{9,1},{17,25},{25,17},{2,10},{10... | collective-permute-start | bytes 6291464 | tf_op jit(solution)/shard_map/ppermute | solution.py:19
  198.0 9.9 %collective-permute-start.17 = (bf16[8,128,1024]{2,1,0:T(8,128)(2,1)}, bf16[8,128,1024]{2,1,0:T(8,128)(2,1)S(1)}, u32[]{:S(2)}, u32[]{:S(2)}) collective-permute-start(bf16[8,128,1024]{2,1,0:T(8,128)(2,1)} %get-tuple-element.360), channel_id=1, source_target_pairs={{0,8},{8,0},{16,24},{24,16},{1,9},{9,1},{17,25},{25,17},{2,10},{10... | collective-permute-start | bytes 6291464 | tf_op jit(solution)/shard_map/ppermute | solution.py:19
  198.0 12.9 %collective-permute-start.18 = (bf16[8,128,1024]{2,1,0:T(8,128)(2,1)}, bf16[8,128,1024]{2,1,0:T(8,128)(2,1)S(1)}, u32[]{:S(2)}, u32[]{:S(2)}) collective-permute-start(bf16[8,128,1024]{2,1,0:T(8,128)(2,1)} %get-tuple-element.361), channel_id=1, source_target_pairs={{0,8},{8,0},{16,24},{24,16},{1,9},{9,1},{17,25},{25,17},{2,10},{10... | collective-permute-start | bytes 6291464 | tf_op jit(solution)/shard_map/ppermute | solution.py:19
  215.7 44.6 %collective-permute-start.20 = (bf16[2,2,128,1024]{3,2,1,0:T(8,128)(2,1)}, bf16[2,2,128,1024]{3,2,1,0:T(8,128)(2,1)S(1)}, u32[]{:S(2)}, u32[]{:S(2)}) collective-permute-start(bf16[2,2,128,1024]{3,2,1,0:T(8,128)(2,1)} %fusion), channel_id=1, source_target_pairs={{0,2},{1,3},{2,0},{3,1},{4,6},{5,7},{6,4},{7,5},{8,10},{9,11},{10,... | collective-permute-start | bytes 3145736 | tf_op jit(solution)/shard_map/ppermute | solution.py:19
  217.1 43.1 %collective-permute-start.19 = (bf16[2,2,128,1024]{3,2,1,0:T(8,128)(2,1)}, bf16[2,2,128,1024]{3,2,1,0:T(8,128)(2,1)}, u32[]{:S(2)}, u32[]{:S(2)}) collective-permute-start(bf16[2,2,128,1024]{3,2,1,0:T(8,128)(2,1)} %bitcast.23), channel_id=1, source_target_pairs={{0,1},{1,0},{2,3},{3,2},{4,5},{5,4},{6,7},{7,6},{8,9},{9,8},{10,11... | collective-permute-start | bytes 3145736 | tf_op jit(solution)/shard_map/ppermute | solution.py:19
  260.3 6.0 %collective-permute-start.21 = (bf16[8,128,1024]{2,1,0:T(8,128)(2,1)}, bf16[8,128,1024]{2,1,0:T(8,128)(2,1)S(1)}, u32[]{:S(2)}, u32[]{:S(2)}) collective-permute-start(bf16[8,128,1024]{2,1,0:T(8,128)(2,1)} %get-tuple-element.383), channel_id=1, source_target_pairs={{0,8},{8,0},{16,24},{24,16},{1,9},{9,1},{17,25},{25,17},{2,10},{10... | collective-permute-start | bytes 6291464 | tf_op jit(solution)/shard_map/ppermute | solution.py:19
  260.3 7.4 %collective-permute-start.22 = (bf16[8,128,1024]{2,1,0:T(8,128)(2,1)}, bf16[8,128,1024]{2,1,0:T(8,128)(2,1)S(1)}, u32[]{:S(2)}, u32[]{:S(2)}) collective-permute-start(bf16[8,128,1024]{2,1,0:T(8,128)(2,1)} %get-tuple-element.384), channel_id=1, source_target_pairs={{0,8},{8,0},{16,24},{24,16},{1,9},{9,1},{17,25},{25,17},{2,10},{10... | collective-permute-start | bytes 6291464 | tf_op jit(solution)/shard_map/ppermute | solution.py:19
  265.3 20.5 %collective-permute-start.24 = (bf16[2,128,1024]{2,1,0:T(8,128)(2,1)}, bf16[2,128,1024]{2,1,0:T(8,128)(2,1)S(1)}, u32[]{:S(2)}, u32[]{:S(2)}) collective-permute-start(bf16[2,128,1024]{2,1,0:T(8,128)(2,1)} %fusion.7), channel_id=1, source_target_pairs={{0,1},{1,0},{2,3},{3,2},{4,5},{5,4},{6,7},{7,6},{8,9},{9,8},{10,11... | collective-permute-start | bytes 1572872 | tf_op jit(solution)/shard_map/ppermute | solution.py:19
  265.7 20.1 %collective-permute-start.23 = (bf16[2,128,1024]{2,1,0:T(8,128)(2,1)}, bf16[2,128,1024]{2,1,0:T(8,128)(2,1)}, u32[]{:S(2)}, u32[]{:S(2)}) collective-permute-start(bf16[2,128,1024]{2,1,0:T(8,128)(2,1)} %fusion.6), channel_id=1, source_target_pairs={{0,2},{1,3},{2,0},{3,1},{4,6},{5,7},{6,4},{7,5},{8,10},{9,11},{10,... | collective-permute-start | bytes 1572872 | tf_op jit(solution)/shard_map/ppermute | solution.py:19
  270.7 42.6 %collective-permute-start.28 = (bf16[2,2,128,1024]{3,2,1,0:T(8,128)(2,1)}, bf16[2,2,128,1024]{3,2,1,0:T(8,128)(2,1)}, u32[]{:S(2)}, u32[]{:S(2)}) collective-permute-start(bf16[2,2,128,1024]{3,2,1,0:T(8,128)(2,1)} %fusion.1), channel_id=1, source_target_pairs={{0,2},{1,3},{2,0},{3,1},{4,6},{5,7},{6,4},{7,5},{8,10},{9,11},{10,... | collective-permute-start | bytes 3145736 | tf_op jit(solution)/shard_map/ppermute | solution.py:19
  271.0 42.4 %collective-permute-start.27 = (bf16[2,2,128,1024]{3,2,1,0:T(8,128)(2,1)}, bf16[2,2,128,1024]{3,2,1,0:T(8,128)(2,1)}, u32[]{:S(2)}, u32[]{:S(2)}) collective-permute-start(bf16[2,2,128,1024]{3,2,1,0:T(8,128)(2,1)} %bitcast.35), channel_id=1, source_target_pairs={{0,1},{1,0},{2,3},{3,2},{4,5},{5,4},{6,7},{7,6},{8,9},{9,8},{10,11... | collective-permute-start | bytes 3145736 | tf_op jit(solution)/shard_map/ppermute | solution.py:19
  288.4 22.5 %collective-permute-start.26 = (bf16[128,1024]{1,0:T(8,128)(2,1)S(1)}, bf16[128,1024]{1,0:T(8,128)(2,1)S(1)}, u32[]{:S(2)}, u32[]{:S(2)}) collective-permute-start(bf16[128,1024]{1,0:T(8,128)(2,1)S(1)} %fusion.22), channel_id=1, source_target_pairs={{0,4},{1,5},{2,6},{3,7},{4,0},{5,1},{6,2},{7,3},{8,12},{9,13},{10,... | collective-permute-start | bytes 786440 | tf_op jit(solution)/shard_map/ppermute | solution.py:19
  291.5 19.8 %collective-permute-start.25 = (bf16[128,1024]{1,0:T(8,128)(2,1)S(1)}, bf16[128,1024]{1,0:T(8,128)(2,1)S(1)}, u32[]{:S(2)}, u32[]{:S(2)}) collective-permute-start(bf16[128,1024]{1,0:T(8,128)(2,1)S(1)} %fusion.21), channel_id=1, source_target_pairs={{0,4},{1,5},{2,6},{3,7},{4,0},{5,1},{6,2},{7,3},{8,12},{9,13},{10,... | collective-permute-start | bytes 786440 | tf_op jit(solution)/shard_map/ppermute | solution.py:19
  313.3 4.4 collective-permute-start.29
  319.7 25.5 %collective-permute-start.32 = (bf16[4,128,1024]{2,1,0:T(8,128)(2,1)S(1)}, bf16[4,128,1024]{2,1,0:T(8,128)(2,1)}, u32[]{:S(2)}, u32[]{:S(2)}) collective-permute-start(bf16[4,128,1024]{2,1,0:T(8,128)(2,1)S(1)} %get-tuple-element.441), channel_id=1, source_target_pairs={{0,16},{8,24},{16,0},{24,8},{1,17},{9,25},{17,1},{25,9},{2,18},{10... | collective-permute-start | bytes 3145736 | tf_op jit(solution)/shard_map/ppermute | solution.py:19
  321.2 24.0 %collective-permute-start.31 = (bf16[2,128,1024]{2,1,0:T(8,128)(2,1)}, bf16[2,128,1024]{2,1,0:T(8,128)(2,1)S(1)}, u32[]{:S(2)}, u32[]{:S(2)}) collective-permute-start(bf16[2,128,1024]{2,1,0:T(8,128)(2,1)} %fusion.5), channel_id=1, source_target_pairs={{0,1},{1,0},{2,3},{3,2},{4,5},{5,4},{6,7},{7,6},{8,9},{9,8},{10,11... | collective-permute-start | bytes 1572872 | tf_op jit(solution)/shard_map/ppermute | solution.py:19
  321.8 23.4 %collective-permute-start.30 = (bf16[2,128,1024]{2,1,0:T(8,128)(2,1)S(1)}, bf16[2,128,1024]{2,1,0:T(8,128)(2,1)S(1)}, u32[]{:S(2)}, u32[]{:S(2)}) collective-permute-start(bf16[2,128,1024]{2,1,0:T(8,128)(2,1)S(1)} %fusion.4), channel_id=1, source_target_pairs={{0,2},{1,3},{2,0},{3,1},{4,6},{5,7},{6,4},{7,5},{8,10},{9,11},{10,... | collective-permute-start | bytes 1572872 | tf_op jit(solution)/shard_map/ppermute | solution.py:19
  346.1 4.5 collective-permute-start.33
  353.8 28.7 %collective-permute-start.37 = (bf16[4,128,1024]{2,1,0:T(8,128)(2,1)}, bf16[4,128,1024]{2,1,0:T(8,128)(2,1)}, u32[]{:S(2)}, u32[]{:S(2)}) collective-permute-start(bf16[4,128,1024]{2,1,0:T(8,128)(2,1)} %get-tuple-element.469), channel_id=1, source_target_pairs={{0,16},{8,24},{16,0},{24,8},{1,17},{9,25},{17,1},{25,9},{2,18},{10... | collective-permute-start | bytes 3145736 | tf_op jit(solution)/shard_map/ppermute | solution.py:19
  354.4 28.1 %collective-permute-start.36 = (bf16[2,2,128,1024]{3,2,1,0:T(8,128)(2,1)}, bf16[2,2,128,1024]{3,2,1,0:T(8,128)(2,1)}, u32[]{:S(2)}, u32[]{:S(2)}) collective-permute-start(bf16[2,2,128,1024]{3,2,1,0:T(8,128)(2,1)} %bitcast.49), channel_id=1, source_target_pairs={{0,1},{1,0},{2,3},{3,2},{4,5},{5,4},{6,7},{7,6},{8,9},{9,8},{10,11... | collective-permute-start | bytes 3145736 | tf_op jit(solution)/shard_map/ppermute | solution.py:19
  356.6 21.7 %collective-permute-start.35 = (bf16[128,1024]{1,0:T(8,128)(2,1)}, bf16[128,1024]{1,0:T(8,128)(2,1)}, u32[]{:S(2)}, u32[]{:S(2)}) collective-permute-start(bf16[128,1024]{1,0:T(8,128)(2,1)} %fusion.20), channel_id=1, source_target_pairs={{0,4},{1,5},{2,6},{3,7},{4,0},{5,1},{6,2},{7,3},{8,12},{9,13},{10,... | collective-permute-start | bytes 786440 | tf_op jit(solution)/shard_map/ppermute | solution.py:19
  358.2 24.3 %collective-permute-start.34 = (bf16[128,1024]{1,0:T(8,128)(2,1)S(1)}, bf16[128,1024]{1,0:T(8,128)(2,1)}, u32[]{:S(2)}, u32[]{:S(2)}) collective-permute-start(bf16[128,1024]{1,0:T(8,128)(2,1)S(1)} %fusion.19), channel_id=1, source_target_pairs={{0,4},{1,5},{2,6},{3,7},{4,0},{5,1},{6,2},{7,3},{8,12},{9,13},{10,... | collective-permute-start | bytes 786440 | tf_op jit(solution)/shard_map/ppermute | solution.py:19
  389.5 18.8 %collective-permute-start.42 = (bf16[2,128,1024]{2,1,0:T(8,128)(2,1)S(1)}, bf16[2,128,1024]{2,1,0:T(8,128)(2,1)S(1)}, u32[]{:S(2)}, u32[]{:S(2)}) collective-permute-start(bf16[2,128,1024]{2,1,0:T(8,128)(2,1)S(1)} %pad_maximum_fusion.4), channel_id=1, source_target_pairs={{0,16},{8,24},{16,0},{24,8},{1,17},{9,25},{17,1},{25,9},{2,18},{10... | collective-permute-start | bytes 1572872 | tf_op jit(solution)/shard_map/ppermute | solution.py:19
  391.0 12.3 %collective-permute-start.40 = (bf16[2,128,1024]{2,1,0:T(8,128)(2,1)S(1)}, bf16[2,128,1024]{2,1,0:T(8,128)(2,1)S(1)}, u32[]{:S(2)}, u32[]{:S(2)}) collective-permute-start(bf16[2,128,1024]{2,1,0:T(8,128)(2,1)S(1)} %fusion.3), channel_id=1, source_target_pairs={{0,2},{1,3},{2,0},{3,1},{4,6},{5,7},{6,4},{7,5},{8,10},{9,11},{10,... | collective-permute-start | bytes 1572872 | tf_op jit(solution)/shard_map/ppermute | solution.py:19
  392.8 10.5 %collective-permute-start.39 = (f32[2,16,128]{2,1,0:T(8,128)S(1)}, f32[2,16,128]{2,1,0:T(8,128)S(1)}, u32[]{:S(2)}, u32[]{:S(2)}) collective-permute-start(f32[2,16,128]{2,1,0:T(8,128)S(1)} %bitcast_add_fusion), channel_id=1, source_target_pairs={{0,2},{1,3},{2,0},{3,1},{4,6},{5,7},{6,4},{7,5},{8,10},{9,11},{10,... | collective-permute-start | bytes 49160 | tf_op jit(solution)/shard_map/ppermute | solution.py:19
  405.7 4.5 collective-permute-start.41
  412.3 6.7 %collective-permute-start.43 = (bf16[2,128,1024]{2,1,0:T(8,128)(2,1)S(1)}, bf16[2,128,1024]{2,1,0:T(8,128)(2,1)S(1)}, u32[]{:S(2)}, u32[]{:S(2)}) collective-permute-start(bf16[2,128,1024]{2,1,0:T(8,128)(2,1)S(1)} %pad_maximum_fusion.5), channel_id=1, source_target_pairs={{0,8},{8,0},{16,24},{24,16},{1,9},{9,1},{17,25},{25,17},{2,10},{10... | collective-permute-start | bytes 1572872 | tf_op jit(solution)/shard_map/ppermute | solution.py:19
  412.4 15.4 %collective-permute-start.48 = (bf16[128,1024]{1,0:T(8,128)(2,1)}, bf16[128,1024]{1,0:T(8,128)(2,1)S(1)}, u32[]{:S(2)}, u32[]{:S(2)}) collective-permute-start(bf16[128,1024]{1,0:T(8,128)(2,1)} %fusion.13), channel_id=1, source_target_pairs={{0,4},{1,5},{2,6},{3,7},{4,0},{5,1},{6,2},{7,3},{8,12},{9,13},{10,... | collective-permute-start | bytes 786440 | tf_op jit(solution)/shard_map/ppermute | solution.py:19
  429.4 26.3 %collective-permute-start.47 = (bf16[2,2,128,1024]{3,2,1,0:T(8,128)(2,1)}, bf16[2,2,128,1024]{3,2,1,0:T(8,128)(2,1)}, u32[]{:S(2)}, u32[]{:S(2)}) collective-permute-start(bf16[2,2,128,1024]{3,2,1,0:T(8,128)(2,1)} %pad_maximum_fusion.2.pair_ref), channel_id=1, source_target_pairs={{0,16},{8,24},{16,0},{24,8},{1,17},{9,25},{17,1},{25,9},{2,18},{10... | collective-permute-start | bytes 3145736 | tf_op jit(solution)/shard_map/ppermute | solution.py:19
  431.7 34.8 %collective-permute-start.50 = (bf16[2,128,1024]{2,1,0:T(8,128)(2,1)}, bf16[2,128,1024]{2,1,0:T(8,128)(2,1)}, u32[]{:S(2)}, u32[]{:S(2)}) collective-permute-start(bf16[2,128,1024]{2,1,0:T(8,128)(2,1)} %pad_maximum_fusion.6.pair_ref), channel_id=1, source_target_pairs={{0,16},{8,24},{16,0},{24,8},{1,17},{9,25},{17,1},{25,9},{2,18},{10... | collective-permute-start | bytes 1572872 | tf_op jit(solution)/shard_map/ppermute | solution.py:19
  (45 other events, 501.4 us)
Sparse Core Ops, SparseCore 0:
  53.1 85.4 all-gather.4
  145.9 51.5 all-gather.6
